TPU v7x, 256 devices: a whole 4x4x8 slice. The times are simulated.
256 devices in a mesh: row: 32 (over y, z), col: 8 (over x, core).
Axes of the slice: x: 4, y: 4, z: 8, core: 2. Of those that a mesh axis runs over, the one named last changes fastest.
Arguments:
- points: float32 [16, 32768], P(None, ('col', 'row')), may hold values from -5 to 5
- inv_scales: float32 [16], replicated, may hold values from 0.1 to 0.4
- amplitude: float32 [1], replicated, may hold values from 0.5 to 2
- noise_var: float32 [1], replicated, may hold values from 0.3 to 1
- targets: float32 [8, 32768], P(None, ('col', 'row')), may hold values from -6 to 6
- initial: float32 [8, 32768], P(None, ('col', 'row')), may hold values from -3 to 3
- ritz_basis: float32 [64, 32768], P(None, ('col', 'row')), may hold values from -0.03125 to 0.03125
Outputs:
- solution: float32 [8, 32768], P(None, ('col', 'row'))
- residual: float32 [8, 32768], P(None, ('col', 'row'))
All inputs are finite; a program needn't handle non-finite values.
Results may differ from a plain program's by a relative error of at most 0.00065.
Values sent between devices are 32-bit elements; how exact they have to be, the bound alone decides.
No kernel may reach another device: no remote copies, remote signals or barrier semaphores. Data moves between devices by JAX's collectives and lax.ppermute only.
A program may use at most 128 MiB of HBM per device.

v0:
```python
import jax
import jax.numpy as jnp
from jax import lax
from jax.sharding import Mesh
from jax.sharding import PartitionSpec as P

ITERS = 1
ROW = ("row_0", "row_1")
COL = ("col_0", "col_1")
COL_ROW = ("col_0", "col_1", "row_0", "row_1")


HIGH = lax.Precision.HIGHEST


def laid_out(pieces, dim):
    dims = list(pieces.shape[1:])
    dims[dim] *= pieces.shape[0]
    return jnp.moveaxis(pieces, 0, dim).reshape(dims)


def from_everyone(array, axis):
    copies = jnp.broadcast_to(array, (lax.axis_size(axis), *array.shape))
    return lax.all_to_all(copies, axis, split_axis=0, concat_axis=0, tiled=True)


def gathered_copies(array, axis, dim):
    return laid_out(from_everyone(array, axis), dim)


def split_up(array, dim, peers):
    dims = array.shape
    pieces = array.reshape(*dims[:dim], peers, dims[dim] // peers, *dims[dim + 1 :])
    return jnp.moveaxis(pieces, dim, 0)


def sum_at_owner(array, axis, dim):
    pieces = split_up(array, dim, lax.axis_size(axis))
    arrived = lax.all_to_all(pieces, axis, split_axis=0, concat_axis=0, tiled=True)
    return arrived.sum(axis=0)


def taken_together(array, axis):
    everything = from_everyone(array, axis)
    return jnp.sum(everything, axis=0)


def one_axis_at_a_time(array, axes):
    far, near = axes
    return taken_together(taken_together(array, near), far)


def in_one(arrays, axis):
    flat, at, gathered = (jnp.concatenate([a.reshape(-1) for a in arrays]), 0, [])
    subtotal = one_axis_at_a_time(flat, axis)
    for a in arrays:
        gathered.append(subtotal[at : at + a.size].reshape(a.shape))
        at += a.size
    return tuple(gathered)


def kernel_tile(col_x, col_sq, row_x, row_sq, gain):
    cross_term = jnp.dot(col_x.T, row_x, precision=HIGH, preferred_element_type=jnp.float32)
    distance = jnp.maximum(col_sq[:, None] + row_sq[None, :] - 2.0 * cross_term, 0.0)
    return gain * jnp.exp(-0.5 * distance)


def coarse_solve(factor, rhs_block):
    middle = lax.linalg.triangular_solve(factor, rhs_block, left_side=True, lower=True)
    return lax.linalg.triangular_solve(factor, middle, left_side=True, lower=True, transpose_a=True)


def matmul(left, right):
    return jnp.dot(left, right, precision=HIGH, preferred_element_type=jnp.float32)


def local(points, inv_scales, amplitude, noise_var, targets, initial, ritz_basis):
    gain = amplitude[0]
    nugget = noise_var[0]
    row_x = gathered_copies(points, ROW, 1) * inv_scales[:, None]
    row_sq = jnp.sum(row_x * row_x, axis=0)
    near_x = gathered_copies(points, COL, 1) * inv_scales[:, None]
    near_sq = jnp.sum(near_x * near_x, axis=0)

    def apply_operator(vectors):
        partial_value = matmul(
            gathered_copies(vectors, COL, 1), kernel_tile(near_x, near_sq, row_x, row_sq, gain)
        )
        return sum_at_owner(partial_value, ROW, 1) + nugget * vectors

    rhs_count = initial.shape[0]
    applied_all = apply_operator(jnp.concatenate([initial, ritz_basis], 0))
    ritz_image = applied_all[rhs_count:]
    first_residual = targets - applied_all[:rhs_count]
    coarse, projected = in_one(
        (matmul(ritz_basis, ritz_image.T), matmul(ritz_basis, first_residual.T)),
        (("row_0", "row_1"), ("col_0", "col_1")),
    )
    coarse = 0.5 * (coarse + coarse.T)
    factor = jnp.linalg.cholesky(coarse)
    coarse_inverse = coarse_solve(factor, jnp.eye(coarse.shape[0], dtype=jnp.float32))
    amounts = matmul(coarse_inverse, projected)
    solution = initial + matmul(amounts.T, ritz_basis)
    residual = first_residual - matmul(amounts.T, ritz_image)

    def residual_stats(current):
        return in_one(
            (matmul(ritz_image, current.T), jnp.sum(current * current, axis=1)),
            (("row_0", "row_1"), ("col_0", "col_1")),
        )

    against, sq_norm = residual_stats(residual)
    direction = residual - matmul(matmul(coarse_inverse, against).T, ritz_basis)

    def plain_step(step, state):
        solution, residual, direction, sq_norm = state
        applied = apply_operator(direction)
        curvature = one_axis_at_a_time(
            jnp.sum(direction * applied, axis=1), (("row_0", "row_1"), ("col_0", "col_1"))
        )
        step_size = sq_norm / curvature
        solution = solution + step_size[:, None] * direction
        residual = residual - step_size[:, None] * applied
        against, new_norm = residual_stats(residual)
        correction = matmul(matmul(coarse_inverse, against).T, ritz_basis)
        direction = residual + (new_norm / sq_norm)[:, None] * direction - correction
        return (solution, residual, direction, new_norm)

    solution, residual, direction, sq_norm = lax.fori_loop(
        0, ITERS, plain_step, (solution, residual, direction, sq_norm)
    )
    return (solution, residual)


def solution(mesh):
    torus = Mesh(mesh.devices.reshape(4, 8, 4, 2), ("row_0", "row_1", "col_0", "col_1"))
    in_specs = (
        P(None, COL_ROW),
        P(),
        P(),
        P(),
        P(None, COL_ROW),
        P(None, COL_ROW),
        P(None, COL_ROW),
    )
    out_specs = (P(None, COL_ROW), P(None, COL_ROW))
    return jax.shard_map(local, mesh=torus, in_specs=in_specs, out_specs=out_specs, check_vma=False)
```

profile of v0, /device:TPU:1, one launch (start us, length us, event | category | flops | bytes accessed | tf_op | source)
XLA Modules:
  0.0 255.8 jit_solution(16806615343434934951)
XLA Ops:
  0.6 1.3 broadcast_in_dim.53
  2.0 6.5 %all-to-all-start.1 = ((f32[8,16,128]{2,1,0:T(8,128)}), f32[8,16,128]{2,1,0:T(8,128)S(1)}, u32[]{:S(2)}, u32[]{:S(2)}) async-start(f32[8,16,128]{2,1,0:T(8,128)} %broadcast_in_dim.53), calls=%async_computation.1 | async-start | bytes 131072 | tf_op jit(solution)/shard_map/all_to_all | solution.py:24
  8.4 0.7 constant_dynamic-update-slice_fusion.1
  9.1 0.8 constant_dynamic-update-slice_fusion
  9.9 3.4 %all-to-all-done.1 = f32[8,16,128]{2,1,0:T(8,128)S(1)} async-done(((f32[8,16,128]{2,1,0:T(8,128)}), f32[8,16,128]{2,1,0:T(8,128)S(1)}, u32[]{:S(2)}, u32[]{:S(2)}) %all-to-all-start.1) | async-done | bytes 65568 | tf_op jit(solution)/shard_map/all_to_all | solution.py:24
  13.3 10.4 %all_to_all.74 = f32[8,72,128]{2,1,0:T(8,128)S(1)} all-to-all(f32[8,72,128]{2,1,0:T(8,128)S(1)} %broadcast_in_dim.52), channel_id=1, replica_groups=mesh['row_0'=4,'row_1'=8,'col_0'=4,'col_1'=2] {'col_0','col_1'}, dimensions={0} | all-to-all | bytes 589824 | tf_op jit(solution)/shard_map/all_to_all | solution.py:24
  23.7 1.4 broadcast_in_dim.54
  25.1 10.5 %all-to-all-start.2 = ((f32[32,16,128]{2,1,0:T(8,128)}), f32[32,16,128]{2,1,0:T(8,128)S(1)}, u32[]{:S(2)}, u32[]{:S(2)}) async-start(f32[32,16,128]{2,1,0:T(8,128)} %broadcast_in_dim.54), calls=%async_computation.2 | async-start | bytes 524288 | tf_op jit(solution)/shard_map/all_to_all | solution.py:24
  36.3 0.7 fusion.6
  37.1 0.1 copy.32
  37.1 0.1 reshape.134
  37.2 8.2 %all-to-all-done.2 = f32[32,16,128]{2,1,0:T(8,128)S(1)} async-done(((f32[32,16,128]{2,1,0:T(8,128)}), f32[32,16,128]{2,1,0:T(8,128)S(1)}, u32[]{:S(2)}, u32[]{:S(2)}) %all-to-all-start.2) | async-done | bytes 262176 | tf_op jit(solution)/shard_map/all_to_all | solution.py:24
  45.3 0.8 fusion.3
  46.1 18.7 %exponential_multiply_fusion = f32[4096,1024]{1,0:T(8,128)S(1)} fusion(f32[4096]{0:T(1024)S(1)} %bitcast.82, f32[1024]{0:T(1024)S(1)} %bitcast.84, f32[]{:T(128)} %bitcast.75, f32[32,16,128]{2,1,0:T(8,128)S(1)} %all-to-all-done.2, f32[16]{0:T(128)} %param.8, f32[8,16,128]{2,1,0:T(8,128)S(1)} %all-to-all-done.1), kind=kOutput, calls=%fused_computation | convolution fusion | flops 830554112 | bytes 17125444 | tf_op jit(solution)/shard_map/dot_general | solution.py:63
  64.8 0.0 copy-start
  64.8 0.0 copy-start.1
  64.8 0.0 copy-start.2
  64.9 5.7 %copy-done = f32[4096,1024]{1,0:T(8,128)} copy-done((f32[4096,1024]{1,0:T(8,128)}, f32[4096,1024]{1,0:T(8,128)S(1)}, u32[]{:S(2)}) %copy-start) | copy-done | bytes 16777240
  70.5 17.5 %convolution_bitcast_fusion = f32[32,72,128]{2,1,0:T(8,128)} fusion(f32[72,1024,1]{1,0,2:T(8,128)S(1)} %reshape.134, f32[32,128,1024]{2,1,0:T(8,128)S(1)} %bitcast.79), kind=kOutput, calls=%fused_computation.1 | convolution fusion | flops 3623878656 | bytes 18251776 | tf_op jit(solution)/shard_map/dot_general | solution.py:74
  88.0 6.5 %all-to-all-start.3 = ((f32[32,72,128]{2,1,0:T(8,128)}), f32[32,72,128]{2,1,0:T(8,128)S(1)}, u32[]{:S(2)}, u32[]{:S(2)}) async-start(f32[32,72,128]{2,1,0:T(8,128)} %convolution_bitcast_fusion), calls=%async_computation.3 | async-start | bytes 2359296 | tf_op jit(solution)/shard_map/all_to_all | solution.py:39
  95.2 27.0 %all-to-all-done.3 = f32[32,72,128]{2,1,0:T(8,128)S(1)} async-done(((f32[32,72,128]{2,1,0:T(8,128)}), f32[32,72,128]{2,1,0:T(8,128)S(1)}, u32[]{:S(2)}, u32[]{:S(2)}) %all-to-all-start.3) | async-done | bytes 1179680 | tf_op jit(solution)/shard_map/all_to_all | solution.py:39
  122.2 0.1 reduce_sum.129
  122.3 0.2 convolution_bitcast_fusion.2
  122.5 0.1 copy.35
  122.5 0.1 reshape.127
  122.6 0.0 copy-done.2
  122.6 0.1 convolution_bitcast_fusion.3
  122.8 0.1 copy.36
  122.8 0.1 reshape.128
  123.0 0.1 broadcast_in_dim.55
  123.1 12.7 %all_to_all.75 = f32[8,1,4608]{2,1,0:T(1,128)S(1)} all-to-all(f32[8,1,4608]{2,1,0:T(1,128)S(1)} %broadcast_in_dim.55), channel_id=1, replica_groups=mesh['row_0'=4,'row_1'=8,'col_0'=4,'col_1'=2] {'col_0','col_1'}, dimensions={0} | all-to-all | bytes 294912 | tf_op jit(solution)/shard_map/all_to_all | solution.py:24
  135.7 0.1 reduce_sum.130
  135.8 0.3 broadcast_in_dim.56
  136.2 20.1 %all_to_all.76 = f32[32,1,4608]{2,1,0:T(1,128)S(1)} all-to-all(f32[32,1,4608]{2,1,0:T(1,128)S(1)} %broadcast_in_dim.56), channel_id=1, replica_groups=mesh['row_0'=4,'row_1'=8,'col_0'=4,'col_1'=2] {'row_0','row_1'}, dimensions={0} | all-to-all | bytes 1179648 | tf_op jit(solution)/shard_map/all_to_all | solution.py:24
  156.3 0.3 reduce_sum.131
  156.6 0.1 reshape.129
  156.7 0.1 copy.39
  156.8 0.1 copy.40
  156.9 5.8 %cholesky.17 = f32[64,64]{1,0:T(8,128)S(1)} custom-call(f32[64,64]{1,0:T(8,128)S(1)} %fusion.13), custom_call_target="Cholesky" | custom-call | tf_op jit(solution)/shard_map/jit(cholesky)/cholesky | solution.py:100
  162.8 0.6 compare_reduce_fusion
  163.4 0.7 fusion.7
  164.1 4.9 %custom-call.8 = f32[1,64,64]{1,2,0:T(8,128)S(1)} custom-call(f32[1,64,64]{2,1,0:T(8,128)S(1)} %fusion.7), custom_call_target="InvertDiagBlocksLowerTriangular" | custom-call | tf_op jit(solution)/shard_map/triangular_solve | solution.py:70
  169.0 0.2 fusion.11
  169.2 0.2 fusion.9
  169.4 0.1 reshape.130
  169.5 0.2 fusion.19
  169.7 0.3 multiply_reduce_fusion.1
  170.0 0.2 fusion.15
  170.1 0.1 reshape.131
  170.3 10.7 %all_to_all.77 = f32[8,1,520]{2,1,0:T(1,128)S(1)} all-to-all(f32[8,1,520]{2,1,0:T(1,128)S(1)} %broadcast_in_dim.57), channel_id=1, replica_groups=mesh['row_0'=4,'row_1'=8,'col_0'=4,'col_1'=2] {'col_0','col_1'}, dimensions={0} | all-to-all | bytes 33280 | tf_op jit(solution)/shard_map/all_to_all | solution.py:24
  181.0 14.0 %all_to_all.78 = f32[32,1,520]{2,1,0:T(1,128)S(1)} all-to-all(f32[32,1,520]{2,1,0:T(1,128)S(1)} %broadcast_in_dim.58), channel_id=1, replica_groups=mesh['row_0'=4,'row_1'=8,'col_0'=4,'col_1'=2] {'row_0','row_1'}, dimensions={0} | all-to-all | bytes 133120 | tf_op jit(solution)/shard_map/all_to_all | solution.py:24
  195.0 0.1 reduce_sum.134
  195.1 0.1 reshape.132
  195.2 0.2 fusion.20
  195.4 0.2 convolution_subtract_fusion
  195.6 9.2 %all_to_all.79 = f32[8,8,128]{2,1,0:T(8,128)S(1)} all-to-all(f32[8,8,128]{2,1,0:T(8,128)S(1)} %broadcast_in_dim.59), channel_id=1, replica_groups=mesh['row_0'=4,'row_1'=8,'col_0'=4,'col_1'=2] {'col_0','col_1'}, dimensions={0} | all-to-all | bytes 65536 | tf_op jit(solution)/shard_map/while/body/eval_jaxpr/all_to_all | solution.py:24
  204.8 16.2 %convolution_bitcast_fusion.1 = f32[32,8,128]{2,1,0:T(8,128)S(1)} fusion(f32[32,128,1024]{2,1,0:T(8,128)} %bitcast.80, f32[8,8,128]{2,1,0:T(8,128)S(1)} %all_to_all.79), kind=kOutput, calls=%fused_computation.2 | convolution fusion | flops 402653184 | bytes 16941056 | tf_op jit(solution)/shard_map/while/body/eval_jaxpr/dot_general | solution.py:74
  220.9 12.1 %all_to_all.80 = f32[32,8,128]{2,1,0:T(8,128)S(1)} all-to-all(f32[32,8,128]{2,1,0:T(8,128)S(1)} %convolution_bitcast_fusion.1), channel_id=1, replica_groups=mesh['row_0'=4,'row_1'=8,'col_0'=4,'col_1'=2] {'row_0','row_1'}, dimensions={0} | all-to-all | bytes 262144 | tf_op jit(solution)/shard_map/while/body/eval_jaxpr/all_to_all | solution.py:39
  233.1 0.1 multiply_reduce_fusion
  233.2 9.1 %all_to_all.81 = f32[8,1,8]{2,1,0:T(1,128)S(1)} all-to-all(f32[8,1,8]{2,1,0:T(1,128)S(1)} %broadcast_in_dim.60), channel_id=1, replica_groups=mesh['row_0'=4,'row_1'=8,'col_0'=4,'col_1'=2] {'col_0','col_1'}, dimensions={0} | all-to-all | bytes 512 | tf_op jit(solution)/shard_map/while/body/eval_jaxpr/all_to_all | solution.py:24
  242.4 12.0 %all_to_all.82 = f32[32,1,8]{2,1,0:T(1,128)S(1)} all-to-all(f32[32,1,8]{2,1,0:T(1,128)S(1)} %broadcast_in_dim.61), channel_id=1, replica_groups=mesh['row_0'=4,'row_1'=8,'col_0'=4,'col_1'=2] {'row_0','row_1'}, dimensions={0} | all-to-all | bytes 2048 | tf_op jit(solution)/shard_map/while/body/eval_jaxpr/all_to_all | solution.py:24
  254.3 0.1 reduce_sum.138
  254.4 0.7 fusion
  255.1 0.7 multiply_subtract_fusion
  (22 shorter events, 0.3 us)
Async XLA Ops:
  2.0 11.3 %all-to-all-start.1 = ((f32[8,16,128]{2,1,0:T(8,128)}), f32[8,16,128]{2,1,0:T(8,128)S(1)}, u32[]{:S(2)}, u32[]{:S(2)}) async-start(f32[8,16,128]{2,1,0:T(8,128)} %broadcast_in_dim.53), calls=%async_computation.1 | async-start | bytes 131072 | tf_op jit(solution)/shard_map/all_to_all | solution.py:24
  25.1 20.2 %all-to-all-start.2 = ((f32[32,16,128]{2,1,0:T(8,128)}), f32[32,16,128]{2,1,0:T(8,128)S(1)}, u32[]{:S(2)}, u32[]{:S(2)}) async-start(f32[32,16,128]{2,1,0:T(8,128)} %broadcast_in_dim.54), calls=%async_computation.2 | async-start | bytes 524288 | tf_op jit(solution)/shard_map/all_to_all | solution.py:24
  64.8 5.7 %copy-start = (f32[4096,1024]{1,0:T(8,128)}, f32[4096,1024]{1,0:T(8,128)S(1)}, u32[]{:S(2)}) copy-start(f32[4096,1024]{1,0:T(8,128)S(1)} %exponential_multiply_fusion) | copy-start | bytes 50331652
  64.8 57.4 %copy-start.1 = (f32[64,128]{1,0:T(8,128)S(1)}, f32[64,128]{1,0:T(8,128)}, u32[]{:S(2)}) copy-start(f32[64,128]{1,0:T(8,128)} %param.13) | copy-start | bytes 98308
  64.8 57.8 %copy-start.2 = (f32[8,128]{1,0:T(8,128)S(1)}, f32[8,128]{1,0:T(8,128)}, u32[]{:S(2)}) copy-start(f32[8,128]{1,0:T(8,128)} %param.11) | copy-start | bytes 12292
  88.0 166.4 %copy-start.3 = (f32[8,128]{1,0:T(8,128)S(1)}, f32[8,128]{1,0:T(8,128)}, u32[]{:S(2)}) copy-start(f32[8,128]{1,0:T(8,128)} %param.12) | copy-start | bytes 12292
  88.0 34.1 %all-to-all-start.3 = ((f32[32,72,128]{2,1,0:T(8,128)}), f32[32,72,128]{2,1,0:T(8,128)S(1)}, u32[]{:S(2)}, u32[]{:S(2)}) async-start(f32[32,72,128]{2,1,0:T(8,128)} %convolution_bitcast_fusion), calls=%async_computation.3 | async-start | bytes 2359296 | tf_op jit(solution)/shard_map/all_to_all | solution.py:39
where the time goes:
time: 257 us; the launch traced here: 256 us
  blocking collectives  110 us (43%)
  matrix products  54.8 us (21%)
  waiting for transfers between devices  38.5 us (15%)
  starting transfers between devices  23.5 us (9%)
  other arithmetic  15.1 us (6%)
  local copies, waits for them, and re-layouts  11.3 us (4%)
    all_to_all x8, blocking collectives, from_everyone(): return lax.all_to_all(copies, axis, split_axis=0, concat_axis=0, tiled=True)  98.2 us
    dot_general x10, matrix products, matmul(): jnp.dot(left, right, precision=HIGH, preferred_element_type=jnp.float32)  35.7 us
    all_to_all x1, waiting for transfers between devices, sum_at_owner(): lax.all_to_all(pieces, axis, split_axis=0, concat_axis=0, tiled=True)  27 us
    dot_general x1, matrix products, kernel_tile(): jnp.dot(col_x.T, row_x, precision=HIGH, preferred_element_type=jnp.float32)  18.7 us
    all_to_all x2, starting transfers between devices, from_everyone(): return lax.all_to_all(copies, axis, split_axis=0, concat_axis=0, tiled=True)  17 us
    all_to_all x1, blocking collectives, sum_at_owner(): lax.all_to_all(pieces, axis, split_axis=0, concat_axis=0, tiled=True)  12.1 us
    all_to_all x2, waiting for transfers between devices, from_everyone(): return lax.all_to_all(copies, axis, split_axis=0, concat_axis=0, tiled=True)  11.6 us
    another operation x3, other arithmetic, local(): factor = jnp.linalg.cholesky(coarse)  6.52 us
  transfers between devices with their start and end apart: 3, of which 3 were waited for; matrix products, arithmetic and copies ran while one was open for 1% of the time, Pallas kernels for 0%

commit v1 on v0

v1 whole, which is shorter than its diff:
```python
import math

import jax
import jax.numpy as jnp
from jax import lax
from jax.experimental import pallas as pl
from jax.experimental.pallas import tpu as pltpu
from jax.sharding import Mesh
from jax.sharding import PartitionSpec as P

CORE = "col_1"
Z = "row_1"
XY = ("col_0", "row_0")
CZ = ("col_1", "row_1")
EVERY = ("col_0", "col_1", "row_0", "row_1")
COL_ROW = EVERY

FEAT = 16
RITZ = 64
RHS = 8
VEC = RHS + RITZ
BLK = 128
NB = 16
PTS = NB * BLK
STEP = 256
CHUNK = 512

HIGH = lax.Precision.HIGHEST
F32 = jnp.float32
BF16 = jnp.bfloat16
NT = (((1,), (1,)), ((), ()))


def split2(x):
    hi = x.astype(BF16)
    return hi, (x - hi.astype(F32)).astype(BF16)


def split3(x):
    hi = x.astype(BF16).astype(F32)
    rest = x - hi
    mid = rest.astype(BF16).astype(F32)
    return hi, mid, rest - mid


def features(x, swap):
    a, b, c = split3(x)
    n1, n2, n3 = split3(-0.5 * jnp.sum(x * x, axis=0, keepdims=True))
    row = lax.broadcasted_iota(jnp.int32, x.shape, 0)
    base = 3 if swap else 0
    norm = jnp.where(row == base, n1, jnp.where(row == base + 1, n2, jnp.where(row == base + 2, n3, 0.0)))
    one = 0 if swap else 3
    norm = jnp.where((row >= one) & (row < one + 3), 1.0, norm)
    zero = jnp.zeros_like(x)
    if swap:
        parts = [a, b, a, b, c, a, norm, zero]
    else:
        parts = [a, a, b, b, a, c, norm, zero]
    return jnp.concatenate(parts, axis=0)


def tile_kernel(near_ref, far_ref, out_ref, scale_ref, hi_ref, lo_ref, part_ref, cols_ref, rows_ref, vec_ref):
    step = pl.program_id(0)

    @pl.when(step == 0)
    def _():
        scale = scale_ref[...] * math.sqrt(math.log2(math.e))
        vec_ref[...] = jnp.zeros_like(vec_ref)
        for b in range(NB):
            src = near_ref if b < NB // 2 else far_ref
            at = b % (NB // 2)
            lanes = pl.ds(b * BLK, BLK)
            cols_ref[:, lanes] = features(src[at, :FEAT, :] * scale, False).astype(BF16)
            hi, lo = split2(src[at, FEAT:, :])
            vec_ref[pl.ds(0, VEC), lanes] = hi
            vec_ref[pl.ds(BLK, VEC), lanes] = lo
            rows_ref[lanes, :] = features(out_ref[b, :FEAT, :] * scale, True).T.astype(BF16)

    mine = rows_ref[pl.ds(pl.multiple_of(step * STEP, STEP), STEP), :]
    total = jnp.zeros((STEP, 2 * BLK), F32)
    for c in range(PTS // CHUNK):
        lanes = pl.ds(c * CHUNK, CHUNK)
        power = jnp.dot(mine, cols_ref[:, lanes], preferred_element_type=F32)
        value = jnp.exp2(jnp.minimum(power, 0.0))
        hi, lo = split2(value)
        hi_ref[:, lanes] = hi
        lo_ref[:, lanes] = lo
        vec = vec_ref[:, lanes]
        total += lax.dot_general(hi, vec, NT, preferred_element_type=F32)
        total += lax.dot_general(lo, vec, NT, preferred_element_type=F32)
    both = total[:, :BLK] + total[:, BLK:]
    for h in range(STEP // BLK):
        part_ref[h] = both[h * BLK : (h + 1) * BLK].T[:VEC]


def make_tile(near, far, out, scales):
    full = lambda shape: pl.BlockSpec(shape, lambda i: (0,) * len(shape))
    return pl.pallas_call(
        tile_kernel,
        grid=(PTS // STEP,),
        in_specs=[full(near.shape), full(far.shape), full(out.shape), full(scales.shape)],
        out_specs=[
            pl.BlockSpec((STEP, PTS), lambda i: (i, 0)),
            pl.BlockSpec((STEP, PTS), lambda i: (i, 0)),
            pl.BlockSpec((STEP // BLK, VEC, BLK), lambda i: (i, 0, 0)),
        ],
        out_shape=[
            jax.ShapeDtypeStruct((PTS, PTS), BF16),
            jax.ShapeDtypeStruct((PTS, PTS), BF16),
            jax.ShapeDtypeStruct((NB, VEC, BLK), F32),
        ],
        scratch_shapes=[
            pltpu.VMEM((BLK, PTS), BF16),
            pltpu.VMEM((PTS, BLK), BF16),
            pltpu.VMEM((2 * BLK, PTS), BF16),
        ],
        name="kernel_tile",
    )(near, far, out, scales)


def gram_kernel(vec_ref, pts_ref, out_ref, left_ref, right_ref):
    for b in range(NB):
        lanes = pl.ds(b * BLK, BLK)
        left_ref[:, lanes] = vec_ref[b]
        right_ref[pl.ds(0, RITZ), lanes] = pts_ref[b, FEAT:, :]
        right_ref[pl.ds(RITZ, RITZ), lanes] = vec_ref[b, RHS:, :]
    out_ref[...] = lax.dot_general(left_ref[...], right_ref[...], NT, precision=HIGH, preferred_element_type=F32)


def make_gram(vec, pts):
    return pl.pallas_call(
        gram_kernel,
        out_shape=jax.ShapeDtypeStruct((VEC, 2 * RITZ), F32),
        scratch_shapes=[pltpu.VMEM((VEC, PTS), F32), pltpu.VMEM((2 * RITZ, PTS), F32)],
        name="gram",
    )(vec, pts)


def apply_kernel(hi_ref, lo_ref, vec_ref, pts_ref, coef_ref, part_ref, sum_ref):
    step = pl.program_id(0)

    @pl.when(step == 0)
    def _():
        sum_ref[...] = jnp.zeros_like(sum_ref)

    for h in range(STEP // BLK):
        basis = jnp.concatenate([pts_ref[h, FEAT:, :], vec_ref[h, RHS:, :]], axis=0)
        direction = vec_ref[h, :RHS, :] - jnp.dot(
            coef_ref[...], basis, precision=HIGH, preferred_element_type=F32
        )
        hi = direction.astype(BF16).astype(F32)
        both = jnp.concatenate([hi, direction - hi], axis=0).astype(BF16)
        rows = pl.ds(h * BLK, BLK)
        sum_ref[...] += jnp.dot(both, hi_ref[rows, :], preferred_element_type=F32)
        sum_ref[...] += jnp.dot(both, lo_ref[rows, :], preferred_element_type=F32)

    @pl.when(step == pl.num_programs(0) - 1)
    def _():
        for b in range(NB):
            lanes = pl.ds(b * BLK, BLK)
            part_ref[b] = sum_ref[pl.ds(0, RHS), lanes] + sum_ref[pl.ds(RHS, RHS), lanes]


def apply_tile(hi, lo, vec, pts, coef):
    return pl.pallas_call(
        apply_kernel,
        grid=(PTS // STEP,),
        in_specs=[
            pl.BlockSpec((STEP, PTS), lambda i: (i, 0)),
            pl.BlockSpec((STEP, PTS), lambda i: (i, 0)),
            pl.BlockSpec((STEP // BLK, VEC, BLK), lambda i: (i, 0, 0)),
            pl.BlockSpec((STEP // BLK, FEAT + RITZ, BLK), lambda i: (i, 0, 0)),
            pl.BlockSpec(coef.shape, lambda i: (0, 0)),
        ],
        out_specs=pl.BlockSpec((NB, RHS, BLK), lambda i: (0, 0, 0)),
        out_shape=jax.ShapeDtypeStruct((NB, RHS, BLK), F32),
        scratch_shapes=[pltpu.VMEM((2 * RHS, PTS), F32)],
        name="apply_tile",
    )(hi, lo, vec, pts, coef)


def exchange(pieces, axis):
    return lax.all_to_all(pieces, axis, split_axis=0, concat_axis=0, tiled=True)


def from_everyone(array, axis):
    return exchange(jnp.broadcast_to(array, (lax.axis_size(axis), *array.shape)), axis)


def other_core(array):
    return lax.ppermute(array, CORE, [(0, 1), (1, 0)])


def matmul(left, right):
    return jnp.dot(left, right, precision=HIGH, preferred_element_type=F32)


def coarse_solve(factor, rhs_block):
    middle = lax.linalg.triangular_solve(factor, rhs_block, left_side=True, lower=True)
    return lax.linalg.triangular_solve(factor, middle, left_side=True, lower=True, transpose_a=True)


def local(points, inv_scales, amplitude, noise_var, targets, initial, ritz_basis):
    gain = amplitude[0]
    nugget = noise_var[0]
    pts = from_everyone(jnp.concatenate([points, ritz_basis], 0), XY)
    vectors = jnp.concatenate([initial, ritz_basis], 0)
    near = from_everyone(jnp.concatenate([points, vectors], 0), Z)
    far = other_core(near)
    hi, lo, part = make_tile(near, far, pts, inv_scales[:, None])

    applied = gain * exchange(part, XY).sum(axis=0) + nugget * vectors
    own = jnp.concatenate([targets - applied[:RHS], applied[RHS:]], 0)
    vec = from_everyone(own, XY)

    gram = make_gram(vec, pts)
    gram = gram + other_core(gram)
    gram = from_everyone(gram, Z).sum(axis=0)
    projected = gram[:RHS, :RITZ].T
    image_first = gram[:RHS, RITZ:].T
    coarse = gram[RHS:, :RITZ]
    image_image = gram[RHS:, RITZ:]
    coarse = 0.5 * (coarse + coarse.T)
    factor = jnp.linalg.cholesky(coarse)
    coarse_inverse = coarse_solve(factor, jnp.eye(RITZ, dtype=F32))
    amounts = matmul(coarse_inverse, projected)
    against = image_first - matmul(image_image, amounts)
    turned = matmul(coarse_inverse, against)
    coef = jnp.concatenate([turned.T, amounts.T], axis=1)

    part = apply_tile(hi, lo, vec, pts, coef)
    own_first = lax.axis_index(CORE) == 0
    part = jnp.where(own_first, part, jnp.concatenate([part[NB // 2 :], part[: NB // 2]], 0))

    solution = initial + matmul(amounts.T, ritz_basis)
    residual = own[:RHS] - matmul(amounts.T, own[RHS:])
    direction = residual - matmul(turned.T, ritz_basis)
    applied = gain * exchange(part, CZ).sum(axis=0) + nugget * direction
    stats = jnp.concatenate([jnp.sum(direction * applied, axis=1), jnp.sum(residual * residual, axis=1)])
    stats = from_everyone(stats[None, :], EVERY).sum(axis=(0, 1))
    size = (stats[RHS:] / stats[:RHS])[:, None]
    return (solution + size * direction, residual - size * applied)


def solution(mesh):
    torus = Mesh(mesh.devices.reshape(4, 8, 4, 2), ("row_0", "row_1", "col_0", "col_1"))
    in_specs = (
        P(None, COL_ROW),
        P(),
        P(),
        P(),
        P(None, COL_ROW),
        P(None, COL_ROW),
        P(None, COL_ROW),
    )
    out_specs = (P(None, COL_ROW), P(None, COL_ROW))
    return jax.shard_map(local, mesh=torus, in_specs=in_specs, out_specs=out_specs, check_vma=False)
```

time: 257 us -> 176 us (0.68)
  blocking collectives: 110 us -> 31.4 us
  matrix products: 54.8 us -> 2.2 us
  Pallas kernels: 0 us -> 30.3 us
  waiting for transfers between devices: 38.5 us -> 49.8 us
  starting transfers between devices: 23.5 us -> 34.4 us
  local copies, waits for them, and re-layouts: 11.3 us -> 6.41 us
  other arithmetic: 15.1 us -> 18.4 us
    all_to_all x9 -> x2, blocking collectives: 110 us -> 31.4 us  [exchange(): return lax.all_to_all(pieces, axis, split_axis=0, concat_axis=0, tiled=True)]
    dot_general x11 -> x6, matrix products: 54.4 us -> 1.81 us  [matmul(): return jnp.dot(left, right, precision=HIGH, preferred_element_type=F32)]
    pallas_call x0 -> x3, Pallas kernels: none -> 30.3 us  [the longest x1 15.3 us: make_tile(): pl.pallas_call(tile_kernel, grid=(PTS // STEP,), in_specs=[full(near.shap...]
    all_to_all x3 -> x5, waiting for transfers between devices: 38.5 us -> 48.7 us  [exchange(): return lax.all_to_all(pieces, axis, split_axis=0, concat_axis=0, tiled=True)]
    ppermute x0 -> x2, starting transfers between devices: none -> 6.46 us  [other_core(): return lax.ppermute(array, CORE, [(0, 1), (1, 0)])]
    unnamed x9 -> x11, local copies, waits for them, and re-layouts: 6.39 us -> 1.66 us
    all_to_all x3 -> x5, starting transfers between devices: 23.5 us -> 28 us  [exchange(): return lax.all_to_all(pieces, axis, split_axis=0, concat_axis=0, tiled=True)]
  transfers between devices with their start and end apart: 3 -> 7, of which waited for: 3 -> 6; matrix products, arithmetic and copies ran while one was open for 1% -> 1% of each run, Pallas kernels for 0% -> 0%
where the time goes in v1:
time: 176 us; the launch traced here: 175 us
  waiting for transfers between devices  49.8 us (28%)
  starting transfers between devices  34.4 us (20%)
  blocking collectives  31.4 us (18%)
  Pallas kernels  30.3 us (17%)
  other arithmetic  18.4 us (10%)
  local copies, waits for them, and re-layouts  6.41 us (4%)
  matrix products  2.2 us (1%)
  between operations  2.07 us (1%)
    all_to_all x5, waiting for transfers between devices, exchange(): return lax.all_to_all(pieces, axis, split_axis=0, concat_axis=0, tiled=True)  48.7 us
    all_to_all x2, blocking collectives, exchange(): return lax.all_to_all(pieces, axis, split_axis=0, concat_axis=0, tiled=True)  31.4 us
    all_to_all x5, starting transfers between devices, exchange(): return lax.all_to_all(pieces, axis, split_axis=0, concat_axis=0, tiled=True)  28 us
    pallas_call x1, Pallas kernels, make_tile(): pl.pallas_call(tile_kernel, grid=(PTS // STEP,), in_specs=[full(near.shap...  15.3 us
    pallas_call x1, Pallas kernels, apply_tile(): pl.pallas_call(apply_kernel, grid=(PTS // STEP,), in_specs=[pl.BlockSpec(...  11.9 us
    another operation x3, other arithmetic, local(): factor = jnp.linalg.cholesky(coarse)  6.52 us
    ppermute x2, starting transfers between devices, other_core(): return lax.ppermute(array, CORE, [(0, 1), (1, 0)])  6.46 us
    another operation x2, other arithmetic, coarse_solve(): lax.linalg.triangular_solve(factor, middle, left_side=True, lower=True, t...  5.55 us
  transfers between devices with their start and end apart: 7, of which 6 were waited for; matrix products, arithmetic and copies ran while one was open for 1% of the time, Pallas kernels for 0%

profile of v1, /device:TPU:1, one launch (start us, length us, event | category | flops | bytes accessed | tf_op | source)
XLA Modules:
  0.0 175.0 jit_solution(4055241095607482278)
XLA Ops:
  0.6 0.8 pad_maximum_fusion
  1.4 0.8 broadcast_in_dim.22
  2.2 9.0 %all-to-all-start = ((f32[8,88,128]{2,1,0:T(8,128)}), f32[8,88,128]{2,1,0:T(8,128)S(1)}, u32[]{:S(2)}, u32[]{:S(2)}) async-start(f32[8,88,128]{2,1,0:T(8,128)} %broadcast_in_dim.22), calls=%async_computation | async-start | bytes 720896 | tf_op jit(solution)/shard_map/all_to_all | solution.py:183
  11.2 0.8 pad_maximum_fusion.1
  11.9 12.7 %all-to-all-done.near_ref = f32[8,88,128]{2,1,0:T(8,128)S(1)} async-done(((f32[8,88,128]{2,1,0:T(8,128)}), f32[8,88,128]{2,1,0:T(8,128)S(1)}, u32[]{:S(2)}, u32[]{:S(2)}) %all-to-all-start) | async-done | bytes 360480 | tf_op jit(solution)/shard_map/all_to_all | solution.py:183
  24.6 0.0 copy-start.1
  24.6 0.9 broadcast_in_dim.23
  25.5 6.8 %all-to-all-start.1 = ((f32[16,80,128]{2,1,0:T(8,128)}), f32[16,80,128]{2,1,0:T(8,128)S(1)}, u32[]{:S(2)}, u32[]{:S(2)}) async-start(f32[16,80,128]{2,1,0:T(8,128)} %broadcast_in_dim.23), calls=%async_computation.1 | async-start | bytes 1310720 | tf_op jit(solution)/shard_map/all_to_all | solution.py:183
  32.3 1.9 %collective-permute-start = (f32[8,88,128]{2,1,0:T(8,128)S(1)}, f32[8,88,128]{2,1,0:T(8,128)S(1)}, u32[]{:S(2)}, u32[]{:S(2)}) collective-permute-start(f32[8,88,128]{2,1,0:T(8,128)S(1)} %all-to-all-done.near_ref), channel_id=1, source_target_pairs={{0,1},{1,0},{2,3},{3,2},{4,5},{5,4},{6,7},{7,6},{8,9},{9,8},{10,11... | collective-permute-start | bytes 1081352 | tf_op jit(solution)/shard_map/ppermute | solution.py:191
  34.2 1.3 copy.16.scale_ref
  35.5 7.6 %all-to-all-done.1.out_ref.pts_ref = f32[16,80,128]{2,1,0:T(8,128)S(1)} async-done(((f32[16,80,128]{2,1,0:T(8,128)}), f32[16,80,128]{2,1,0:T(8,128)S(1)}, u32[]{:S(2)}, u32[]{:S(2)}) %all-to-all-start.1) | async-done | bytes 655392 | tf_op jit(solution)/shard_map/all_to_all | solution.py:183
  43.1 0.0 copy-start
  43.1 0.0 collective-permute-done.far_ref
  43.1 0.0 copy-done.1
  43.1 0.8 copy-done
  44.0 0.0 copy-start.3
  44.0 0.7 copy-done.3
  44.7 15.3 %kernel_tile.1 = (bf16[2048,2048]{1,0:T(8,128)(2,1)}, bf16[2048,2048]{1,0:T(8,128)(2,1)}, f32[16,72,128]{2,1,0:T(8,128)}) custom-call(f32[8,88,128]{2,1,0:T(8,128)} %copy-done.1, f32[8,88,128]{2,1,0:T(8,128)} %copy-done.3, f32[16,80,128]{2,1,0:T(8,128)} %copy-done, f32[16,1]{1,0:T(8,128)} %copy.16.scale_ref), custom_call_target="tpu_custom_call" | custom-call | tf_op jit(solution)/shard_map/kernel_tile/pallas_call | solution.py:98
  60.1 4.2 %all-to-all-start.2 = ((f32[16,72,128]{2,1,0:T(8,128)}), f32[16,72,128]{2,1,0:T(8,128)S(1)}, u32[]{:S(2)}, u32[]{:S(2)}) async-start(f32[16,72,128]{2,1,0:T(8,128)} %get-tuple-element.5), calls=%async_computation.2 | async-start | bytes 1179648 | tf_op jit(solution)/shard_map/all_to_all | solution.py:183
  65.5 8.5 %all-to-all-done.2 = f32[16,72,128]{2,1,0:T(8,128)S(1)} async-done(((f32[16,72,128]{2,1,0:T(8,128)}), f32[16,72,128]{2,1,0:T(8,128)S(1)}, u32[]{:S(2)}, u32[]{:S(2)}) %all-to-all-start.2) | async-done | bytes 589856 | tf_op jit(solution)/shard_map/all_to_all | solution.py:183
  74.1 0.8 fusion.1
  74.8 0.7 slice_subtract_fusion
  75.6 12.6 %all_to_all.35.vec_ref = f32[16,72,128]{2,1,0:T(8,128)} all-to-all(f32[16,72,128]{2,1,0:T(8,128)S(1)} %broadcast_in_dim.25), channel_id=1, replica_groups=mesh['row_0'=4,'row_1'=8,'col_0'=4,'col_1'=2] {'col_0','row_0'}, dimensions={0} | all-to-all | bytes 1179648 | tf_op jit(solution)/shard_map/all_to_all | solution.py:183
  88.2 3.1 %gram.1 = f32[72,128]{1,0:T(8,128)} custom-call(f32[16,72,128]{2,1,0:T(8,128)} %all_to_all.35.vec_ref, f32[16,80,128]{2,1,0:T(8,128)} %copy-done), custom_call_target="tpu_custom_call" | custom-call | tf_op jit(solution)/shard_map/gram/pallas_call | solution.py:131
  91.3 4.6 %collective-permute-start.1 = (f32[72,128]{1,0:T(8,128)}, f32[72,128]{1,0:T(8,128)S(1)}, u32[]{:S(2)}, u32[]{:S(2)}) collective-permute-start(f32[72,128]{1,0:T(8,128)} %gram.1), channel_id=1, source_target_pairs={{0,1},{1,0},{2,3},{3,2},{4,5},{5,4},{6,7},{7,6},{8,9},{9,8},{10,11... | collective-permute-start | bytes 110600 | tf_op jit(solution)/shard_map/ppermute | solution.py:191
  95.9 1.1 collective-permute-done.1
  97.0 0.8 add.32
  97.7 0.7 broadcast_in_dim.26
  98.5 3.4 %all-to-all-start.4 = ((f32[8,72,128]{2,1,0:T(8,128)}), f32[8,72,128]{2,1,0:T(8,128)S(1)}, u32[]{:S(2)}, u32[]{:S(2)}) async-start(f32[8,72,128]{2,1,0:T(8,128)} %broadcast_in_dim.26), calls=%async_computation.4 | async-start | bytes 589824 | tf_op jit(solution)/shard_map/all_to_all | solution.py:183
  101.9 13.0 %all-to-all-done.4 = f32[8,72,128]{2,1,0:T(8,128)S(1)} async-done(((f32[8,72,128]{2,1,0:T(8,128)}), f32[8,72,128]{2,1,0:T(8,128)S(1)}, u32[]{:S(2)}, u32[]{:S(2)}) %all-to-all-start.4) | async-done | bytes 294944 | tf_op jit(solution)/shard_map/all_to_all | solution.py:183
  114.9 0.1 copy.22
  115.0 0.1 copy.19
  115.1 5.8 %cholesky.17 = f32[64,64]{1,0:T(8,128)S(1)} custom-call(f32[64,64]{1,0:T(8,128)S(1)} %fusion.8), custom_call_target="Cholesky" | custom-call | tf_op jit(solution)/shard_map/jit(cholesky)/cholesky | solution.py:224
  121.0 0.6 compare_reduce_fusion
  121.6 0.7 fusion.2
  122.3 4.9 %custom-call.8 = f32[1,64,64]{1,2,0:T(8,128)S(1)} custom-call(f32[1,64,64]{2,1,0:T(8,128)S(1)} %fusion.2), custom_call_target="InvertDiagBlocksLowerTriangular" | custom-call | tf_op jit(solution)/shard_map/triangular_solve | solution.py:200
  127.2 0.2 fusion.6
  127.4 0.2 fusion.4
  127.6 0.1 fusion.10
  127.8 0.2 convolution_subtract_fusion.1
  128.0 0.2 fusion.14
  128.2 0.7 pad_maximum_fusion.3.coef_ref
  128.9 0.0 copy-start.2
  128.9 0.0 copy-start.4
  128.9 11.9 %apply_tile.1 = f32[16,8,128]{2,1,0:T(8,128)} custom-call(bf16[2048,2048]{1,0:T(8,128)(2,1)} %get-tuple-element.6.hi_ref, bf16[2048,2048]{1,0:T(8,128)(2,1)} %get-tuple-element.7.lo_ref, f32[16,72,128]{2,1,0:T(8,128)} %all_to_all.35.vec_ref, f32[16,80,128]{2,1,0:T(8,128)} %copy-done, f32[8,128]{1,0:T(8,128)} %pad_maximum_fusion.3.coef_ref), custom_call_target="tpu_custom_call" | custom-call | tf_op jit(solution)/shard_map/apply_tile/pallas_call | solution.py:165
  140.8 0.8 fusion.13
  141.5 0.6 maximum_select_fusion
  142.2 4.6 %all-to-all-start.5 = ((f32[16,8,128]{2,1,0:T(8,128)}), f32[16,8,128]{2,1,0:T(8,128)S(1)}, u32[]{:S(2)}, u32[]{:S(2)}) async-start(f32[16,8,128]{2,1,0:T(8,128)} %maximum_select_fusion), calls=%async_computation.5 | async-start | bytes 131072 | tf_op jit(solution)/shard_map/all_to_all | solution.py:183
  146.8 0.2 multiply_reduce_fusion
  147.1 6.9 %all-to-all-done.5 = f32[16,8,128]{2,1,0:T(8,128)S(1)} async-done(((f32[16,8,128]{2,1,0:T(8,128)}), f32[16,8,128]{2,1,0:T(8,128)S(1)}, u32[]{:S(2)}, u32[]{:S(2)}) %all-to-all-start.5) | async-done | bytes 65568 | tf_op jit(solution)/shard_map/all_to_all | solution.py:183
  154.0 0.0 copy-done.2
  154.0 0.3 multiply_reduce_fusion.1
  154.3 0.1 pad_maximum_fusion.4
  154.3 0.1 broadcast_in_dim.27
  154.4 18.8 %all_to_all.36 = f32[256,1,16]{2,1,0:T(1,128)S(1)} all-to-all(f32[256,1,16]{2,1,0:T(1,128)S(1)} %broadcast_in_dim.27), channel_id=1, replica_groups=mesh['row_0'=4,'row_1'=8,'col_0'=4,'col_1'=2] {'col_0','col_1','row_0','..., dimensions={0} | all-to-all | bytes 32768 | tf_op jit(solution)/shard_map/all_to_all | solution.py:183
  173.2 0.3 reduce_sum.59
  173.5 0.1 slice_divide_fusion
  173.6 0.0 copy-done.4
  173.6 0.7 fusion
  174.3 0.7 multiply_subtract_fusion
  (10 shorter events, 0.2 us)
Async XLA Ops:
  2.2 22.4 %all-to-all-start = ((f32[8,88,128]{2,1,0:T(8,128)}), f32[8,88,128]{2,1,0:T(8,128)S(1)}, u32[]{:S(2)}, u32[]{:S(2)}) async-start(f32[8,88,128]{2,1,0:T(8,128)} %broadcast_in_dim.22), calls=%async_computation | async-start | bytes 720896 | tf_op jit(solution)/shard_map/all_to_all | solution.py:183
  24.6 18.5 %copy-start.1 = (f32[8,88,128]{2,1,0:T(8,128)}, f32[8,88,128]{2,1,0:T(8,128)S(1)}, u32[]{:S(2)}) copy-start(f32[8,88,128]{2,1,0:T(8,128)S(1)} %all-to-all-done.near_ref) | copy-start | bytes 1081348
  25.5 17.6 %all-to-all-start.1 = ((f32[16,80,128]{2,1,0:T(8,128)}), f32[16,80,128]{2,1,0:T(8,128)S(1)}, u32[]{:S(2)}, u32[]{:S(2)}) async-start(f32[16,80,128]{2,1,0:T(8,128)} %broadcast_in_dim.23), calls=%async_computation.1 | async-start | bytes 1310720 | tf_op jit(solution)/shard_map/all_to_all | solution.py:183
  32.3 10.8 %collective-permute-start = (f32[8,88,128]{2,1,0:T(8,128)S(1)}, f32[8,88,128]{2,1,0:T(8,128)S(1)}, u32[]{:S(2)}, u32[]{:S(2)}) collective-permute-start(f32[8,88,128]{2,1,0:T(8,128)S(1)} %all-to-all-done.near_ref), channel_id=1, source_target_pairs={{0,1},{1,0},{2,3},{3,2},{4,5},{5,4},{6,7},{7,6},{8,9},{9,8},{10,11... | collective-permute-start | bytes 1081352 | tf_op jit(solution)/shard_map/ppermute | solution.py:191
  43.1 0.8 copy-start
  44.0 0.7 copy-start.3
  60.1 14.0 %all-to-all-start.2 = ((f32[16,72,128]{2,1,0:T(8,128)}), f32[16,72,128]{2,1,0:T(8,128)S(1)}, u32[]{:S(2)}, u32[]{:S(2)}) async-start(f32[16,72,128]{2,1,0:T(8,128)} %get-tuple-element.5), calls=%async_computation.2 | async-start | bytes 1179648 | tf_op jit(solution)/shard_map/all_to_all | solution.py:183
  91.3 5.7 %collective-permute-start.1 = (f32[72,128]{1,0:T(8,128)}, f32[72,128]{1,0:T(8,128)S(1)}, u32[]{:S(2)}, u32[]{:S(2)}) collective-permute-start(f32[72,128]{1,0:T(8,128)} %gram.1), channel_id=1, source_target_pairs={{0,1},{1,0},{2,3},{3,2},{4,5},{5,4},{6,7},{7,6},{8,9},{9,8},{10,11... | collective-permute-start | bytes 110600 | tf_op jit(solution)/shard_map/ppermute | solution.py:191
  98.5 16.4 %all-to-all-start.4 = ((f32[8,72,128]{2,1,0:T(8,128)}), f32[8,72,128]{2,1,0:T(8,128)S(1)}, u32[]{:S(2)}, u32[]{:S(2)}) async-start(f32[8,72,128]{2,1,0:T(8,128)} %broadcast_in_dim.26), calls=%async_computation.4 | async-start | bytes 589824 | tf_op jit(solution)/shard_map/all_to_all | solution.py:183
  128.9 25.1 %copy-start.2 = (f32[64,128]{1,0:T(8,128)S(1)}, f32[64,128]{1,0:T(8,128)}, u32[]{:S(2)}) copy-start(f32[64,128]{1,0:T(8,128)} %param.13) | copy-start | bytes 98308
  128.9 44.7 %copy-start.4 = (f32[8,128]{1,0:T(8,128)S(1)}, f32[8,128]{1,0:T(8,128)}, u32[]{:S(2)}) copy-start(f32[8,128]{1,0:T(8,128)} %param.12) | copy-start | bytes 12292
  142.2 11.8 %all-to-all-start.5 = ((f32[16,8,128]{2,1,0:T(8,128)}), f32[16,8,128]{2,1,0:T(8,128)S(1)}, u32[]{:S(2)}, u32[]{:S(2)}) async-start(f32[16,8,128]{2,1,0:T(8,128)} %maximum_select_fusion), calls=%async_computation.5 | async-start | bytes 131072 | tf_op jit(solution)/shard_map/all_to_all | solution.py:183

commit v2 on v1

v2 whole, which is shorter than its diff:
```python
import math

import jax
import jax.numpy as jnp
from jax import lax
from jax.experimental import pallas as pl
from jax.experimental.pallas import tpu as pltpu
from jax.sharding import Mesh
from jax.sharding import PartitionSpec as P

CORE = "col_1"
Z = "row_1"
XY = ("col_0", "row_0")
CZ = ("col_1", "row_1")
EVERY = ("col_0", "col_1", "row_0", "row_1")
COL_ROW = EVERY

FEAT = 16
RITZ = 64
RHS = 8
VEC = RHS + RITZ
BLK = 128
NB = 16
PTS = NB * BLK
STEP = 256
CHUNK = 512
PACKED = RHS + RITZ // 2 + 1
WORLD = 256
TILE_MIB = 12
APPLY_MIB = 8

HIGH = lax.Precision.HIGHEST
F32 = jnp.float32
BF16 = jnp.bfloat16
NT = (((1,), (1,)), ((), ()))


def split2(x):
    hi = x.astype(BF16)
    return hi, (x - hi.astype(F32)).astype(BF16)


def split3(x):
    hi = x.astype(BF16).astype(F32)
    rest = x - hi
    mid = rest.astype(BF16).astype(F32)
    return hi, mid, rest - mid


def features(x, swap):
    a, b, c = split3(x)
    n1, n2, n3 = split3(-0.5 * jnp.sum(x * x, axis=0, keepdims=True))
    row = lax.broadcasted_iota(jnp.int32, x.shape, 0)
    base = 3 if swap else 0
    norm = jnp.where(row == base, n1, jnp.where(row == base + 1, n2, jnp.where(row == base + 2, n3, 0.0)))
    one = 0 if swap else 3
    norm = jnp.where((row >= one) & (row < one + 3), 1.0, norm)
    zero = jnp.zeros_like(x)
    if swap:
        parts = [a, b, a, b, c, a, norm, zero]
    else:
        parts = [a, a, b, b, a, c, norm, zero]
    return jnp.concatenate(parts, axis=0)


def vmem():
    return pl.BlockSpec(memory_space=pltpu.VMEM)


def smem():
    return pl.BlockSpec(memory_space=pltpu.SMEM)


def shape(*dims):
    return jax.ShapeDtypeStruct(dims, F32)


def limit(mib):
    return pltpu.CompilerParams(vmem_limit_bytes=mib << 20)


def spread_kernel(points_ref, scale_ref, initial_ref, ritz_ref, near_ref, pts_ref):
    scaled = points_ref[...] * (scale_ref[...].T * math.sqrt(math.log2(math.e)))
    for b in range(NB // 2):
        near_ref[b, pl.ds(0, FEAT), :] = scaled
        near_ref[b, pl.ds(FEAT, RHS), :] = initial_ref[...]
        near_ref[b, pl.ds(FEAT + RHS, RITZ), :] = ritz_ref[...]
    for b in range(NB):
        pts_ref[b, pl.ds(0, FEAT), :] = scaled
        pts_ref[b, pl.ds(FEAT, RITZ), :] = ritz_ref[...]


def spread(points, scales, initial, ritz):
    return pl.pallas_call(
        spread_kernel,
        out_shape=[shape(NB // 2, FEAT + VEC, BLK), shape(NB, FEAT + RITZ, BLK)],
        compiler_params=limit(8),
        name="spread",
    )(points, scales, initial, ritz)


def tile_kernel(near_ref, far_ref, out_ref, hi_ref, lo_ref, part_ref, cols_ref, rows_ref, vec_ref):
    vec_ref[...] = jnp.zeros_like(vec_ref)
    for b in range(NB):
        src = near_ref if b < NB // 2 else far_ref
        at = b % (NB // 2)
        lanes = pl.ds(b * BLK, BLK)
        cols_ref[:, lanes] = features(src[at, :FEAT, :], False).astype(BF16)
        hi, lo = split2(src[at, FEAT:, :])
        vec_ref[pl.ds(0, VEC), lanes] = hi
        vec_ref[pl.ds(BLK, VEC), lanes] = lo
        rows_ref[lanes, :] = features(out_ref[b, :FEAT, :], True).T.astype(BF16)

    def one_step(step, carry):
        rows = pl.ds(pl.multiple_of(step * STEP, STEP), STEP)
        mine = rows_ref[rows, :]
        total = jnp.zeros((STEP, 2 * BLK), F32)
        for c in range(PTS // CHUNK):
            lanes = pl.ds(c * CHUNK, CHUNK)
            power = jnp.dot(mine, cols_ref[:, lanes], preferred_element_type=F32)
            value = jnp.exp2(jnp.minimum(power, 0.0))
            hi, lo = split2(value)
            hi_ref[rows, lanes] = hi
            lo_ref[rows, lanes] = lo
            vec = vec_ref[:, lanes]
            total += lax.dot_general(hi, vec, NT, preferred_element_type=F32)
            total += lax.dot_general(lo, vec, NT, preferred_element_type=F32)
        both = total[:, :BLK] + total[:, BLK:]
        for h in range(STEP // BLK):
            part_ref[step * (STEP // BLK) + h] = both[h * BLK : (h + 1) * BLK].T[:VEC]
        return carry

    lax.fori_loop(0, PTS // STEP, one_step, 0)


def make_tile(near, far, out):
    return pl.pallas_call(
        tile_kernel,
        in_specs=[vmem(), vmem(), vmem()],
        out_specs=[vmem(), vmem(), vmem()],
        out_shape=[
            pltpu.VMEM((PTS, PTS), BF16),
            pltpu.VMEM((PTS, PTS), BF16),
            shape(NB, VEC, BLK),
        ],
        scratch_shapes=[
            pltpu.VMEM((BLK, PTS), BF16),
            pltpu.VMEM((PTS, BLK), BF16),
            pltpu.VMEM((2 * BLK, PTS), BF16),
        ],
        compiler_params=limit(TILE_MIB),
        name="kernel_tile",
    )(near, far, out)


def owner_kernel(got_ref, initial_ref, ritz_ref, targets_ref, gain_ref, nugget_ref, out_ref):
    total = got_ref[0]
    for b in range(1, NB):
        total += got_ref[b]
    first = targets_ref[...] - (gain_ref[0] * total[:RHS] + nugget_ref[0] * initial_ref[...])
    image = gain_ref[0] * total[RHS:] + nugget_ref[0] * ritz_ref[...]
    for b in range(NB):
        out_ref[b, pl.ds(0, RHS), :] = first
        out_ref[b, pl.ds(RHS, RITZ), :] = image


def at_owner(got, initial, ritz, targets, gain, nugget):
    return pl.pallas_call(
        owner_kernel,
        in_specs=[vmem(), vmem(), vmem(), vmem(), smem(), smem()],
        out_shape=shape(NB, VEC, BLK),
        compiler_params=limit(8),
        name="at_owner",
    )(got, initial, ritz, targets, gain, nugget)


def square_iota():
    return lax.broadcasted_iota(jnp.int32, (RITZ, RITZ), 0), lax.broadcasted_iota(jnp.int32, (RITZ, RITZ), 1)


def gram_kernel(vec_ref, pts_ref, out_ref, left_ref, right_ref):
    for b in range(NB):
        lanes = pl.ds(b * BLK, BLK)
        left_ref[:, lanes] = vec_ref[b]
        right_ref[pl.ds(0, RITZ), lanes] = pts_ref[b, FEAT:, :]
        right_ref[pl.ds(RITZ, RITZ), lanes] = vec_ref[b, RHS:, :]
    gram = lax.dot_general(left_ref[...], right_ref[...], NT, precision=HIGH, preferred_element_type=F32)
    coarse = gram[RHS:, :RITZ]
    coarse = 0.5 * (coarse + coarse.T)
    image = gram[RHS:, RITZ:]
    i, j = square_iota()
    packed = jnp.where(j >= i, coarse, image)
    diagonal = jnp.sum(jnp.where(i == j, image, 0.0), axis=0, keepdims=True)
    for b in range(NB // 2):
        out_ref[b, pl.ds(0, RHS), :] = gram[:RHS]
        out_ref[b, pl.ds(RHS, RITZ // 2), :] = jnp.concatenate([packed[: RITZ // 2], packed[RITZ // 2 :]], axis=1)
        out_ref[b, pl.ds(RHS + RITZ // 2, 1), :] = jnp.concatenate([diagonal, diagonal], axis=1)


def make_gram(vec, pts):
    return pl.pallas_call(
        gram_kernel,
        out_shape=shape(NB // 2, PACKED, BLK),
        scratch_shapes=[pltpu.VMEM((VEC, PTS), F32), pltpu.VMEM((2 * RITZ, PTS), F32)],
        compiler_params=limit(12),
        name="gram",
    )(vec, pts)


def inverse(matrix):
    i, j = square_iota()
    work = jnp.concatenate([matrix, jnp.where(i == j, 1.0, 0.0)], axis=1)
    row = lax.broadcasted_iota(jnp.int32, work.shape, 0)
    for k in range(0, RITZ, 2):
        col0 = jnp.broadcast_to(work[:, k : k + 1], work.shape)
        col1 = jnp.broadcast_to(work[:, k + 1 : k + 2], work.shape)
        a, b = col0[k : k + 1], col1[k : k + 1]
        c, d = col0[k + 1 : k + 2], col1[k + 1 : k + 2]
        top, low = work[k : k + 1], work[k + 1 : k + 2]
        scale = 1.0 / (a * d - b * c)
        new_top = (d * top - b * low) * scale
        new_low = (a * low - c * top) * scale
        work = work - (col0 * new_top + col1 * new_low)
        work = jnp.where(row == k, new_top, jnp.where(row == k + 1, new_low, work))
    return work[:, RITZ:]


def apply_kernel(
    gram_ref, more_ref, hi_ref, lo_ref, vec_ref, pts_ref, initial_ref, place_ref, part_ref, own_ref, both_ref
):
    gram = gram_ref[...] + more_ref[...]
    projected = gram[:RHS, :RITZ]
    first = gram[:RHS, RITZ:]
    square = jnp.concatenate([gram[RHS : RHS + RITZ // 2, :RITZ], gram[RHS : RHS + RITZ // 2, RITZ:]], axis=0)
    turned = square.T
    i, j = square_iota()
    coarse = jnp.where(j >= i, square, turned)
    image = jnp.where(j < i, square, jnp.where(j > i, turned, gram[RHS + RITZ // 2 :, :RITZ]))
    solve = inverse(coarse)
    amounts = lax.dot_general(projected, solve, NT, precision=HIGH, preferred_element_type=F32)
    against = first - jnp.dot(amounts, image, precision=HIGH, preferred_element_type=F32)
    turns = lax.dot_general(against, solve, NT, precision=HIGH, preferred_element_type=F32)
    zero = jnp.zeros_like(turns)
    coef = jnp.concatenate([turns, amounts], axis=1)
    for b in range(NB):
        basis = jnp.concatenate([pts_ref[b, FEAT:, :], vec_ref[b, RHS:, :]], axis=0)
        direction = vec_ref[b, :RHS, :] - jnp.dot(coef, basis, precision=HIGH, preferred_element_type=F32)
        hi = direction.astype(BF16).astype(F32)
        both_ref[:, pl.ds(b * BLK, BLK)] = jnp.concatenate([hi, direction - hi], axis=0).astype(BF16)
    both = both_ref[...]
    for c in range(PTS // CHUNK):
        lanes = pl.ds(c * CHUNK, CHUNK)
        total = jnp.dot(both, hi_ref[:, lanes], preferred_element_type=F32)
        total += jnp.dot(both, lo_ref[:, lanes], preferred_element_type=F32)
        value = total[:RHS] + total[RHS:]
        for h in range(CHUNK // BLK):
            at = c * (CHUNK // BLK) + h
            half = (at // (NB // 2) + place_ref[1]) % 2
            part_ref[half * (NB // 2) + at % (NB // 2)] = value[:, h * BLK : (h + 1) * BLK]
    mine = place_ref[0]
    basis = jnp.concatenate([pts_ref[mine, FEAT:, :], vec_ref[mine, RHS:, :]], axis=0)
    wanted = jnp.concatenate(
        [coef, jnp.concatenate([zero, amounts], axis=1), jnp.concatenate([-amounts, zero], axis=1)], axis=0
    )
    base = vec_ref[mine, :RHS, :]
    base = jnp.concatenate([base, base, initial_ref[...]], axis=0)
    own_ref[...] = base - jnp.dot(wanted, basis, precision=HIGH, preferred_element_type=F32)


def apply_tile(gram, more, hi, lo, vec, pts, initial, place):
    return pl.pallas_call(
        apply_kernel,
        in_specs=[vmem()] * 7 + [smem()],
        out_shape=[shape(NB, RHS, BLK), shape(3 * RHS, BLK)],
        scratch_shapes=[pltpu.VMEM((2 * RHS, PTS), BF16)],
        compiler_params=limit(APPLY_MIB),
        name="apply_tile",
    )(gram, more, hi, lo, vec, pts, initial, place)


def stats_kernel(got_ref, own_ref, gain_ref, nugget_ref, applied_ref, out_ref):
    total = got_ref[0]
    for b in range(1, NB):
        total += got_ref[b]
    direction = own_ref[pl.ds(0, RHS), :]
    residual = own_ref[pl.ds(RHS, RHS), :]
    applied = gain_ref[0] * total + nugget_ref[0] * direction
    applied_ref[...] = applied
    sums = jnp.concatenate(
        [
            jnp.sum(direction * applied, axis=1, keepdims=True),
            jnp.sum(residual * residual, axis=1, keepdims=True),
        ],
        axis=0,
    )
    sums = jnp.broadcast_to(sums, (2 * RHS, BLK)).T[:RHS]
    for b in range(WORLD // RHS):
        out_ref[pl.ds(b * RHS, RHS), :] = sums


def make_stats(got, own, gain, nugget):
    return pl.pallas_call(
        stats_kernel,
        in_specs=[vmem(), vmem(), smem(), smem()],
        out_shape=[shape(RHS, BLK), shape(WORLD, 2 * RHS)],
        compiler_params=limit(8),
        name="stats",
    )(got, own, gain, nugget)


def finish_kernel(got_ref, own_ref, applied_ref, solution_ref, residual_ref):
    sums = jnp.sum(got_ref[...], axis=0, keepdims=True)
    i = lax.broadcasted_iota(jnp.int32, (2 * RHS, 2 * RHS), 0)
    j = lax.broadcasted_iota(jnp.int32, (2 * RHS, 2 * RHS), 1)
    sums = jnp.sum(jnp.where(i == j, sums, 0.0), axis=1, keepdims=True)
    size = sums[RHS:] / sums[:RHS]
    solution_ref[...] = own_ref[pl.ds(2 * RHS, RHS), :] + size * own_ref[pl.ds(0, RHS), :]
    residual_ref[...] = own_ref[pl.ds(RHS, RHS), :] - size * applied_ref[...]


def finish(got, own, applied):
    return pl.pallas_call(
        finish_kernel,
        out_shape=[shape(RHS, BLK), shape(RHS, BLK)],
        compiler_params=limit(8),
        name="finish",
    )(got, own, applied)


def exchange(pieces, axis):
    return lax.all_to_all(pieces, axis, split_axis=0, concat_axis=0, tiled=True)


def other_core(array):
    return lax.ppermute(array, CORE, [(0, 1), (1, 0)])


def local(points, inv_scales, amplitude, noise_var, targets, initial, ritz_basis):
    near, pts = spread(points, inv_scales[None, :], initial, ritz_basis)
    near = exchange(near, Z)
    near, pts = lax.optimization_barrier((near, pts))
    far = other_core(near)
    pts = exchange(pts, XY)
    hi, lo, part = make_tile(near, far, pts)

    vec = exchange(at_owner(exchange(part, XY), initial, ritz_basis, targets, amplitude, noise_var), XY)
    gram = jnp.sum(exchange(make_gram(vec, pts), Z), axis=0)
    place = jnp.stack([lax.axis_index(XY), lax.axis_index(CORE)]).astype(jnp.int32)
    part, own = apply_tile(gram, other_core(gram), hi, lo, vec, pts, initial, place)
    applied, stats = make_stats(exchange(part, CZ), own, amplitude, noise_var)
    return tuple(finish(exchange(stats, EVERY), own, applied))


def solution(mesh):
    torus = Mesh(mesh.devices.reshape(4, 8, 4, 2), ("row_0", "row_1", "col_0", "col_1"))
    in_specs = (
        P(None, COL_ROW),
        P(),
        P(),
        P(),
        P(None, COL_ROW),
        P(None, COL_ROW),
        P(None, COL_ROW),
    )
    out_specs = (P(None, COL_ROW), P(None, COL_ROW))
    return jax.shard_map(local, mesh=torus, in_specs=in_specs, out_specs=out_specs, check_vma=False)
```

time: 176 us -> 158 us (0.90)
  blocking collectives: 31.4 us -> 63.1 us
  waiting for transfers between devices: 49.8 us -> 25.2 us
  other arithmetic: 18.4 us -> 0.09 us
  local copies, waits for them, and re-layouts: 6.41 us -> 18.2 us
  starting transfers between devices: 34.4 us -> 23.2 us
  Pallas kernels: 30.3 us -> 25.5 us
  matrix products: 2.2 us -> 0 us
    all_to_all x2 -> x4, blocking collectives: 31.4 us -> 63.1 us  [exchange(): return lax.all_to_all(pieces, axis, split_axis=0, concat_axis=0, tiled=True)]
    all_to_all x5 -> x3, waiting for transfers between devices: 48.7 us -> 23.1 us  [exchange(): return lax.all_to_all(pieces, axis, split_axis=0, concat_axis=0, tiled=True)]
    unnamed x11 -> x24, local copies, waits for them, and re-layouts: 1.66 us -> 18.2 us
    all_to_all x5 -> x3, starting transfers between devices: 28 us -> 15.3 us  [exchange(): return lax.all_to_all(pieces, axis, split_axis=0, concat_axis=0, tiled=True)]
    another operation x5 -> x1, other arithmetic: 12.1 us -> 0.07 us  [local(): jnp.stack([lax.axis_index(XY), lax.axis_index(CORE)]).astype(jnp.int32)]
    pallas_call x3 -> x7, Pallas kernels: 30.3 us -> 25.5 us  [the longest x1 13.7 us: make_tile(): pl.pallas_call(tile_kernel, in_specs=[vmem(), vmem(), vmem()], out_specs=...]
    broadcast_in_dim x6 -> x0, local copies, waits for them, and re-layouts: 3.88 us -> none  [the longest x5 2.56 us: from_everyone(): jnp.broadcast_to(array, (lax.axis_size(axis), *array.shape))]
    concatenate x5 -> x0, other arithmetic: 2.33 us -> none  [the longest x1 0.78 us: local(): near = from_everyone(jnp.concatenate([points, vectors], 0), Z)]
  transfers between devices with their start and end apart: 7 -> 5, of which waited for: 6 -> 5; matrix products, arithmetic and copies ran while one was open for 1% -> 0% of each run, Pallas kernels for 0% -> 0%
where the time goes in v2:
time: 158 us; the launch traced here: 157 us
  blocking collectives  63.1 us (40%)
  Pallas kernels  25.5 us (16%)
  waiting for transfers between devices  25.2 us (16%)
  starting transfers between devices  23.2 us (15%)
  local copies, waits for them, and re-layouts  18.2 us (12%)
  between operations  1.98 us (1%)
    all_to_all x4, blocking collectives, exchange(): return lax.all_to_all(pieces, axis, split_axis=0, concat_axis=0, tiled=True)  63.1 us
    all_to_all x3, waiting for transfers between devices, exchange(): return lax.all_to_all(pieces, axis, split_axis=0, concat_axis=0, tiled=True)  23.1 us
    unnamed x24, local copies, waits for them, and re-layouts  18.2 us
    all_to_all x3, starting transfers between devices, exchange(): return lax.all_to_all(pieces, axis, split_axis=0, concat_axis=0, tiled=True)  15.3 us
    pallas_call x1, Pallas kernels, make_tile(): pl.pallas_call(tile_kernel, in_specs=[vmem(), vmem(), vmem()], out_specs=...  13.7 us
    ppermute x2, starting transfers between devices, other_core(): return lax.ppermute(array, CORE, [(0, 1), (1, 0)])  7.92 us
    pallas_call x1, Pallas kernels, apply_tile(): pl.pallas_call(apply_kernel, in_specs=[vmem()] * 7 + [smem()], out_shape=...  7.69 us
  transfers between devices with their start and end apart: 5, of which 5 were waited for; matrix products, arithmetic and copies ran while one was open for 0% of the time, Pallas kernels for 0%

profile of v2, /device:TPU:1, one launch (start us, length us, event | category | flops | bytes accessed | tf_op | source)
XLA Modules:
  0.0 157.2 jit_solution(10892194577496478896)
XLA Ops:
  0.6 0.0 copy-start.4
  0.6 0.7 copy-done.4
  1.4 0.0 copy-start.6
  1.4 0.7 copy-done.6
  2.1 0.0 copy-start.9
  2.1 0.7 copy-done.9
  2.8 0.0 copy-start.11
  2.8 0.7 copy-done.11
  3.4 0.0 copy-start.8
  3.4 1.0 spread.1
  4.4 21.8 %all_to_all.41.near_ref = f32[8,88,128]{2,1,0:T(8,128)S(1)} all-to-all(f32[8,88,128]{2,1,0:T(8,128)S(1)} %get-tuple-element.13), channel_id=1, replica_groups=mesh['row_0'=4,'row_1'=8,'col_0'=4,'col_1'=2] {'row_1'}, dimensions={0} | all-to-all | bytes 720896 | tf_op jit(solution)/shard_map/all_to_all | solution.py:331
  26.2 6.8 %all-to-all-start.1 = ((f32[16,80,128]{2,1,0:T(8,128)}), f32[16,80,128]{2,1,0:T(8,128)S(1)}, u32[]{:S(2)}, u32[]{:S(2)}) async-start(f32[16,80,128]{2,1,0:T(8,128)} %get-tuple-element.16), calls=%async_computation.1 | async-start | bytes 1310720 | tf_op jit(solution)/shard_map/all_to_all | solution.py:331
  33.0 2.3 %collective-permute-start = (f32[8,88,128]{2,1,0:T(8,128)S(1)}, f32[8,88,128]{2,1,0:T(8,128)S(1)}, u32[]{:S(2)}, u32[]{:S(2)}) collective-permute-start(f32[8,88,128]{2,1,0:T(8,128)S(1)} %all_to_all.41.near_ref), channel_id=1, source_target_pairs={{0,1},{1,0},{2,3},{3,2},{4,5},{5,4},{6,7},{7,6},{8,9},{9,8},{10,11... | collective-permute-start | bytes 1081352 | tf_op jit(solution)/shard_map/ppermute | solution.py:335
  35.3 1.3 collective-permute-done.far_ref
  36.6 6.4 %all-to-all-done.1.out_ref.pts_ref = f32[16,80,128]{2,1,0:T(8,128)S(1)} async-done(((f32[16,80,128]{2,1,0:T(8,128)}), f32[16,80,128]{2,1,0:T(8,128)S(1)}, u32[]{:S(2)}, u32[]{:S(2)}) %all-to-all-start.1) | async-done | bytes 655392 | tf_op jit(solution)/shard_map/all_to_all | solution.py:331
  43.0 13.7 %kernel_tile.1 = (bf16[2048,2048]{1,0:T(8,128)(2,1)S(1)}, bf16[2048,2048]{1,0:T(8,128)(2,1)S(1)}, f32[16,72,128]{2,1,0:T(8,128)}) custom-call(f32[8,88,128]{2,1,0:T(8,128)S(1)} %all_to_all.41.near_ref, f32[8,88,128]{2,1,0:T(8,128)S(1)} %collective-permute-done.far_ref, f32[16,80,128]{2,1,0:T(8,128)S(1)} %all-to-all-done.1.out_ref.pts_ref), custom_call_target="tpu_custom_call" | custom-call | tf_op jit(solution)/shard_map/kernel_tile/pallas_call | solution.py:137
  56.7 0.0 copy-start
  56.7 3.2 %copy-done = bf16[2048,2048]{1,0:T(8,128)(2,1)} copy-done((bf16[2048,2048]{1,0:T(8,128)(2,1)}, bf16[2048,2048]{1,0:T(8,128)(2,1)S(1)}, u32[]{:S(2)}) %copy-start) | copy-done | bytes 8388632
  60.0 0.0 copy-start.2
  60.0 3.2 %copy-done.2 = bf16[2048,2048]{1,0:T(8,128)(2,1)} copy-done((bf16[2048,2048]{1,0:T(8,128)(2,1)}, bf16[2048,2048]{1,0:T(8,128)(2,1)S(1)}, u32[]{:S(2)}) %copy-start.2) | copy-done | bytes 8388632
  63.2 4.2 %all-to-all-start.2 = ((f32[16,72,128]{2,1,0:T(8,128)}), f32[16,72,128]{2,1,0:T(8,128)S(1)}, u32[]{:S(2)}, u32[]{:S(2)}) async-start(f32[16,72,128]{2,1,0:T(8,128)} %get-tuple-element.17), calls=%async_computation.2 | async-start | bytes 1179648 | tf_op jit(solution)/shard_map/all_to_all | solution.py:331
  68.7 8.1 %all-to-all-done.2.got_ref = f32[16,72,128]{2,1,0:T(8,128)S(1)} async-done(((f32[16,72,128]{2,1,0:T(8,128)}), f32[16,72,128]{2,1,0:T(8,128)S(1)}, u32[]{:S(2)}, u32[]{:S(2)}) %all-to-all-start.2) | async-done | bytes 589856 | tf_op jit(solution)/shard_map/all_to_all | solution.py:331
  76.8 0.0 copy-start.5
  76.8 0.8 copy-done.5
  77.5 0.0 copy-start.7
  77.6 0.7 copy-done.7
  78.2 0.0 copy-start.10
  78.2 0.7 copy-done.10
  78.9 0.1 at_owner.1
  79.0 12.6 %all_to_all.42.vec_ref = f32[16,72,128]{2,1,0:T(8,128)S(1)} all-to-all(f32[16,72,128]{2,1,0:T(8,128)S(1)} %at_owner.1), channel_id=1, replica_groups=mesh['row_0'=4,'row_1'=8,'col_0'=4,'col_1'=2] {'col_0','row_0'}, dimensions={0} | all-to-all | bytes 1179648 | tf_op jit(solution)/shard_map/all_to_all | solution.py:331
  91.6 2.1 %gram.1 = f32[8,41,128]{2,1,0:T(8,128)} custom-call(f32[16,72,128]{2,1,0:T(8,128)S(1)} %all_to_all.42.vec_ref, f32[16,80,128]{2,1,0:T(8,128)S(1)} %all-to-all-done.1.out_ref.pts_ref), custom_call_target="tpu_custom_call" | custom-call | tf_op jit(solution)/shard_map/gram/pallas_call | solution.py:201
  93.6 4.3 %all-to-all-start.4 = ((f32[8,41,128]{2,1,0:T(8,128)}), f32[8,41,128]{2,1,0:T(8,128)S(1)}, u32[]{:S(2)}, u32[]{:S(2)}) async-start(f32[8,41,128]{2,1,0:T(8,128)} %gram.1), calls=%async_computation.4 | async-start | bytes 393216 | tf_op jit(solution)/shard_map/all_to_all | solution.py:331
  97.9 8.6 %all-to-all-done.4 = f32[8,41,128]{2,1,0:T(8,128)S(1)} async-done(((f32[8,41,128]{2,1,0:T(8,128)}), f32[8,41,128]{2,1,0:T(8,128)S(1)}, u32[]{:S(2)}, u32[]{:S(2)}) %all-to-all-start.4) | async-done | bytes 167968 | tf_op jit(solution)/shard_map/all_to_all | solution.py:331
  106.6 5.6 %collective-permute-start.1 = (f32[41,128]{1,0:T(8,128)S(1)}, f32[41,128]{1,0:T(8,128)S(1)}, u32[]{:S(2)}, u32[]{:S(2)}) collective-permute-start(f32[41,128]{1,0:T(8,128)S(1)} %reduce_sum.9.gram_ref), channel_id=1, source_target_pairs={{0,1},{1,0},{2,3},{3,2},{4,5},{5,4},{6,7},{7,6},{8,9},{9,8},{10,11... | collective-permute-start | bytes 62984 | tf_op jit(solution)/shard_map/ppermute | solution.py:335
  112.2 0.1 pad_add_fusion.place_ref
  112.3 0.8 collective-permute-done.1.more_ref
  113.1 0.0 copy-done.8
  113.1 0.0 copy-start.1
  113.1 3.4 %copy-done.1 = bf16[2048,2048]{1,0:T(8,128)(2,1)S(1)} copy-done((bf16[2048,2048]{1,0:T(8,128)(2,1)S(1)}, bf16[2048,2048]{1,0:T(8,128)(2,1)}, u32[]{:S(2)}) %copy-start.1) | copy-done | bytes 8388632
  116.4 0.0 copy-start.3
  116.5 3.4 %copy-done.3 = bf16[2048,2048]{1,0:T(8,128)(2,1)S(1)} copy-done((bf16[2048,2048]{1,0:T(8,128)(2,1)S(1)}, bf16[2048,2048]{1,0:T(8,128)(2,1)}, u32[]{:S(2)}) %copy-start.3) | copy-done | bytes 8388632
  119.8 7.7 %apply_tile.1 = (f32[16,8,128]{2,1,0:T(8,128)S(1)}, f32[24,128]{1,0:T(8,128)S(1)}) custom-call(f32[41,128]{1,0:T(8,128)S(1)} %reduce_sum.9.gram_ref, f32[41,128]{1,0:T(8,128)S(1)} %collective-permute-done.1.more_ref, bf16[2048,2048]{1,0:T(8,128)(2,1)S(1)} %copy-done.1, bf16[2048,2048]{1,0:T(8,128)(2,1)S(1)} %copy-done.3, ...), custom_call_target="tpu_custom_call" | custom-call | tf_op jit(solution)/shard_map/apply_tile/pallas_call | solution.py:271
  127.5 10.0 %all_to_all.43.got_ref = f32[16,8,128]{2,1,0:T(8,128)S(1)} all-to-all(f32[16,8,128]{2,1,0:T(8,128)S(1)} %get-tuple-element.20), channel_id=1, replica_groups=mesh['row_0'=4,'row_1'=8,'col_0'=4,'col_1'=2] {'col_1','row_1'}, dimensions={0} | all-to-all | bytes 131072 | tf_op jit(solution)/shard_map/all_to_all | solution.py:331
  137.5 0.2 stats.1
  137.7 18.8 %all_to_all.44 = f32[256,1,16]{2,1,0:T(1,128)S(1)} all-to-all(f32[256,1,16]{2,1,0:T(1,128)S(1)} %bitcast.8), channel_id=1, replica_groups=mesh['row_0'=4,'row_1'=8,'col_0'=4,'col_1'=2] {'col_0','col_1','row_0','..., dimensions={0} | all-to-all | bytes 32768 | tf_op jit(solution)/shard_map/all_to_all | solution.py:331
  156.5 0.7 finish.1
  (1 shorter events, 0.0 us)
Async XLA Ops:
  0.6 0.8 copy-start.4
  1.4 0.7 copy-start.6
  2.1 0.7 copy-start.9
  2.8 0.7 copy-start.11
  3.4 109.6 %copy-start.8 = (f32[8,128]{1,0:T(8,128)S(1)}, f32[8,128]{1,0:T(8,128)}, u32[]{:S(2)}) copy-start(f32[8,128]{1,0:T(8,128)} %initial_ref.5) | copy-start | bytes 12292
  26.2 16.7 %all-to-all-start.1 = ((f32[16,80,128]{2,1,0:T(8,128)}), f32[16,80,128]{2,1,0:T(8,128)S(1)}, u32[]{:S(2)}, u32[]{:S(2)}) async-start(f32[16,80,128]{2,1,0:T(8,128)} %get-tuple-element.16), calls=%async_computation.1 | async-start | bytes 1310720 | tf_op jit(solution)/shard_map/all_to_all | solution.py:331
  33.0 3.6 %collective-permute-start = (f32[8,88,128]{2,1,0:T(8,128)S(1)}, f32[8,88,128]{2,1,0:T(8,128)S(1)}, u32[]{:S(2)}, u32[]{:S(2)}) collective-permute-start(f32[8,88,128]{2,1,0:T(8,128)S(1)} %all_to_all.41.near_ref), channel_id=1, source_target_pairs={{0,1},{1,0},{2,3},{3,2},{4,5},{5,4},{6,7},{7,6},{8,9},{9,8},{10,11... | collective-permute-start | bytes 1081352 | tf_op jit(solution)/shard_map/ppermute | solution.py:335
  56.7 3.2 %copy-start = (bf16[2048,2048]{1,0:T(8,128)(2,1)}, bf16[2048,2048]{1,0:T(8,128)(2,1)S(1)}, u32[]{:S(2)}) copy-start(bf16[2048,2048]{1,0:T(8,128)(2,1)S(1)} %get-tuple-element.18.hi_ref) | copy-start | bytes 25165828
  60.0 3.2 %copy-start.2 = (bf16[2048,2048]{1,0:T(8,128)(2,1)}, bf16[2048,2048]{1,0:T(8,128)(2,1)S(1)}, u32[]{:S(2)}) copy-start(bf16[2048,2048]{1,0:T(8,128)(2,1)S(1)} %get-tuple-element.19.lo_ref) | copy-start | bytes 25165828
  63.2 13.6 %all-to-all-start.2 = ((f32[16,72,128]{2,1,0:T(8,128)}), f32[16,72,128]{2,1,0:T(8,128)S(1)}, u32[]{:S(2)}, u32[]{:S(2)}) async-start(f32[16,72,128]{2,1,0:T(8,128)} %get-tuple-element.17), calls=%async_computation.2 | async-start | bytes 1179648 | tf_op jit(solution)/shard_map/all_to_all | solution.py:331
  76.8 0.8 copy-start.5
  77.5 0.7 copy-start.7
  78.2 0.7 copy-start.10
  93.6 13.0 %all-to-all-start.4 = ((f32[8,41,128]{2,1,0:T(8,128)}), f32[8,41,128]{2,1,0:T(8,128)S(1)}, u32[]{:S(2)}, u32[]{:S(2)}) async-start(f32[8,41,128]{2,1,0:T(8,128)} %gram.1), calls=%async_computation.4 | async-start | bytes 393216 | tf_op jit(solution)/shard_map/all_to_all | solution.py:331
  106.6 6.5 %collective-permute-start.1 = (f32[41,128]{1,0:T(8,128)S(1)}, f32[41,128]{1,0:T(8,128)S(1)}, u32[]{:S(2)}, u32[]{:S(2)}) collective-permute-start(f32[41,128]{1,0:T(8,128)S(1)} %reduce_sum.9.gram_ref), channel_id=1, source_target_pairs={{0,1},{1,0},{2,3},{3,2},{4,5},{5,4},{6,7},{7,6},{8,9},{9,8},{10,11... | collective-permute-start | bytes 62984 | tf_op jit(solution)/shard_map/ppermute | solution.py:335
  113.1 3.4 %copy-start.1 = (bf16[2048,2048]{1,0:T(8,128)(2,1)S(1)}, bf16[2048,2048]{1,0:T(8,128)(2,1)}, u32[]{:S(2)}) copy-start(bf16[2048,2048]{1,0:T(8,128)(2,1)} %copy-done) | copy-start | bytes 25165828
  116.4 3.4 %copy-start.3 = (bf16[2048,2048]{1,0:T(8,128)(2,1)S(1)}, bf16[2048,2048]{1,0:T(8,128)(2,1)}, u32[]{:S(2)}) copy-start(bf16[2048,2048]{1,0:T(8,128)(2,1)} %copy-done.2) | copy-start | bytes 25165828

commit v3 on v2

--- a/solution.py
+++ b/solution.py
@@ -22,12 +22,10 @@
 BLK = 128
 NB = 16
 PTS = NB * BLK
-STEP = 256
-CHUNK = 512
+STEP = 512
+CHUNK = 256
 PACKED = RHS + RITZ // 2 + 1
 WORLD = 256
-TILE_MIB = 12
-APPLY_MIB = 8
 
 HIGH = lax.Precision.HIGHEST
 F32 = jnp.float32
@@ -67,6 +65,10 @@
     return pl.BlockSpec(memory_space=pltpu.VMEM)
 
 
+def in_hbm(array):
+    return pltpu.with_memory_space_constraint(array, pltpu.HBM)
+
+
 def smem():
     return pl.BlockSpec(memory_space=pltpu.SMEM)
 
@@ -79,99 +81,137 @@
     return pltpu.CompilerParams(vmem_limit_bytes=mib << 20)
 
 
-def spread_kernel(points_ref, scale_ref, initial_ref, ritz_ref, near_ref, pts_ref):
+def hbm():
+    return pl.BlockSpec(memory_space=pltpu.HBM)
+
+
+def spread_kernel(
+    points_hbm, scale_hbm, initial_hbm, ritz_hbm, targets_hbm, near_ref, pts_ref, held_ref, points_ref, scale_ref, sem
+):
+    copies = [
+        pltpu.make_async_copy(points_hbm, points_ref, sem.at[0]),
+        pltpu.make_async_copy(scale_hbm, scale_ref, sem.at[1]),
+        pltpu.make_async_copy(targets_hbm, held_ref.at[pl.ds(0, RHS)], sem.at[2]),
+        pltpu.make_async_copy(initial_hbm, held_ref.at[pl.ds(RHS, RHS)], sem.at[3]),
+        pltpu.make_async_copy(ritz_hbm, held_ref.at[pl.ds(2 * RHS, RITZ)], sem.at[4]),
+    ]
+    for copy in copies:
+        copy.start()
+    for copy in copies:
+        copy.wait()
     scaled = points_ref[...] * (scale_ref[...].T * math.sqrt(math.log2(math.e)))
     for b in range(NB // 2):
         near_ref[b, pl.ds(0, FEAT), :] = scaled
-        near_ref[b, pl.ds(FEAT, RHS), :] = initial_ref[...]
-        near_ref[b, pl.ds(FEAT + RHS, RITZ), :] = ritz_ref[...]
+        near_ref[b, pl.ds(FEAT, VEC), :] = held_ref[pl.ds(RHS, VEC), :]
     for b in range(NB):
         pts_ref[b, pl.ds(0, FEAT), :] = scaled
-        pts_ref[b, pl.ds(FEAT, RITZ), :] = ritz_ref[...]
-
-
-def spread(points, scales, initial, ritz):
+        pts_ref[b, pl.ds(FEAT, RITZ), :] = held_ref[pl.ds(2 * RHS, RITZ), :]
+
+
+def spread(points, scales, initial, ritz, targets):
     return pl.pallas_call(
         spread_kernel,
-        out_shape=[shape(NB // 2, FEAT + VEC, BLK), shape(NB, FEAT + RITZ, BLK)],
+        in_specs=[hbm()] * 5,
+        out_specs=[vmem()] * 3,
+        out_shape=[shape(NB // 2, FEAT + VEC, BLK), shape(NB, FEAT + RITZ, BLK), shape(RHS + VEC, BLK)],
+        scratch_shapes=[
+            pltpu.VMEM((FEAT, BLK), F32),
+            pltpu.VMEM((1, FEAT), F32),
+            pltpu.SemaphoreType.DMA((5,)),
+        ],
         compiler_params=limit(8),
         name="spread",
-    )(points, scales, initial, ritz)
-
-
-def tile_kernel(near_ref, far_ref, out_ref, hi_ref, lo_ref, part_ref, cols_ref, rows_ref, vec_ref):
-    vec_ref[...] = jnp.zeros_like(vec_ref)
+    )(*map(in_hbm, (points, scales, initial, ritz, targets)))
+
+
+def tile_kernel(
+    near_ref, far_ref, out_ref, hi_hbm, lo_hbm, part_ref, hi_ref, lo_ref, cols_ref, rows_ref, vec_ref, sem
+):
     for b in range(NB):
         src = near_ref if b < NB // 2 else far_ref
         at = b % (NB // 2)
         lanes = pl.ds(b * BLK, BLK)
         cols_ref[:, lanes] = features(src[at, :FEAT, :], False).astype(BF16)
-        hi, lo = split2(src[at, FEAT:, :])
-        vec_ref[pl.ds(0, VEC), lanes] = hi
-        vec_ref[pl.ds(BLK, VEC), lanes] = lo
+        tall = jnp.concatenate([src[at, FEAT:, :], jnp.zeros((BLK - VEC, BLK), F32)], axis=0).T
+        hi, lo = split2(tall)
+        vec_ref[lanes, pl.ds(0, BLK)] = hi
+        vec_ref[lanes, pl.ds(BLK, BLK)] = lo
         rows_ref[lanes, :] = features(out_ref[b, :FEAT, :], True).T.astype(BF16)
+
+    def copies(step):
+        rows = pl.ds(pl.multiple_of(step * STEP, STEP), STEP)
+        return (
+            pltpu.make_async_copy(hi_ref.at[rows], hi_hbm.at[rows], sem.at[0, step]),
+            pltpu.make_async_copy(lo_ref.at[rows], lo_hbm.at[rows], sem.at[1, step]),
+        )
 
     def one_step(step, carry):
         rows = pl.ds(pl.multiple_of(step * STEP, STEP), STEP)
         mine = rows_ref[rows, :]
-        total = jnp.zeros((STEP, 2 * BLK), F32)
         for c in range(PTS // CHUNK):
             lanes = pl.ds(c * CHUNK, CHUNK)
             power = jnp.dot(mine, cols_ref[:, lanes], preferred_element_type=F32)
-            value = jnp.exp2(jnp.minimum(power, 0.0))
-            hi, lo = split2(value)
+            hi, lo = split2(jnp.exp2(jnp.minimum(power, 0.0)))
             hi_ref[rows, lanes] = hi
             lo_ref[rows, lanes] = lo
-            vec = vec_ref[:, lanes]
-            total += lax.dot_general(hi, vec, NT, preferred_element_type=F32)
-            total += lax.dot_general(lo, vec, NT, preferred_element_type=F32)
+        for copy in copies(step):
+            copy.start()
+        total = jnp.dot(hi_ref[rows, :], vec_ref[...], preferred_element_type=F32)
+        total += jnp.dot(lo_ref[rows, :], vec_ref[...], preferred_element_type=F32)
         both = total[:, :BLK] + total[:, BLK:]
         for h in range(STEP // BLK):
             part_ref[step * (STEP // BLK) + h] = both[h * BLK : (h + 1) * BLK].T[:VEC]
         return carry
 
     lax.fori_loop(0, PTS // STEP, one_step, 0)
+    for step in range(PTS // STEP):
+        for copy in copies(step):
+            copy.wait()
 
 
 def make_tile(near, far, out):
     return pl.pallas_call(
         tile_kernel,
         in_specs=[vmem(), vmem(), vmem()],
-        out_specs=[vmem(), vmem(), vmem()],
+        out_specs=[hbm(), hbm(), vmem()],
         out_shape=[
-            pltpu.VMEM((PTS, PTS), BF16),
-            pltpu.VMEM((PTS, PTS), BF16),
+            pltpu.HBM((PTS, PTS), BF16),
+            pltpu.HBM((PTS, PTS), BF16),
             shape(NB, VEC, BLK),
         ],
         scratch_shapes=[
+            pltpu.VMEM((PTS, PTS), BF16),
+            pltpu.VMEM((PTS, PTS), BF16),
             pltpu.VMEM((BLK, PTS), BF16),
             pltpu.VMEM((PTS, BLK), BF16),
-            pltpu.VMEM((2 * BLK, PTS), BF16),
+            pltpu.VMEM((PTS, 2 * BLK), BF16),
+            pltpu.SemaphoreType.DMA((2, PTS // STEP)),
         ],
-        compiler_params=limit(TILE_MIB),
+        compiler_params=limit(40),
         name="kernel_tile",
     )(near, far, out)
 
 
-def owner_kernel(got_ref, initial_ref, ritz_ref, targets_ref, gain_ref, nugget_ref, out_ref):
+def owner_kernel(got_ref, held_ref, gain_ref, nugget_ref, out_ref):
     total = got_ref[0]
     for b in range(1, NB):
         total += got_ref[b]
-    first = targets_ref[...] - (gain_ref[0] * total[:RHS] + nugget_ref[0] * initial_ref[...])
-    image = gain_ref[0] * total[RHS:] + nugget_ref[0] * ritz_ref[...]
+    applied = gain_ref[0] * total + nugget_ref[0] * held_ref[pl.ds(RHS, VEC), :]
+    first = held_ref[pl.ds(0, RHS), :] - applied[:RHS]
+    image = applied[RHS:]
     for b in range(NB):
         out_ref[b, pl.ds(0, RHS), :] = first
         out_ref[b, pl.ds(RHS, RITZ), :] = image
 
 
-def at_owner(got, initial, ritz, targets, gain, nugget):
+def at_owner(got, held, gain, nugget):
     return pl.pallas_call(
         owner_kernel,
-        in_specs=[vmem(), vmem(), vmem(), vmem(), smem(), smem()],
+        in_specs=[vmem(), vmem(), smem(), smem()],
         out_shape=shape(NB, VEC, BLK),
         compiler_params=limit(8),
         name="at_owner",
-    )(got, initial, ritz, targets, gain, nugget)
+    )(got, held, gain, nugget)
 
 
 def square_iota():
@@ -226,8 +266,33 @@
 
 
 def apply_kernel(
-    gram_ref, more_ref, hi_ref, lo_ref, vec_ref, pts_ref, initial_ref, place_ref, part_ref, own_ref, both_ref
+    gram_ref,
+    more_ref,
+    hi_hbm,
+    lo_hbm,
+    vec_ref,
+    pts_ref,
+    held_ref,
+    place_ref,
+    part_ref,
+    own_ref,
+    both_ref,
+    hi_ref,
+    lo_ref,
+    sum_ref,
+    sem,
 ):
+    copies = []
+    for step in range(PTS // STEP):
+        rows = pl.ds(step * STEP, STEP)
+        copies.append(
+            (
+                pltpu.make_async_copy(hi_hbm.at[rows], hi_ref.at[rows], sem.at[0, step]),
+                pltpu.make_async_copy(lo_hbm.at[rows], lo_ref.at[rows], sem.at[1, step]),
+            )
+        )
+        for copy in copies[-1]:
+            copy.start()
     gram = gram_ref[...] + more_ref[...]
     projected = gram[:RHS, :RITZ]
     first = gram[:RHS, RITZ:]
@@ -247,35 +312,46 @@
         direction = vec_ref[b, :RHS, :] - jnp.dot(coef, basis, precision=HIGH, preferred_element_type=F32)
         hi = direction.astype(BF16).astype(F32)
         both_ref[:, pl.ds(b * BLK, BLK)] = jnp.concatenate([hi, direction - hi], axis=0).astype(BF16)
-    both = both_ref[...]
-    for c in range(PTS // CHUNK):
-        lanes = pl.ds(c * CHUNK, CHUNK)
-        total = jnp.dot(both, hi_ref[:, lanes], preferred_element_type=F32)
-        total += jnp.dot(both, lo_ref[:, lanes], preferred_element_type=F32)
-        value = total[:RHS] + total[RHS:]
-        for h in range(CHUNK // BLK):
-            at = c * (CHUNK // BLK) + h
-            half = (at // (NB // 2) + place_ref[1]) % 2
-            part_ref[half * (NB // 2) + at % (NB // 2)] = value[:, h * BLK : (h + 1) * BLK]
+    for step in range(PTS // STEP):
+        rows = pl.ds(step * STEP, STEP)
+        both = both_ref[:, rows]
+        for copy in copies[step]:
+            copy.wait()
+        total = jnp.dot(both, hi_ref[rows, :], preferred_element_type=F32)
+        total += jnp.dot(both, lo_ref[rows, :], preferred_element_type=F32)
+        if step == 0:
+            sum_ref[...] = total
+        else:
+            sum_ref[...] += total
+    for at in range(NB):
+        lanes = pl.ds(at * BLK, BLK)
+        half = (at // (NB // 2) + place_ref[1]) % 2
+        part_ref[half * (NB // 2) + at % (NB // 2)] = sum_ref[pl.ds(0, RHS), lanes] + sum_ref[pl.ds(RHS, RHS), lanes]
     mine = place_ref[0]
     basis = jnp.concatenate([pts_ref[mine, FEAT:, :], vec_ref[mine, RHS:, :]], axis=0)
     wanted = jnp.concatenate(
         [coef, jnp.concatenate([zero, amounts], axis=1), jnp.concatenate([-amounts, zero], axis=1)], axis=0
     )
     base = vec_ref[mine, :RHS, :]
-    base = jnp.concatenate([base, base, initial_ref[...]], axis=0)
+    base = jnp.concatenate([base, base, held_ref[pl.ds(RHS, RHS), :]], axis=0)
     own_ref[...] = base - jnp.dot(wanted, basis, precision=HIGH, preferred_element_type=F32)
 
 
-def apply_tile(gram, more, hi, lo, vec, pts, initial, place):
+def apply_tile(gram, more, hi, lo, vec, pts, held, place):
     return pl.pallas_call(
         apply_kernel,
-        in_specs=[vmem()] * 7 + [smem()],
+        in_specs=[vmem(), vmem(), hbm(), hbm(), vmem(), vmem(), vmem(), smem()],
         out_shape=[shape(NB, RHS, BLK), shape(3 * RHS, BLK)],
-        scratch_shapes=[pltpu.VMEM((2 * RHS, PTS), BF16)],
-        compiler_params=limit(APPLY_MIB),
+        scratch_shapes=[
+            pltpu.VMEM((2 * RHS, PTS), BF16),
+            pltpu.VMEM((PTS, PTS), BF16),
+            pltpu.VMEM((PTS, PTS), BF16),
+            pltpu.VMEM((2 * RHS, PTS), F32),
+            pltpu.SemaphoreType.DMA((2, PTS // STEP)),
+        ],
+        compiler_params=limit(32),
         name="apply_tile",
-    )(gram, more, hi, lo, vec, pts, initial, place)
+    )(gram, more, in_hbm(hi), in_hbm(lo), vec, pts, held, place)
 
 
 def stats_kernel(got_ref, own_ref, gain_ref, nugget_ref, applied_ref, out_ref):
@@ -336,17 +412,17 @@
 
 
 def local(points, inv_scales, amplitude, noise_var, targets, initial, ritz_basis):
-    near, pts = spread(points, inv_scales[None, :], initial, ritz_basis)
+    near, pts, held = spread(points, inv_scales[None, :], initial, ritz_basis, targets)
     near = exchange(near, Z)
     near, pts = lax.optimization_barrier((near, pts))
     far = other_core(near)
     pts = exchange(pts, XY)
     hi, lo, part = make_tile(near, far, pts)
 
-    vec = exchange(at_owner(exchange(part, XY), initial, ritz_basis, targets, amplitude, noise_var), XY)
+    vec = exchange(at_owner(exchange(part, XY), held, amplitude, noise_var), XY)
     gram = jnp.sum(exchange(make_gram(vec, pts), Z), axis=0)
     place = jnp.stack([lax.axis_index(XY), lax.axis_index(CORE)]).astype(jnp.int32)
-    part, own = apply_tile(gram, other_core(gram), hi, lo, vec, pts, initial, place)
+    part, own = apply_tile(gram, other_core(gram), hi, lo, vec, pts, held, place)
     applied, stats = make_stats(exchange(part, CZ), own, amplitude, noise_var)
     return tuple(finish(exchange(stats, EVERY), own, applied))
 

time: 158 us -> 142 us (0.90)
  local copies, waits for them, and re-layouts: 18.2 us -> 0 us
  Pallas kernels: 25.5 us -> 27.7 us
    unnamed x24 -> x0, local copies, waits for them, and re-layouts: 18.2 us -> none
    pallas_call x3, Pallas kernels: 8.75 us -> 12.3 us  [the longest x1 10.4 us: apply_tile(): pl.pallas_call(apply_kernel, in_specs=[vmem(), vmem(), hbm(), hbm(), vmem...]
where the time goes in v3:
time: 142 us; the launch traced here: 141 us
  blocking collectives  63.1 us (44%)
  Pallas kernels  27.7 us (20%)
  waiting for transfers between devices  25.2 us (18%)
  starting transfers between devices  23.2 us (16%)
  between operations  1.98 us (1%)
    all_to_all x4, blocking collectives, exchange(): return lax.all_to_all(pieces, axis, split_axis=0, concat_axis=0, tiled=True)  63.1 us
    all_to_all x3, waiting for transfers between devices, exchange(): return lax.all_to_all(pieces, axis, split_axis=0, concat_axis=0, tiled=True)  23.1 us
    all_to_all x3, starting transfers between devices, exchange(): return lax.all_to_all(pieces, axis, split_axis=0, concat_axis=0, tiled=True)  15.3 us
    pallas_call x1, Pallas kernels, make_tile(): pl.pallas_call(tile_kernel, in_specs=[vmem(), vmem(), vmem()], out_specs=...  12.4 us
    pallas_call x1, Pallas kernels, apply_tile(): pl.pallas_call(apply_kernel, in_specs=[vmem(), vmem(), hbm(), hbm(), vmem...  10.4 us
    ppermute x2, starting transfers between devices, other_core(): return lax.ppermute(array, CORE, [(0, 1), (1, 0)])  7.91 us
  transfers between devices with their start and end apart: 5, of which 5 were waited for; matrix products, arithmetic and copies ran while one was open for 0% of the time, Pallas kernels for 0%

profile of v3, /device:TPU:1, one launch (start us, length us, event | category | flops | bytes accessed | tf_op | source)
XLA Modules:
  0.0 141.3 jit_solution(13417210599469745193)
XLA Ops:
  0.6 1.9 %spread.1 = (f32[8,88,128]{2,1,0:T(8,128)S(1)}, f32[16,80,128]{2,1,0:T(8,128)}, f32[80,128]{1,0:T(8,128)S(1)}) custom-call(f32[16,128]{1,0:T(8,128)} %points_hbm.1, f32[1,16]{1,0:T(1,128)} %bitcast.9, f32[8,128]{1,0:T(8,128)} %initial_hbm.1, f32[64,128]{1,0:T(8,128)} %ritz_hbm.1, f32[8,128]{1,0:T(8,128)} %targets_hbm.1), custom_call_target="tpu_custom_call" | custom-call | tf_op jit(solution)/shard_map/spread/pallas_call | solution.py:112
  2.5 21.8 %all_to_all.41.near_ref = f32[8,88,128]{2,1,0:T(8,128)S(1)} all-to-all(f32[8,88,128]{2,1,0:T(8,128)S(1)} %get-tuple-element.14), channel_id=1, replica_groups=mesh['row_0'=4,'row_1'=8,'col_0'=4,'col_1'=2] {'row_1'}, dimensions={0} | all-to-all | bytes 720896 | tf_op jit(solution)/shard_map/all_to_all | solution.py:407
  24.3 6.8 %all-to-all-start.1 = ((f32[16,80,128]{2,1,0:T(8,128)}), f32[16,80,128]{2,1,0:T(8,128)S(1)}, u32[]{:S(2)}, u32[]{:S(2)}) async-start(f32[16,80,128]{2,1,0:T(8,128)} %get-tuple-element.17), calls=%async_computation.1 | async-start | bytes 1310720 | tf_op jit(solution)/shard_map/all_to_all | solution.py:407
  31.1 2.3 %collective-permute-start = (f32[8,88,128]{2,1,0:T(8,128)S(1)}, f32[8,88,128]{2,1,0:T(8,128)S(1)}, u32[]{:S(2)}, u32[]{:S(2)}) collective-permute-start(f32[8,88,128]{2,1,0:T(8,128)S(1)} %all_to_all.41.near_ref), channel_id=1, source_target_pairs={{0,1},{1,0},{2,3},{3,2},{4,5},{5,4},{6,7},{7,6},{8,9},{9,8},{10,11... | collective-permute-start | bytes 1081352 | tf_op jit(solution)/shard_map/ppermute | solution.py:411
  33.4 1.3 collective-permute-done.far_ref
  34.7 6.4 %all-to-all-done.1.out_ref.pts_ref = f32[16,80,128]{2,1,0:T(8,128)S(1)} async-done(((f32[16,80,128]{2,1,0:T(8,128)}), f32[16,80,128]{2,1,0:T(8,128)S(1)}, u32[]{:S(2)}, u32[]{:S(2)}) %all-to-all-start.1) | async-done | bytes 655392 | tf_op jit(solution)/shard_map/all_to_all | solution.py:407
  41.1 12.4 %kernel_tile.1 = (bf16[2048,2048]{1,0:T(8,128)(2,1)}, bf16[2048,2048]{1,0:T(8,128)(2,1)}, f32[16,72,128]{2,1,0:T(8,128)}) custom-call(f32[8,88,128]{2,1,0:T(8,128)S(1)} %all_to_all.41.near_ref, f32[8,88,128]{2,1,0:T(8,128)S(1)} %collective-permute-done.far_ref, f32[16,80,128]{2,1,0:T(8,128)S(1)} %all-to-all-done.1.out_ref.pts_ref), custom_call_target="tpu_custom_call" | custom-call | tf_op jit(solution)/shard_map/kernel_tile/pallas_call | solution.py:173
  53.4 4.2 %all-to-all-start.2 = ((f32[16,72,128]{2,1,0:T(8,128)}), f32[16,72,128]{2,1,0:T(8,128)S(1)}, u32[]{:S(2)}, u32[]{:S(2)}) async-start(f32[16,72,128]{2,1,0:T(8,128)} %get-tuple-element.18), calls=%async_computation.2 | async-start | bytes 1179648 | tf_op jit(solution)/shard_map/all_to_all | solution.py:407
  59.0 8.1 %all-to-all-done.2.got_ref = f32[16,72,128]{2,1,0:T(8,128)S(1)} async-done(((f32[16,72,128]{2,1,0:T(8,128)}), f32[16,72,128]{2,1,0:T(8,128)S(1)}, u32[]{:S(2)}, u32[]{:S(2)}) %all-to-all-start.2) | async-done | bytes 589856 | tf_op jit(solution)/shard_map/all_to_all | solution.py:407
  67.1 0.1 at_owner.1
  67.1 12.6 %all_to_all.42.vec_ref = f32[16,72,128]{2,1,0:T(8,128)S(1)} all-to-all(f32[16,72,128]{2,1,0:T(8,128)S(1)} %at_owner.1), channel_id=1, replica_groups=mesh['row_0'=4,'row_1'=8,'col_0'=4,'col_1'=2] {'col_0','row_0'}, dimensions={0} | all-to-all | bytes 1179648 | tf_op jit(solution)/shard_map/all_to_all | solution.py:407
  79.7 2.1 %gram.1 = f32[8,41,128]{2,1,0:T(8,128)} custom-call(f32[16,72,128]{2,1,0:T(8,128)S(1)} %all_to_all.42.vec_ref, f32[16,80,128]{2,1,0:T(8,128)S(1)} %all-to-all-done.1.out_ref.pts_ref), custom_call_target="tpu_custom_call" | custom-call | tf_op jit(solution)/shard_map/gram/pallas_call | solution.py:241
  81.8 4.3 %all-to-all-start.4 = ((f32[8,41,128]{2,1,0:T(8,128)}), f32[8,41,128]{2,1,0:T(8,128)S(1)}, u32[]{:S(2)}, u32[]{:S(2)}) async-start(f32[8,41,128]{2,1,0:T(8,128)} %gram.1), calls=%async_computation.4 | async-start | bytes 393216 | tf_op jit(solution)/shard_map/all_to_all | solution.py:407
  86.1 8.6 %all-to-all-done.4 = f32[8,41,128]{2,1,0:T(8,128)S(1)} async-done(((f32[8,41,128]{2,1,0:T(8,128)}), f32[8,41,128]{2,1,0:T(8,128)S(1)}, u32[]{:S(2)}, u32[]{:S(2)}) %all-to-all-start.4) | async-done | bytes 167968 | tf_op jit(solution)/shard_map/all_to_all | solution.py:407
  94.7 5.6 %collective-permute-start.1 = (f32[41,128]{1,0:T(8,128)S(1)}, f32[41,128]{1,0:T(8,128)S(1)}, u32[]{:S(2)}, u32[]{:S(2)}) collective-permute-start(f32[41,128]{1,0:T(8,128)S(1)} %reduce_sum.9.gram_ref), channel_id=1, source_target_pairs={{0,1},{1,0},{2,3},{3,2},{4,5},{5,4},{6,7},{7,6},{8,9},{9,8},{10,11... | collective-permute-start | bytes 62984 | tf_op jit(solution)/shard_map/ppermute | solution.py:411
  100.4 0.1 pad_add_fusion.place_ref
  100.4 0.8 collective-permute-done.1.more_ref
  101.2 10.4 %apply_tile.1 = (f32[16,8,128]{2,1,0:T(8,128)S(1)}, f32[24,128]{1,0:T(8,128)S(1)}) custom-call(f32[41,128]{1,0:T(8,128)S(1)} %reduce_sum.9.gram_ref, f32[41,128]{1,0:T(8,128)S(1)} %collective-permute-done.1.more_ref, bf16[2048,2048]{1,0:T(8,128)(2,1)} %get-tuple-element.20.hi_hbm, bf16[2048,2048]{1,0:T(8,128)(2,1)} %get-tuple-element.21.lo_hbm, ...), custom_call_target="tpu_custom_call" | custom-call | tf_op jit(solution)/shard_map/apply_tile/pallas_call | solution.py:341
  111.6 10.0 %all_to_all.43.got_ref = f32[16,8,128]{2,1,0:T(8,128)S(1)} all-to-all(f32[16,8,128]{2,1,0:T(8,128)S(1)} %get-tuple-element.22), channel_id=1, replica_groups=mesh['row_0'=4,'row_1'=8,'col_0'=4,'col_1'=2] {'col_1','row_1'}, dimensions={0} | all-to-all | bytes 131072 | tf_op jit(solution)/shard_map/all_to_all | solution.py:407
  121.6 0.2 stats.1
  121.8 18.8 %all_to_all.44 = f32[256,1,16]{2,1,0:T(1,128)S(1)} all-to-all(f32[256,1,16]{2,1,0:T(1,128)S(1)} %bitcast.8), channel_id=1, replica_groups=mesh['row_0'=4,'row_1'=8,'col_0'=4,'col_1'=2] {'col_0','col_1','row_0','..., dimensions={0} | all-to-all | bytes 32768 | tf_op jit(solution)/shard_map/all_to_all | solution.py:407
  140.6 0.7 finish.1
  (1 shorter events, 0.0 us)
Async XLA Ops:
  24.3 16.7 %all-to-all-start.1 = ((f32[16,80,128]{2,1,0:T(8,128)}), f32[16,80,128]{2,1,0:T(8,128)S(1)}, u32[]{:S(2)}, u32[]{:S(2)}) async-start(f32[16,80,128]{2,1,0:T(8,128)} %get-tuple-element.17), calls=%async_computation.1 | async-start | bytes 1310720 | tf_op jit(solution)/shard_map/all_to_all | solution.py:407
  31.1 3.6 %collective-permute-start = (f32[8,88,128]{2,1,0:T(8,128)S(1)}, f32[8,88,128]{2,1,0:T(8,128)S(1)}, u32[]{:S(2)}, u32[]{:S(2)}) collective-permute-start(f32[8,88,128]{2,1,0:T(8,128)S(1)} %all_to_all.41.near_ref), channel_id=1, source_target_pairs={{0,1},{1,0},{2,3},{3,2},{4,5},{5,4},{6,7},{7,6},{8,9},{9,8},{10,11... | collective-permute-start | bytes 1081352 | tf_op jit(solution)/shard_map/ppermute | solution.py:411
  53.4 13.6 %all-to-all-start.2 = ((f32[16,72,128]{2,1,0:T(8,128)}), f32[16,72,128]{2,1,0:T(8,128)S(1)}, u32[]{:S(2)}, u32[]{:S(2)}) async-start(f32[16,72,128]{2,1,0:T(8,128)} %get-tuple-element.18), calls=%async_computation.2 | async-start | bytes 1179648 | tf_op jit(solution)/shard_map/all_to_all | solution.py:407
  81.8 13.0 %all-to-all-start.4 = ((f32[8,41,128]{2,1,0:T(8,128)}), f32[8,41,128]{2,1,0:T(8,128)S(1)}, u32[]{:S(2)}, u32[]{:S(2)}) async-start(f32[8,41,128]{2,1,0:T(8,128)} %gram.1), calls=%async_computation.4 | async-start | bytes 393216 | tf_op jit(solution)/shard_map/all_to_all | solution.py:407
  94.7 6.5 %collective-permute-start.1 = (f32[41,128]{1,0:T(8,128)S(1)}, f32[41,128]{1,0:T(8,128)S(1)}, u32[]{:S(2)}, u32[]{:S(2)}) collective-permute-start(f32[41,128]{1,0:T(8,128)S(1)} %reduce_sum.9.gram_ref), channel_id=1, source_target_pairs={{0,1},{1,0},{2,3},{3,2},{4,5},{5,4},{6,7},{7,6},{8,9},{9,8},{10,11... | collective-permute-start | bytes 62984 | tf_op jit(solution)/shard_map/ppermute | solution.py:411

commit v4 on v3

--- a/solution.py
+++ b/solution.py
@@ -22,8 +22,10 @@
 BLK = 128
 NB = 16
 PTS = NB * BLK
-STEP = 512
+STEP = 256
 CHUNK = 256
+READ = 512
+HALF = 2 * RHS + 2 * RITZ
 PACKED = RHS + RITZ // 2 + 1
 WORLD = 256
 
@@ -139,32 +141,35 @@
         rows_ref[lanes, :] = features(out_ref[b, :FEAT, :], True).T.astype(BF16)
 
     def copies(step):
-        rows = pl.ds(pl.multiple_of(step * STEP, STEP), STEP)
+        rows = pl.ds(step * STEP, STEP)
         return (
             pltpu.make_async_copy(hi_ref.at[rows], hi_hbm.at[rows], sem.at[0, step]),
             pltpu.make_async_copy(lo_ref.at[rows], lo_hbm.at[rows], sem.at[1, step]),
         )
 
-    def one_step(step, carry):
-        rows = pl.ds(pl.multiple_of(step * STEP, STEP), STEP)
-        mine = rows_ref[rows, :]
+    steps = PTS // STEP
+    for step in range(steps + 1):
+        rows, before = pl.ds(step * STEP, STEP), pl.ds((step - 1) * STEP, STEP)
+        if step > 0:
+            for copy in copies(step - 1):
+                copy.start()
+        total = jnp.zeros((STEP, 2 * BLK), F32)
         for c in range(PTS // CHUNK):
             lanes = pl.ds(c * CHUNK, CHUNK)
-            power = jnp.dot(mine, cols_ref[:, lanes], preferred_element_type=F32)
-            hi, lo = split2(jnp.exp2(jnp.minimum(power, 0.0)))
-            hi_ref[rows, lanes] = hi
-            lo_ref[rows, lanes] = lo
-        for copy in copies(step):
-            copy.start()
-        total = jnp.dot(hi_ref[rows, :], vec_ref[...], preferred_element_type=F32)
-        total += jnp.dot(lo_ref[rows, :], vec_ref[...], preferred_element_type=F32)
-        both = total[:, :BLK] + total[:, BLK:]
-        for h in range(STEP // BLK):
-            part_ref[step * (STEP // BLK) + h] = both[h * BLK : (h + 1) * BLK].T[:VEC]
-        return carry
-
-    lax.fori_loop(0, PTS // STEP, one_step, 0)
-    for step in range(PTS // STEP):
+            if step > 0:
+                vec = vec_ref[lanes, :]
+                total += jnp.dot(hi_ref[before, lanes], vec, preferred_element_type=F32)
+                total += jnp.dot(lo_ref[before, lanes], vec, preferred_element_type=F32)
+            if step < steps:
+                power = jnp.dot(rows_ref[rows, :], cols_ref[:, lanes], preferred_element_type=F32)
+                hi, lo = split2(jnp.exp2(jnp.minimum(power, 0.0)))
+                hi_ref[rows, lanes] = hi
+                lo_ref[rows, lanes] = lo
+        if step > 0:
+            both = total[:, :BLK] + total[:, BLK:]
+            for h in range(STEP // BLK):
+                part_ref[(step - 1) * (STEP // BLK) + h] = both[h * BLK : (h + 1) * BLK].T[:VEC]
+    for step in range(steps):
         for copy in copies(step):
             copy.wait()
 
@@ -265,34 +270,53 @@
     return work[:, RITZ:]
 
 
-def apply_kernel(
-    gram_ref,
-    more_ref,
-    hi_hbm,
-    lo_hbm,
-    vec_ref,
-    pts_ref,
-    held_ref,
-    place_ref,
-    part_ref,
-    own_ref,
-    both_ref,
-    hi_ref,
-    lo_ref,
-    sum_ref,
-    sem,
-):
+def apply_kernel(hi_hbm, lo_hbm, vec_ref, pts_ref, out_ref, rows_ref, hi_ref, lo_ref, sem):
     copies = []
-    for step in range(PTS // STEP):
-        rows = pl.ds(step * STEP, STEP)
+    for step in range(PTS // READ):
+        lanes = pl.ds(step * READ, READ)
         copies.append(
             (
-                pltpu.make_async_copy(hi_hbm.at[rows], hi_ref.at[rows], sem.at[0, step]),
-                pltpu.make_async_copy(lo_hbm.at[rows], lo_ref.at[rows], sem.at[1, step]),
+                pltpu.make_async_copy(hi_hbm.at[:, lanes], hi_ref.at[:, lanes], sem.at[0, step]),
+                pltpu.make_async_copy(lo_hbm.at[:, lanes], lo_ref.at[:, lanes], sem.at[1, step]),
             )
         )
         for copy in copies[-1]:
             copy.start()
+    for b in range(NB):
+        lanes = pl.ds(b * BLK, BLK)
+        first = vec_ref[b, :RHS, :]
+        hi, lo = split2(
+            jnp.concatenate([first, jnp.zeros_like(first), pts_ref[b, FEAT:, :], vec_ref[b, RHS:, :]], axis=0)
+        )
+        rows_ref[pl.ds(0, HALF), lanes] = hi
+        rows_ref[pl.ds(HALF, HALF), lanes] = lo
+    for step in range(PTS // READ):
+        lanes = pl.ds(step * READ, READ)
+        for copy in copies[step]:
+            copy.wait()
+        both = jnp.dot(rows_ref[...], hi_ref[:, lanes], preferred_element_type=F32)
+        more = jnp.dot(rows_ref[pl.ds(0, HALF), :], lo_ref[:, lanes], preferred_element_type=F32)
+        out_ref[:, lanes] = both[:HALF] + both[HALF:] + more
+
+
+def apply_tile(hi, lo, vec, pts):
+    return pl.pallas_call(
+        apply_kernel,
+        in_specs=[hbm(), hbm(), vmem(), vmem()],
+        out_shape=shape(HALF, PTS),
+        scratch_shapes=[
+            pltpu.VMEM((2 * HALF, PTS), BF16),
+            pltpu.VMEM((PTS, PTS), BF16),
+            pltpu.VMEM((PTS, PTS), BF16),
+            pltpu.SemaphoreType.DMA((2, PTS // READ)),
+        ],
+        compiler_params=limit(32),
+        cost_estimate=pl.CostEstimate(flops=8 * HALF * PTS * PTS, bytes_accessed=4 * PTS * PTS, transcendentals=0),
+        name="apply_tile",
+    )(in_hbm(hi), in_hbm(lo), vec, pts)
+
+
+def solve_kernel(gram_ref, more_ref, image_ref, vec_ref, pts_ref, held_ref, place_ref, part_ref, own_ref):
     gram = gram_ref[...] + more_ref[...]
     projected = gram[:RHS, :RITZ]
     first = gram[:RHS, RITZ:]
@@ -307,26 +331,12 @@
     turns = lax.dot_general(against, solve, NT, precision=HIGH, preferred_element_type=F32)
     zero = jnp.zeros_like(turns)
     coef = jnp.concatenate([turns, amounts], axis=1)
-    for b in range(NB):
-        basis = jnp.concatenate([pts_ref[b, FEAT:, :], vec_ref[b, RHS:, :]], axis=0)
-        direction = vec_ref[b, :RHS, :] - jnp.dot(coef, basis, precision=HIGH, preferred_element_type=F32)
-        hi = direction.astype(BF16).astype(F32)
-        both_ref[:, pl.ds(b * BLK, BLK)] = jnp.concatenate([hi, direction - hi], axis=0).astype(BF16)
-    for step in range(PTS // STEP):
-        rows = pl.ds(step * STEP, STEP)
-        both = both_ref[:, rows]
-        for copy in copies[step]:
-            copy.wait()
-        total = jnp.dot(both, hi_ref[rows, :], preferred_element_type=F32)
-        total += jnp.dot(both, lo_ref[rows, :], preferred_element_type=F32)
-        if step == 0:
-            sum_ref[...] = total
-        else:
-            sum_ref[...] += total
+    value = image_ref[pl.ds(0, RHS), :] - jnp.dot(
+        coef, image_ref[pl.ds(2 * RHS, 2 * RITZ), :], precision=HIGH, preferred_element_type=F32
+    )
     for at in range(NB):
-        lanes = pl.ds(at * BLK, BLK)
         half = (at // (NB // 2) + place_ref[1]) % 2
-        part_ref[half * (NB // 2) + at % (NB // 2)] = sum_ref[pl.ds(0, RHS), lanes] + sum_ref[pl.ds(RHS, RHS), lanes]
+        part_ref[half * (NB // 2) + at % (NB // 2)] = value[:, at * BLK : (at + 1) * BLK]
     mine = place_ref[0]
     basis = jnp.concatenate([pts_ref[mine, FEAT:, :], vec_ref[mine, RHS:, :]], axis=0)
     wanted = jnp.concatenate(
@@ -337,21 +347,14 @@
     own_ref[...] = base - jnp.dot(wanted, basis, precision=HIGH, preferred_element_type=F32)
 
 
-def apply_tile(gram, more, hi, lo, vec, pts, held, place):
-    return pl.pallas_call(
-        apply_kernel,
-        in_specs=[vmem(), vmem(), hbm(), hbm(), vmem(), vmem(), vmem(), smem()],
+def solve(gram, more, image, vec, pts, held, place):
+    return pl.pallas_call(
+        solve_kernel,
+        in_specs=[vmem()] * 6 + [smem()],
         out_shape=[shape(NB, RHS, BLK), shape(3 * RHS, BLK)],
-        scratch_shapes=[
-            pltpu.VMEM((2 * RHS, PTS), BF16),
-            pltpu.VMEM((PTS, PTS), BF16),
-            pltpu.VMEM((PTS, PTS), BF16),
-            pltpu.VMEM((2 * RHS, PTS), F32),
-            pltpu.SemaphoreType.DMA((2, PTS // STEP)),
-        ],
-        compiler_params=limit(32),
-        name="apply_tile",
-    )(gram, more, in_hbm(hi), in_hbm(lo), vec, pts, held, place)
+        compiler_params=limit(12),
+        name="solve",
+    )(gram, more, image, vec, pts, held, place)
 
 
 def stats_kernel(got_ref, own_ref, gain_ref, nugget_ref, applied_ref, out_ref):
@@ -413,16 +416,17 @@
 
 def local(points, inv_scales, amplitude, noise_var, targets, initial, ritz_basis):
     near, pts, held = spread(points, inv_scales[None, :], initial, ritz_basis, targets)
+    pts = exchange(pts, XY)
+    near, pts = lax.optimization_barrier((near, pts))
     near = exchange(near, Z)
-    near, pts = lax.optimization_barrier((near, pts))
     far = other_core(near)
-    pts = exchange(pts, XY)
     hi, lo, part = make_tile(near, far, pts)
 
     vec = exchange(at_owner(exchange(part, XY), held, amplitude, noise_var), XY)
     gram = jnp.sum(exchange(make_gram(vec, pts), Z), axis=0)
+    image = apply_tile(hi, lo, vec, pts)
     place = jnp.stack([lax.axis_index(XY), lax.axis_index(CORE)]).astype(jnp.int32)
-    part, own = apply_tile(gram, other_core(gram), hi, lo, vec, pts, held, place)
+    part, own = solve(gram, other_core(gram), image, vec, pts, held, place)
     applied, stats = make_stats(exchange(part, CZ), own, amplitude, noise_var)
     return tuple(finish(exchange(stats, EVERY), own, applied))
 

time: 142 us -> 144 us (1.014)
  blocking collectives: 63.1 us -> 80.8 us
  starting transfers between devices: 23.2 us -> 14.8 us
  waiting for transfers between devices: 25.2 us -> 19.3 us
  Pallas kernels: 27.7 us -> 25.9 us
    all_to_all x4 -> x5, blocking collectives: 63.1 us -> 80.8 us  [exchange(): return lax.all_to_all(pieces, axis, split_axis=0, concat_axis=0, tiled=True)]
    all_to_all x3 -> x2, starting transfers between devices: 15.3 us -> 6.99 us  [exchange(): return lax.all_to_all(pieces, axis, split_axis=0, concat_axis=0, tiled=True)]
    all_to_all x3 -> x2, waiting for transfers between devices: 23.1 us -> 18 us  [exchange(): return lax.all_to_all(pieces, axis, split_axis=0, concat_axis=0, tiled=True)]
    pallas_call x1, Pallas kernels: 12.4 us -> 9.55 us  [make_tile(): pl.pallas_call(tile_kernel, in_specs=[vmem(), vmem(), vmem()], out_specs=...]
    pallas_call x1 -> x2, Pallas kernels: 10.4 us -> 12.2 us  [the longest x1 7.12 us: apply_tile(): pl.pallas_call(apply_kernel, in_specs=[hbm(), hbm(), vmem(), vmem()], out...]
  transfers between devices with their start and end apart: 5 -> 4, of which waited for: 5 -> 3; matrix products, arithmetic and copies ran while one was open for 0% -> 0% of each run, Pallas kernels for 0% -> 5%
where the time goes in v4:
time: 144 us; the launch traced here: 143 us
  blocking collectives  80.8 us (56%)
  Pallas kernels  25.9 us (18%)
  waiting for transfers between devices  19.3 us (13%)
  starting transfers between devices  14.8 us (10%)
  between operations  1.99 us (1%)
    all_to_all x5, blocking collectives, exchange(): return lax.all_to_all(pieces, axis, split_axis=0, concat_axis=0, tiled=True)  80.8 us
    all_to_all x2, waiting for transfers between devices, exchange(): return lax.all_to_all(pieces, axis, split_axis=0, concat_axis=0, tiled=True)  18 us
    pallas_call x1, Pallas kernels, make_tile(): pl.pallas_call(tile_kernel, in_specs=[vmem(), vmem(), vmem()], out_specs=...  9.55 us
    ppermute x2, starting transfers between devices, other_core(): return lax.ppermute(array, CORE, [(0, 1), (1, 0)])  7.84 us
    pallas_call x1, Pallas kernels, apply_tile(): pl.pallas_call(apply_kernel, in_specs=[hbm(), hbm(), vmem(), vmem()], out...  7.12 us
    all_to_all x2, starting transfers between devices, exchange(): return lax.all_to_all(pieces, axis, split_axis=0, concat_axis=0, tiled=True)  6.99 us
    pallas_call x1, Pallas kernels, solve(): pl.pallas_call(solve_kernel, in_specs=[vmem()] * 6 + [smem()], out_shape=...  5.13 us
  transfers between devices with their start and end apart: 4, of which 3 were waited for; matrix products, arithmetic and copies ran while one was open for 0% of the time, Pallas kernels for 5%

profile of v4, /device:TPU:1, one launch (start us, length us, event | category | flops | bytes accessed | tf_op | source)
XLA Modules:
  0.0 143.0 jit_solution(6236708394011228111)
XLA Ops:
  0.6 1.0 spread.1
  1.7 19.1 %all_to_all.41.out_ref.pts_ref = f32[16,80,128]{2,1,0:T(8,128)S(1)} all-to-all(f32[16,80,128]{2,1,0:T(8,128)S(1)} %get-tuple-element.15), channel_id=1, replica_groups=mesh['row_0'=4,'row_1'=8,'col_0'=4,'col_1'=2] {'col_0','row_0'}, dimensions={0} | all-to-all | bytes 1310720 | tf_op jit(solution)/shard_map/all_to_all | solution.py:410
  20.7 19.3 %all_to_all.42.near_ref = f32[8,88,128]{2,1,0:T(8,128)S(1)} all-to-all(f32[8,88,128]{2,1,0:T(8,128)S(1)} %get-tuple-element.16), channel_id=1, replica_groups=mesh['row_0'=4,'row_1'=8,'col_0'=4,'col_1'=2] {'row_1'}, dimensions={0} | all-to-all | bytes 720896 | tf_op jit(solution)/shard_map/all_to_all | solution.py:410
  40.1 3.6 %collective-permute-start = (f32[8,88,128]{2,1,0:T(8,128)S(1)}, f32[8,88,128]{2,1,0:T(8,128)S(1)}, u32[]{:S(2)}, u32[]{:S(2)}) collective-permute-start(f32[8,88,128]{2,1,0:T(8,128)S(1)} %all_to_all.42.near_ref), channel_id=1, source_target_pairs={{0,1},{1,0},{2,3},{3,2},{4,5},{5,4},{6,7},{7,6},{8,9},{9,8},{10,11... | collective-permute-start | bytes 1081352 | tf_op jit(solution)/shard_map/ppermute | solution.py:414
  43.6 1.3 collective-permute-done.far_ref
  44.9 9.6 %kernel_tile.1 = (bf16[2048,2048]{1,0:T(8,128)(2,1)}, bf16[2048,2048]{1,0:T(8,128)(2,1)}, f32[16,72,128]{2,1,0:T(8,128)}) custom-call(f32[8,88,128]{2,1,0:T(8,128)S(1)} %all_to_all.42.near_ref, f32[8,88,128]{2,1,0:T(8,128)S(1)} %collective-permute-done.far_ref, f32[16,80,128]{2,1,0:T(8,128)S(1)} %all_to_all.41.out_ref.pts_ref), custom_call_target="tpu_custom_call" | custom-call | tf_op jit(solution)/shard_map/kernel_tile/pallas_call | solution.py:178
  54.5 3.6 %all-to-all-start.2 = ((f32[16,72,128]{2,1,0:T(8,128)}), f32[16,72,128]{2,1,0:T(8,128)S(1)}, u32[]{:S(2)}, u32[]{:S(2)}) async-start(f32[16,72,128]{2,1,0:T(8,128)} %get-tuple-element.18), calls=%async_computation.2 | async-start | bytes 1179648 | tf_op jit(solution)/shard_map/all_to_all | solution.py:410
  59.4 9.6 %all-to-all-done.2.got_ref = f32[16,72,128]{2,1,0:T(8,128)S(1)} async-done(((f32[16,72,128]{2,1,0:T(8,128)}), f32[16,72,128]{2,1,0:T(8,128)S(1)}, u32[]{:S(2)}, u32[]{:S(2)}) %all-to-all-start.2) | async-done | bytes 589856 | tf_op jit(solution)/shard_map/all_to_all | solution.py:410
  69.0 0.1 at_owner.1
  69.0 14.0 %all_to_all.43.vec_ref = f32[16,72,128]{2,1,0:T(8,128)S(1)} all-to-all(f32[16,72,128]{2,1,0:T(8,128)S(1)} %at_owner.1), channel_id=1, replica_groups=mesh['row_0'=4,'row_1'=8,'col_0'=4,'col_1'=2] {'col_0','row_0'}, dimensions={0} | all-to-all | bytes 1179648 | tf_op jit(solution)/shard_map/all_to_all | solution.py:410
  83.0 2.1 %gram.1 = f32[8,41,128]{2,1,0:T(8,128)} custom-call(f32[16,72,128]{2,1,0:T(8,128)S(1)} %all_to_all.43.vec_ref, f32[16,80,128]{2,1,0:T(8,128)S(1)} %all_to_all.41.out_ref.pts_ref), custom_call_target="tpu_custom_call" | custom-call | tf_op jit(solution)/shard_map/gram/pallas_call | solution.py:246
  85.1 3.4 %all-to-all-start.4 = ((f32[8,41,128]{2,1,0:T(8,128)}), f32[8,41,128]{2,1,0:T(8,128)S(1)}, u32[]{:S(2)}, u32[]{:S(2)}) async-start(f32[8,41,128]{2,1,0:T(8,128)} %gram.1), calls=%async_computation.4 | async-start | bytes 393216 | tf_op jit(solution)/shard_map/all_to_all | solution.py:410
  88.5 0.1 pad_add_fusion.place_ref
  88.6 8.5 %all-to-all-done.4 = f32[8,41,128]{2,1,0:T(8,128)S(1)} async-done(((f32[8,41,128]{2,1,0:T(8,128)}), f32[8,41,128]{2,1,0:T(8,128)S(1)}, u32[]{:S(2)}, u32[]{:S(2)}) %all-to-all-start.4) | async-done | bytes 167968 | tf_op jit(solution)/shard_map/all_to_all | solution.py:410
  97.1 4.3 %collective-permute-start.1 = (f32[41,128]{1,0:T(8,128)S(1)}, f32[41,128]{1,0:T(8,128)S(1)}, u32[]{:S(2)}, u32[]{:S(2)}) collective-permute-start(f32[41,128]{1,0:T(8,128)S(1)} %reduce_sum.9.gram_ref), channel_id=1, source_target_pairs={{0,1},{1,0},{2,3},{3,2},{4,5},{5,4},{6,7},{7,6},{8,9},{9,8},{10,11... | collective-permute-start | bytes 62984 | tf_op jit(solution)/shard_map/ppermute | solution.py:414
  101.4 7.1 %apply_tile.1.image_ref = f32[144,2048]{1,0:T(8,128)S(1)} custom-call(bf16[2048,2048]{1,0:T(8,128)(2,1)} %get-tuple-element.20.hi_hbm, bf16[2048,2048]{1,0:T(8,128)(2,1)} %get-tuple-element.21.lo_hbm, f32[16,72,128]{2,1,0:T(8,128)S(1)} %all_to_all.43.vec_ref, f32[16,80,128]{2,1,0:T(8,128)S(1)} %all_to_all.41.out_ref.pts_ref), custom_call_target="tpu_custom_call" | custom-call | flops 4831838208 | bytes 16777216 | tf_op jit(solution)/shard_map/apply_tile/pallas_call | solution.py:303
  108.5 0.0 collective-permute-done.1.more_ref
  108.5 5.1 %solve.1 = (f32[16,8,128]{2,1,0:T(8,128)S(1)}, f32[24,128]{1,0:T(8,128)S(1)}) custom-call(f32[41,128]{1,0:T(8,128)S(1)} %reduce_sum.9.gram_ref, f32[41,128]{1,0:T(8,128)S(1)} %collective-permute-done.1.more_ref, f32[144,2048]{1,0:T(8,128)S(1)} %apply_tile.1.image_ref, f32[16,72,128]{2,1,0:T(8,128)S(1)} %all_to_all.43.vec_ref, ...), custom_call_target="tpu_custom_call" | custom-call | tf_op jit(solution)/shard_map/solve/pallas_call | solution.py:351
  113.6 9.6 %all_to_all.44.got_ref = f32[16,8,128]{2,1,0:T(8,128)S(1)} all-to-all(f32[16,8,128]{2,1,0:T(8,128)S(1)} %get-tuple-element.22), channel_id=1, replica_groups=mesh['row_0'=4,'row_1'=8,'col_0'=4,'col_1'=2] {'col_1','row_1'}, dimensions={0} | all-to-all | bytes 131072 | tf_op jit(solution)/shard_map/all_to_all | solution.py:410
  123.3 0.2 stats.1
  123.5 18.8 %all_to_all.45 = f32[256,1,16]{2,1,0:T(1,128)S(1)} all-to-all(f32[256,1,16]{2,1,0:T(1,128)S(1)} %bitcast.8), channel_id=1, replica_groups=mesh['row_0'=4,'row_1'=8,'col_0'=4,'col_1'=2] {'col_0','col_1','row_0','..., dimensions={0} | all-to-all | bytes 32768 | tf_op jit(solution)/shard_map/all_to_all | solution.py:410
  142.3 0.7 finish.1
  (1 shorter events, 0.0 us)
Async XLA Ops:
  40.1 4.9 %collective-permute-start = (f32[8,88,128]{2,1,0:T(8,128)S(1)}, f32[8,88,128]{2,1,0:T(8,128)S(1)}, u32[]{:S(2)}, u32[]{:S(2)}) collective-permute-start(f32[8,88,128]{2,1,0:T(8,128)S(1)} %all_to_all.42.near_ref), channel_id=1, source_target_pairs={{0,1},{1,0},{2,3},{3,2},{4,5},{5,4},{6,7},{7,6},{8,9},{9,8},{10,11... | collective-permute-start | bytes 1081352 | tf_op jit(solution)/shard_map/ppermute | solution.py:414
  54.5 14.5 %all-to-all-start.2 = ((f32[16,72,128]{2,1,0:T(8,128)}), f32[16,72,128]{2,1,0:T(8,128)S(1)}, u32[]{:S(2)}, u32[]{:S(2)}) async-start(f32[16,72,128]{2,1,0:T(8,128)} %get-tuple-element.18), calls=%async_computation.2 | async-start | bytes 1179648 | tf_op jit(solution)/shard_map/all_to_all | solution.py:410
  85.1 11.9 %all-to-all-start.4 = ((f32[8,41,128]{2,1,0:T(8,128)}), f32[8,41,128]{2,1,0:T(8,128)S(1)}, u32[]{:S(2)}, u32[]{:S(2)}) async-start(f32[8,41,128]{2,1,0:T(8,128)} %gram.1), calls=%async_computation.4 | async-start | bytes 393216 | tf_op jit(solution)/shard_map/all_to_all | solution.py:410
  97.1 11.4 %collective-permute-start.1 = (f32[41,128]{1,0:T(8,128)S(1)}, f32[41,128]{1,0:T(8,128)S(1)}, u32[]{:S(2)}, u32[]{:S(2)}) collective-permute-start(f32[41,128]{1,0:T(8,128)S(1)} %reduce_sum.9.gram_ref), channel_id=1, source_target_pairs={{0,1},{1,0},{2,3},{3,2},{4,5},{5,4},{6,7},{7,6},{8,9},{9,8},{10,11... | collective-permute-start | bytes 62984 | tf_op jit(solution)/shard_map/ppermute | solution.py:414

commit v5 on v4

--- a/solution.py
+++ b/solution.py
@@ -416,15 +416,18 @@
 
 def local(points, inv_scales, amplitude, noise_var, targets, initial, ritz_basis):
     near, pts, held = spread(points, inv_scales[None, :], initial, ritz_basis, targets)
+    near = exchange(near, Z)
+    near, pts = lax.optimization_barrier((near, pts))
+    far = other_core(near)
     pts = exchange(pts, XY)
-    near, pts = lax.optimization_barrier((near, pts))
-    near = exchange(near, Z)
-    far = other_core(near)
     hi, lo, part = make_tile(near, far, pts)
 
     vec = exchange(at_owner(exchange(part, XY), held, amplitude, noise_var), XY)
-    gram = jnp.sum(exchange(make_gram(vec, pts), Z), axis=0)
+    gram = make_gram(vec, pts)
+    vec, gram = lax.optimization_barrier((vec, gram))
     image = apply_tile(hi, lo, vec, pts)
+    image, gram = lax.optimization_barrier((image, exchange(gram, Z)))
+    gram = jnp.sum(gram, axis=0)
     place = jnp.stack([lax.axis_index(XY), lax.axis_index(CORE)]).astype(jnp.int32)
     part, own = solve(gram, other_core(gram), image, vec, pts, held, place)
     applied, stats = make_stats(exchange(part, CZ), own, amplitude, noise_var)

time: 144 us -> 137 us (0.951)
  blocking collectives: 80.8 us -> 52.5 us
  starting transfers between devices: 14.8 us -> 26.8 us
  waiting for transfers between devices: 19.3 us -> 27.3 us
  Pallas kernels: 25.9 us -> 27.5 us
    all_to_all x5 -> x3, blocking collectives: 80.8 us -> 52.5 us  [exchange(): return lax.all_to_all(pieces, axis, split_axis=0, concat_axis=0, tiled=True)]
    all_to_all x2 -> x4, starting transfers between devices: 6.99 us -> 18.8 us  [exchange(): return lax.all_to_all(pieces, axis, split_axis=0, concat_axis=0, tiled=True)]
    all_to_all x2 -> x4, waiting for transfers between devices: 18 us -> 25.2 us  [exchange(): return lax.all_to_all(pieces, axis, split_axis=0, concat_axis=0, tiled=True)]
  transfers between devices with their start and end apart: 4 -> 6, of which waited for: 3 -> 6; matrix products, arithmetic and copies ran while one was open for 0% -> 0% of each run, Pallas kernels for 5% -> 5%
where the time goes in v5:
time: 137 us; the launch traced here: 136 us
  blocking collectives  52.5 us (38%)
  Pallas kernels  27.5 us (20%)
  waiting for transfers between devices  27.3 us (20%)
  starting transfers between devices  26.8 us (20%)
  between operations  1.99 us (1%)
    all_to_all x3, blocking collectives, exchange(): return lax.all_to_all(pieces, axis, split_axis=0, concat_axis=0, tiled=True)  52.5 us
    all_to_all x4, waiting for transfers between devices, exchange(): return lax.all_to_all(pieces, axis, split_axis=0, concat_axis=0, tiled=True)  25.2 us
    all_to_all x4, starting transfers between devices, exchange(): return lax.all_to_all(pieces, axis, split_axis=0, concat_axis=0, tiled=True)  18.8 us
    pallas_call x1, Pallas kernels, make_tile(): pl.pallas_call(tile_kernel, in_specs=[vmem(), vmem(), vmem()], out_specs=...  9.52 us
    ppermute x2, starting transfers between devices, other_core(): return lax.ppermute(array, CORE, [(0, 1), (1, 0)])  7.99 us
    pallas_call x1, Pallas kernels, apply_tile(): pl.pallas_call(apply_kernel, in_specs=[hbm(), hbm(), vmem(), vmem()], out...  7.12 us
    pallas_call x1, Pallas kernels, solve(): pl.pallas_call(solve_kernel, in_specs=[vmem()] * 6 + [smem()], out_shape=...  5.13 us
  transfers between devices with their start and end apart: 6, of which 6 were waited for; matrix products, arithmetic and copies ran while one was open for 0% of the time, Pallas kernels for 5%

profile of v5, /device:TPU:1, one launch (start us, length us, event | category | flops | bytes accessed | tf_op | source)
XLA Modules:
  0.0 136.2 jit_solution(4427940622394075407)
XLA Ops:
  0.6 1.9 %spread.1 = (f32[8,88,128]{2,1,0:T(8,128)S(1)}, f32[16,80,128]{2,1,0:T(8,128)}, f32[80,128]{1,0:T(8,128)S(1)}) custom-call(f32[16,128]{1,0:T(8,128)} %points_hbm.1, f32[1,16]{1,0:T(1,128)} %bitcast.9, f32[8,128]{1,0:T(8,128)} %initial_hbm.1, f32[64,128]{1,0:T(8,128)} %ritz_hbm.1, f32[8,128]{1,0:T(8,128)} %targets_hbm.1), custom_call_target="tpu_custom_call" | custom-call | tf_op jit(solution)/shard_map/spread/pallas_call | solution.py:114
  2.5 21.8 %all_to_all.41.near_ref = f32[8,88,128]{2,1,0:T(8,128)S(1)} all-to-all(f32[8,88,128]{2,1,0:T(8,128)S(1)} %get-tuple-element.18), channel_id=1, replica_groups=mesh['row_0'=4,'row_1'=8,'col_0'=4,'col_1'=2] {'row_1'}, dimensions={0} | all-to-all | bytes 720896 | tf_op jit(solution)/shard_map/all_to_all | solution.py:410
  24.3 6.8 %all-to-all-start.1 = ((f32[16,80,128]{2,1,0:T(8,128)}), f32[16,80,128]{2,1,0:T(8,128)S(1)}, u32[]{:S(2)}, u32[]{:S(2)}) async-start(f32[16,80,128]{2,1,0:T(8,128)} %get-tuple-element.21), calls=%async_computation.1 | async-start | bytes 1310720 | tf_op jit(solution)/shard_map/all_to_all | solution.py:410
  31.1 2.3 %collective-permute-start = (f32[8,88,128]{2,1,0:T(8,128)S(1)}, f32[8,88,128]{2,1,0:T(8,128)S(1)}, u32[]{:S(2)}, u32[]{:S(2)}) collective-permute-start(f32[8,88,128]{2,1,0:T(8,128)S(1)} %all_to_all.41.near_ref), channel_id=1, source_target_pairs={{0,1},{1,0},{2,3},{3,2},{4,5},{5,4},{6,7},{7,6},{8,9},{9,8},{10,11... | collective-permute-start | bytes 1081352 | tf_op jit(solution)/shard_map/ppermute | solution.py:414
  33.4 1.3 collective-permute-done.far_ref
  34.7 6.4 %all-to-all-done.1.out_ref.pts_ref = f32[16,80,128]{2,1,0:T(8,128)S(1)} async-done(((f32[16,80,128]{2,1,0:T(8,128)}), f32[16,80,128]{2,1,0:T(8,128)S(1)}, u32[]{:S(2)}, u32[]{:S(2)}) %all-to-all-start.1) | async-done | bytes 655392 | tf_op jit(solution)/shard_map/all_to_all | solution.py:410
  41.1 9.5 %kernel_tile.1 = (bf16[2048,2048]{1,0:T(8,128)(2,1)}, bf16[2048,2048]{1,0:T(8,128)(2,1)}, f32[16,72,128]{2,1,0:T(8,128)}) custom-call(f32[8,88,128]{2,1,0:T(8,128)S(1)} %all_to_all.41.near_ref, f32[8,88,128]{2,1,0:T(8,128)S(1)} %collective-permute-done.far_ref, f32[16,80,128]{2,1,0:T(8,128)S(1)} %all-to-all-done.1.out_ref.pts_ref), custom_call_target="tpu_custom_call" | custom-call | tf_op jit(solution)/shard_map/kernel_tile/pallas_call | solution.py:178
  50.6 4.3 %all-to-all-start.2 = ((f32[16,72,128]{2,1,0:T(8,128)}), f32[16,72,128]{2,1,0:T(8,128)S(1)}, u32[]{:S(2)}, u32[]{:S(2)}) async-start(f32[16,72,128]{2,1,0:T(8,128)} %get-tuple-element.24), calls=%async_computation.2 | async-start | bytes 1179648 | tf_op jit(solution)/shard_map/all_to_all | solution.py:410
  56.2 8.1 %all-to-all-done.2.got_ref = f32[16,72,128]{2,1,0:T(8,128)S(1)} async-done(((f32[16,72,128]{2,1,0:T(8,128)}), f32[16,72,128]{2,1,0:T(8,128)S(1)}, u32[]{:S(2)}, u32[]{:S(2)}) %all-to-all-start.2) | async-done | bytes 589856 | tf_op jit(solution)/shard_map/all_to_all | solution.py:410
  64.2 0.9 at_owner.1
  65.1 3.6 %all-to-all-start.3 = ((f32[16,72,128]{2,1,0:T(8,128)}), f32[16,72,128]{2,1,0:T(8,128)S(1)}, u32[]{:S(2)}, u32[]{:S(2)}) async-start(f32[16,72,128]{2,1,0:T(8,128)} %at_owner.1), calls=%async_computation.3 | async-start | bytes 1179648 | tf_op jit(solution)/shard_map/all_to_all | solution.py:410
  68.7 9.3 %all-to-all-done.3.vec_ref = f32[16,72,128]{2,1,0:T(8,128)S(1)} async-done(((f32[16,72,128]{2,1,0:T(8,128)}), f32[16,72,128]{2,1,0:T(8,128)S(1)}, u32[]{:S(2)}, u32[]{:S(2)}) %all-to-all-start.3) | async-done | bytes 589856 | tf_op jit(solution)/shard_map/all_to_all | solution.py:410
  78.0 2.1 %gram.1 = f32[8,41,128]{2,1,0:T(8,128)} custom-call(f32[16,72,128]{2,1,0:T(8,128)S(1)} %all-to-all-done.3.vec_ref, f32[16,80,128]{2,1,0:T(8,128)S(1)} %all-to-all-done.1.out_ref.pts_ref), custom_call_target="tpu_custom_call" | custom-call | tf_op jit(solution)/shard_map/gram/pallas_call | solution.py:246
  80.1 4.2 %all-to-all-start.4 = ((f32[8,41,128]{2,1,0:T(8,128)}), f32[8,41,128]{2,1,0:T(8,128)S(1)}, u32[]{:S(2)}, u32[]{:S(2)}) async-start(f32[8,41,128]{2,1,0:T(8,128)} %gram.1), calls=%async_computation.4 | async-start | bytes 393216 | tf_op jit(solution)/shard_map/all_to_all | solution.py:410
  84.3 7.1 %apply_tile.1.image_ref = f32[144,2048]{1,0:T(8,128)S(1)} custom-call(bf16[2048,2048]{1,0:T(8,128)(2,1)} %get-tuple-element.22.hi_hbm, bf16[2048,2048]{1,0:T(8,128)(2,1)} %get-tuple-element.23.lo_hbm, f32[16,72,128]{2,1,0:T(8,128)S(1)} %all-to-all-done.3.vec_ref, f32[16,80,128]{2,1,0:T(8,128)S(1)} %all-to-all-done.1.out_ref.pts_ref), custom_call_target="tpu_custom_call" | custom-call | flops 4831838208 | bytes 16777216 | tf_op jit(solution)/shard_map/apply_tile/pallas_call | solution.py:303
  91.4 1.5 %all-to-all-done.4 = f32[8,41,128]{2,1,0:T(8,128)S(1)} async-done(((f32[8,41,128]{2,1,0:T(8,128)}), f32[8,41,128]{2,1,0:T(8,128)S(1)}, u32[]{:S(2)}, u32[]{:S(2)}) %all-to-all-start.4) | async-done | bytes 167968 | tf_op jit(solution)/shard_map/all_to_all | solution.py:410
  92.9 5.7 %collective-permute-start.1 = (f32[41,128]{1,0:T(8,128)S(1)}, f32[41,128]{1,0:T(8,128)S(1)}, u32[]{:S(2)}, u32[]{:S(2)}) collective-permute-start(f32[41,128]{1,0:T(8,128)S(1)} %reduce_sum.9.gram_ref), channel_id=1, source_target_pairs={{0,1},{1,0},{2,3},{3,2},{4,5},{5,4},{6,7},{7,6},{8,9},{9,8},{10,11... | collective-permute-start | bytes 62984 | tf_op jit(solution)/shard_map/ppermute | solution.py:414
  98.6 0.1 pad_add_fusion.place_ref
  98.7 0.8 collective-permute-done.1.more_ref
  99.5 5.1 %solve.1 = (f32[16,8,128]{2,1,0:T(8,128)S(1)}, f32[24,128]{1,0:T(8,128)S(1)}) custom-call(f32[41,128]{1,0:T(8,128)S(1)} %reduce_sum.9.gram_ref, f32[41,128]{1,0:T(8,128)S(1)} %collective-permute-done.1.more_ref, f32[144,2048]{1,0:T(8,128)S(1)} %apply_tile.1.image_ref, f32[16,72,128]{2,1,0:T(8,128)S(1)} %all-to-all-done.3.vec_ref, ...), custom_call_target="tpu_custom_call" | custom-call | tf_op jit(solution)/shard_map/solve/pallas_call | solution.py:351
  104.6 11.9 %all_to_all.42.got_ref = f32[16,8,128]{2,1,0:T(8,128)S(1)} all-to-all(f32[16,8,128]{2,1,0:T(8,128)S(1)} %get-tuple-element.30), channel_id=1, replica_groups=mesh['row_0'=4,'row_1'=8,'col_0'=4,'col_1'=2] {'col_1','row_1'}, dimensions={0} | all-to-all | bytes 131072 | tf_op jit(solution)/shard_map/all_to_all | solution.py:410
  116.5 0.2 stats.1
  116.7 18.8 %all_to_all.43 = f32[256,1,16]{2,1,0:T(1,128)S(1)} all-to-all(f32[256,1,16]{2,1,0:T(1,128)S(1)} %bitcast.8), channel_id=1, replica_groups=mesh['row_0'=4,'row_1'=8,'col_0'=4,'col_1'=2] {'col_0','col_1','row_0','..., dimensions={0} | all-to-all | bytes 32768 | tf_op jit(solution)/shard_map/all_to_all | solution.py:410
  135.5 0.7 finish.1
  (1 shorter events, 0.0 us)
Async XLA Ops:
  24.3 16.7 %all-to-all-start.1 = ((f32[16,80,128]{2,1,0:T(8,128)}), f32[16,80,128]{2,1,0:T(8,128)S(1)}, u32[]{:S(2)}, u32[]{:S(2)}) async-start(f32[16,80,128]{2,1,0:T(8,128)} %get-tuple-element.21), calls=%async_computation.1 | async-start | bytes 1310720 | tf_op jit(solution)/shard_map/all_to_all | solution.py:410
  31.1 3.6 %collective-permute-start = (f32[8,88,128]{2,1,0:T(8,128)S(1)}, f32[8,88,128]{2,1,0:T(8,128)S(1)}, u32[]{:S(2)}, u32[]{:S(2)}) collective-permute-start(f32[8,88,128]{2,1,0:T(8,128)S(1)} %all_to_all.41.near_ref), channel_id=1, source_target_pairs={{0,1},{1,0},{2,3},{3,2},{4,5},{5,4},{6,7},{7,6},{8,9},{9,8},{10,11... | collective-permute-start | bytes 1081352 | tf_op jit(solution)/shard_map/ppermute | solution.py:414
  50.6 13.7 %all-to-all-start.2 = ((f32[16,72,128]{2,1,0:T(8,128)}), f32[16,72,128]{2,1,0:T(8,128)S(1)}, u32[]{:S(2)}, u32[]{:S(2)}) async-start(f32[16,72,128]{2,1,0:T(8,128)} %get-tuple-element.24), calls=%async_computation.2 | async-start | bytes 1179648 | tf_op jit(solution)/shard_map/all_to_all | solution.py:410
  65.1 12.9 %all-to-all-start.3 = ((f32[16,72,128]{2,1,0:T(8,128)}), f32[16,72,128]{2,1,0:T(8,128)S(1)}, u32[]{:S(2)}, u32[]{:S(2)}) async-start(f32[16,72,128]{2,1,0:T(8,128)} %at_owner.1), calls=%async_computation.3 | async-start | bytes 1179648 | tf_op jit(solution)/shard_map/all_to_all | solution.py:410
  80.1 12.9 %all-to-all-start.4 = ((f32[8,41,128]{2,1,0:T(8,128)}), f32[8,41,128]{2,1,0:T(8,128)S(1)}, u32[]{:S(2)}, u32[]{:S(2)}) async-start(f32[8,41,128]{2,1,0:T(8,128)} %gram.1), calls=%async_computation.4 | async-start | bytes 393216 | tf_op jit(solution)/shard_map/all_to_all | solution.py:410
  92.9 6.5 %collective-permute-start.1 = (f32[41,128]{1,0:T(8,128)S(1)}, f32[41,128]{1,0:T(8,128)S(1)}, u32[]{:S(2)}, u32[]{:S(2)}) collective-permute-start(f32[41,128]{1,0:T(8,128)S(1)} %reduce_sum.9.gram_ref), channel_id=1, source_target_pairs={{0,1},{1,0},{2,3},{3,2},{4,5},{5,4},{6,7},{7,6},{8,9},{9,8},{10,11... | collective-permute-start | bytes 62984 | tf_op jit(solution)/shard_map/ppermute | solution.py:414

commit v6 on v5

--- a/solution.py
+++ b/solution.py
@@ -8,9 +8,10 @@
 from jax.sharding import Mesh
 from jax.sharding import PartitionSpec as P
 
+
 CORE = "col_1"
 Z = "row_1"
-XY = ("col_0", "row_0")
+XY = ("row_0", "col_0")
 CZ = ("col_1", "row_1")
 EVERY = ("col_0", "col_1", "row_0", "row_1")
 COL_ROW = EVERY
@@ -24,7 +25,7 @@
 PTS = NB * BLK
 STEP = 256
 CHUNK = 256
-READ = 512
+READ = 256
 HALF = 2 * RHS + 2 * RITZ
 PACKED = RHS + RITZ // 2 + 1
 WORLD = 256
@@ -88,7 +89,18 @@
 
 
 def spread_kernel(
-    points_hbm, scale_hbm, initial_hbm, ritz_hbm, targets_hbm, near_ref, pts_ref, held_ref, points_ref, scale_ref, sem
+    points_hbm,
+    scale_hbm,
+    initial_hbm,
+    ritz_hbm,
+    targets_hbm,
+    near_ref,
+    pts_ref,
+    ritz_ref,
+    held_ref,
+    points_ref,
+    scale_ref,
+    sem,
 ):
     copies = [
         pltpu.make_async_copy(points_hbm, points_ref, sem.at[0]),
@@ -105,17 +117,21 @@
     for b in range(NB // 2):
         near_ref[b, pl.ds(0, FEAT), :] = scaled
         near_ref[b, pl.ds(FEAT, VEC), :] = held_ref[pl.ds(RHS, VEC), :]
-    for b in range(NB):
-        pts_ref[b, pl.ds(0, FEAT), :] = scaled
-        pts_ref[b, pl.ds(FEAT, RITZ), :] = held_ref[pl.ds(2 * RHS, RITZ), :]
+    pts_ref[...] = scaled
+    ritz_ref[...] = held_ref[pl.ds(2 * RHS, RITZ), :]
 
 
 def spread(points, scales, initial, ritz, targets):
     return pl.pallas_call(
         spread_kernel,
         in_specs=[hbm()] * 5,
-        out_specs=[vmem()] * 3,
-        out_shape=[shape(NB // 2, FEAT + VEC, BLK), shape(NB, FEAT + RITZ, BLK), shape(RHS + VEC, BLK)],
+        out_specs=[vmem()] * 4,
+        out_shape=[
+            shape(NB // 2, FEAT + VEC, BLK),
+            shape(FEAT, BLK),
+            shape(RITZ, BLK),
+            shape(RHS + VEC, BLK),
+        ],
         scratch_shapes=[
             pltpu.VMEM((FEAT, BLK), F32),
             pltpu.VMEM((1, FEAT), F32),
@@ -138,7 +154,7 @@
         hi, lo = split2(tall)
         vec_ref[lanes, pl.ds(0, BLK)] = hi
         vec_ref[lanes, pl.ds(BLK, BLK)] = lo
-        rows_ref[lanes, :] = features(out_ref[b, :FEAT, :], True).T.astype(BF16)
+        rows_ref[lanes, :] = features(out_ref[b], True).T.astype(BF16)
 
     def copies(step):
         rows = pl.ds(step * STEP, STEP)
@@ -223,11 +239,11 @@
     return lax.broadcasted_iota(jnp.int32, (RITZ, RITZ), 0), lax.broadcasted_iota(jnp.int32, (RITZ, RITZ), 1)
 
 
-def gram_kernel(vec_ref, pts_ref, out_ref, left_ref, right_ref):
+def gram_kernel(vec_ref, ritz_ref, out_ref, left_ref, right_ref):
     for b in range(NB):
         lanes = pl.ds(b * BLK, BLK)
         left_ref[:, lanes] = vec_ref[b]
-        right_ref[pl.ds(0, RITZ), lanes] = pts_ref[b, FEAT:, :]
+        right_ref[pl.ds(0, RITZ), lanes] = ritz_ref[b]
         right_ref[pl.ds(RITZ, RITZ), lanes] = vec_ref[b, RHS:, :]
     gram = lax.dot_general(left_ref[...], right_ref[...], NT, precision=HIGH, preferred_element_type=F32)
     coarse = gram[RHS:, :RITZ]
@@ -242,35 +258,51 @@
         out_ref[b, pl.ds(RHS + RITZ // 2, 1), :] = jnp.concatenate([diagonal, diagonal], axis=1)
 
 
-def make_gram(vec, pts):
+def make_gram(vec, ritz):
     return pl.pallas_call(
         gram_kernel,
         out_shape=shape(NB // 2, PACKED, BLK),
         scratch_shapes=[pltpu.VMEM((VEC, PTS), F32), pltpu.VMEM((2 * RITZ, PTS), F32)],
         compiler_params=limit(12),
         name="gram",
-    )(vec, pts)
+    )(vec, ritz)
 
 
 def inverse(matrix):
+    full = (8, 2 * RITZ)
     i, j = square_iota()
     work = jnp.concatenate([matrix, jnp.where(i == j, 1.0, 0.0)], axis=1)
-    row = lax.broadcasted_iota(jnp.int32, work.shape, 0)
-    for k in range(0, RITZ, 2):
-        col0 = jnp.broadcast_to(work[:, k : k + 1], work.shape)
-        col1 = jnp.broadcast_to(work[:, k + 1 : k + 2], work.shape)
-        a, b = col0[k : k + 1], col1[k : k + 1]
-        c, d = col0[k + 1 : k + 2], col1[k + 1 : k + 2]
-        top, low = work[k : k + 1], work[k + 1 : k + 2]
+    work = [work[b : b + 8] for b in range(0, RITZ, 8)]
+    sub = lax.broadcasted_iota(jnp.int32, full, 0)
+
+    def pair(a, b, c, d, top, low):
         scale = 1.0 / (a * d - b * c)
-        new_top = (d * top - b * low) * scale
-        new_low = (a * low - c * top) * scale
-        work = work - (col0 * new_top + col1 * new_low)
-        work = jnp.where(row == k, new_top, jnp.where(row == k + 1, new_low, work))
-    return work[:, RITZ:]
-
-
-def apply_kernel(hi_hbm, lo_hbm, vec_ref, pts_ref, out_ref, rows_ref, hi_ref, lo_ref, sem):
+        return (d * top - b * low) * scale, (a * low - c * top) * scale
+
+    for k in range(0, RITZ, 4):
+        at, row = k // 8, k % 8
+        cols = [[jnp.broadcast_to(w[:, k + q : k + q + 1], full) for w in work] for q in range(4)]
+        rows = [jnp.broadcast_to(work[at][row + q : row + q + 1], full) for q in range(4)]
+        e = [[jnp.broadcast_to(cols[r][at][row + q : row + q + 1], full) for r in range(4)] for q in range(4)]
+        r0, r1 = pair(e[0][0], e[0][1], e[1][0], e[1][1], rows[0], rows[1])
+        f = [pair(e[0][0], e[0][1], e[1][0], e[1][1], e[0][r], e[1][r]) for r in (2, 3)]
+        rows[2] = rows[2] - e[2][0] * r0 - e[2][1] * r1
+        rows[3] = rows[3] - e[3][0] * r0 - e[3][1] * r1
+        g = [[e[q][r] - e[q][0] * f[r - 2][0] - e[q][1] * f[r - 2][1] for r in (2, 3)] for q in (2, 3)]
+        r2, r3 = pair(g[0][0], g[0][1], g[1][0], g[1][1], rows[2], rows[3])
+        r0 = r0 - f[0][0] * r2 - f[1][0] * r3
+        r1 = r1 - f[0][1] * r2 - f[1][1] * r3
+        final = (r0, r1, r2, r3)
+        work = [
+            w - ((cols[0][b] * r0 + cols[1][b] * r1) + (cols[2][b] * r2 + cols[3][b] * r3))
+            for b, w in enumerate(work)
+        ]
+        for q in range(4):
+            work[at] = jnp.where(sub == row + q, final[q], work[at])
+    return jnp.concatenate(work, axis=0)[:, RITZ:]
+
+
+def apply_kernel(hi_hbm, lo_hbm, vec_ref, ritz_ref, out_ref, split_ref, rows_ref, hi_ref, lo_ref, sem):
     copies = []
     for step in range(PTS // READ):
         lanes = pl.ds(step * READ, READ)
@@ -285,9 +317,7 @@
     for b in range(NB):
         lanes = pl.ds(b * BLK, BLK)
         first = vec_ref[b, :RHS, :]
-        hi, lo = split2(
-            jnp.concatenate([first, jnp.zeros_like(first), pts_ref[b, FEAT:, :], vec_ref[b, RHS:, :]], axis=0)
-        )
+        hi, lo = split2(jnp.concatenate([first, jnp.zeros_like(first), ritz_ref[b], vec_ref[b, RHS:, :]], axis=0))
         rows_ref[pl.ds(0, HALF), lanes] = hi
         rows_ref[pl.ds(HALF, HALF), lanes] = lo
     for step in range(PTS // READ):
@@ -296,14 +326,17 @@
             copy.wait()
         both = jnp.dot(rows_ref[...], hi_ref[:, lanes], preferred_element_type=F32)
         more = jnp.dot(rows_ref[pl.ds(0, HALF), :], lo_ref[:, lanes], preferred_element_type=F32)
-        out_ref[:, lanes] = both[:HALF] + both[HALF:] + more
-
-
-def apply_tile(hi, lo, vec, pts):
+        value = both[:HALF] + both[HALF:] + more
+        out_ref[:, lanes] = value[:RHS]
+        for part, piece in enumerate(split3(value[2 * RHS :])):
+            split_ref[pl.ds(part * 2 * RITZ, 2 * RITZ), lanes] = piece.astype(BF16)
+
+
+def apply_tile(hi, lo, vec, ritz):
     return pl.pallas_call(
         apply_kernel,
         in_specs=[hbm(), hbm(), vmem(), vmem()],
-        out_shape=shape(HALF, PTS),
+        out_shape=[shape(RHS, PTS), jax.ShapeDtypeStruct((6 * RITZ, PTS), BF16)],
         scratch_shapes=[
             pltpu.VMEM((2 * HALF, PTS), BF16),
             pltpu.VMEM((PTS, PTS), BF16),
@@ -313,10 +346,10 @@
         compiler_params=limit(32),
         cost_estimate=pl.CostEstimate(flops=8 * HALF * PTS * PTS, bytes_accessed=4 * PTS * PTS, transcendentals=0),
         name="apply_tile",
-    )(in_hbm(hi), in_hbm(lo), vec, pts)
-
-
-def solve_kernel(gram_ref, more_ref, image_ref, vec_ref, pts_ref, held_ref, place_ref, part_ref, own_ref):
+    )(in_hbm(hi), in_hbm(lo), vec, ritz)
+
+
+def solve_kernel(gram_ref, more_ref, image_ref, split_ref, vec_ref, held_ref, place_ref, part_ref, own_ref):
     gram = gram_ref[...] + more_ref[...]
     projected = gram[:RHS, :RITZ]
     first = gram[:RHS, RITZ:]
@@ -331,14 +364,18 @@
     turns = lax.dot_general(against, solve, NT, precision=HIGH, preferred_element_type=F32)
     zero = jnp.zeros_like(turns)
     coef = jnp.concatenate([turns, amounts], axis=1)
-    value = image_ref[pl.ds(0, RHS), :] - jnp.dot(
-        coef, image_ref[pl.ds(2 * RHS, 2 * RITZ), :], precision=HIGH, preferred_element_type=F32
-    )
+    pieces = split3(coef)
+    value = image_ref[...]
+    for part, rows in ((2, 1), (1, 2), (0, 3)):
+        left = jnp.concatenate(pieces[:rows], axis=0).astype(BF16)
+        more = jnp.dot(left, split_ref[pl.ds(part * 2 * RITZ, 2 * RITZ), :], preferred_element_type=F32)
+        for q in range(rows):
+            value -= more[q * RHS : (q + 1) * RHS]
     for at in range(NB):
-        half = (at // (NB // 2) + place_ref[1]) % 2
+        half = (at // (NB // 2) + place_ref[2]) % 2
         part_ref[half * (NB // 2) + at % (NB // 2)] = value[:, at * BLK : (at + 1) * BLK]
-    mine = place_ref[0]
-    basis = jnp.concatenate([pts_ref[mine, FEAT:, :], vec_ref[mine, RHS:, :]], axis=0)
+    mine = place_ref[1] * 4 + place_ref[0]
+    basis = jnp.concatenate([held_ref[pl.ds(2 * RHS, RITZ), :], vec_ref[mine, RHS:, :]], axis=0)
     wanted = jnp.concatenate(
         [coef, jnp.concatenate([zero, amounts], axis=1), jnp.concatenate([-amounts, zero], axis=1)], axis=0
     )
@@ -347,14 +384,14 @@
     own_ref[...] = base - jnp.dot(wanted, basis, precision=HIGH, preferred_element_type=F32)
 
 
-def solve(gram, more, image, vec, pts, held, place):
+def solve(gram, more, image, split, vec, held, place):
     return pl.pallas_call(
         solve_kernel,
         in_specs=[vmem()] * 6 + [smem()],
         out_shape=[shape(NB, RHS, BLK), shape(3 * RHS, BLK)],
         compiler_params=limit(12),
         name="solve",
-    )(gram, more, image, vec, pts, held, place)
+    )(gram, more, image, split, vec, held, place)
 
 
 def stats_kernel(got_ref, own_ref, gain_ref, nugget_ref, applied_ref, out_ref):
@@ -410,26 +447,41 @@
     return lax.all_to_all(pieces, axis, split_axis=0, concat_axis=0, tiled=True)
 
 
+def all_around(array, axis):
+    size, here = lax.axis_size(axis), lax.axis_index(axis)
+    whole = jnp.zeros((size, *array.shape), array.dtype)
+    for k in range(size):
+        block = array if k == 0 else lax.ppermute(array, axis, [(i, (i + k) % size) for i in range(size)])
+        whole = lax.dynamic_update_index_in_dim(whole, block, (here - k + size) % size, 0)
+    return whole
+
+
 def other_core(array):
     return lax.ppermute(array, CORE, [(0, 1), (1, 0)])
 
 
 def local(points, inv_scales, amplitude, noise_var, targets, initial, ritz_basis):
-    near, pts, held = spread(points, inv_scales[None, :], initial, ritz_basis, targets)
+    near, pts, ritz, held = spread(points, inv_scales[None, :], initial, ritz_basis, targets)
+    place = jnp.stack([lax.axis_index("col_0"), lax.axis_index("row_0"), lax.axis_index(CORE)]).astype(jnp.int32)
     near = exchange(near, Z)
-    near, pts = lax.optimization_barrier((near, pts))
+    pts = all_around(pts, "col_0")
+    pts = all_around(pts, "row_0").reshape(NB, FEAT, BLK)
     far = other_core(near)
-    pts = exchange(pts, XY)
     hi, lo, part = make_tile(near, far, pts)
 
-    vec = exchange(at_owner(exchange(part, XY), held, amplitude, noise_var), XY)
-    gram = make_gram(vec, pts)
+    part, ritz = lax.optimization_barrier((part, ritz))
+    part = exchange(part, XY)
+    ritz = all_around(ritz, "col_0")
+    own = at_owner(part, held, amplitude, noise_var)
+    own, ritz = lax.optimization_barrier((own, ritz))
+    vec = exchange(own, XY)
+    ritz = all_around(ritz, "row_0").reshape(NB, RITZ, BLK)
+    gram = make_gram(vec, ritz)
     vec, gram = lax.optimization_barrier((vec, gram))
-    image = apply_tile(hi, lo, vec, pts)
-    image, gram = lax.optimization_barrier((image, exchange(gram, Z)))
+    image, split = apply_tile(hi, lo, vec, ritz)
+    image, split, gram = lax.optimization_barrier((image, split, exchange(gram, Z)))
     gram = jnp.sum(gram, axis=0)
-    place = jnp.stack([lax.axis_index(XY), lax.axis_index(CORE)]).astype(jnp.int32)
-    part, own = solve(gram, other_core(gram), image, vec, pts, held, place)
+    part, own = solve(gram, other_core(gram), image, split, vec, held, place)
     applied, stats = make_stats(exchange(part, CZ), own, amplitude, noise_var)
     return tuple(finish(exchange(stats, EVERY), own, applied))
 

time: 137 us -> 140 us (1.022)
  blocking collectives: 52.5 us -> 33.2 us
  starting transfers between devices: 26.8 us -> 44.5 us
  Pallas kernels: 27.5 us -> 30.3 us
    all_to_all x3 -> x2, blocking collectives: 52.5 us -> 33.2 us  [exchange(): return lax.all_to_all(pieces, axis, split_axis=0, concat_axis=0, tiled=True)]
    ppermute x0 -> x12, starting transfers between devices: none -> 13.5 us  [all_around(): lax.ppermute(array, axis, [(i, (i + k) % size) for i in range(size)])]
    ppermute x0 -> x12, waiting for transfers between devices: none -> 4.49 us  [all_around(): lax.ppermute(array, axis, [(i, (i + k) % size) for i in range(size)])]
    all_to_all x4, starting transfers between devices: 18.8 us -> 23.2 us  [exchange(): return lax.all_to_all(pieces, axis, split_axis=0, concat_axis=0, tiled=True)]
    all_to_all x4, waiting for transfers between devices: 25.2 us -> 21.9 us  [exchange(): return lax.all_to_all(pieces, axis, split_axis=0, concat_axis=0, tiled=True)]
    pallas_call x1, Pallas kernels: 7.12 us -> 10.3 us  [apply_tile(): pl.pallas_call(apply_kernel, in_specs=[hbm(), hbm(), vmem(), vmem()], out...]
  transfers between devices with their start and end apart: 6 -> 18, of which waited for: 6 -> 7; matrix products, arithmetic and copies ran while one was open for 0% -> 0% of each run, Pallas kernels for 5% -> 7%
where the time goes in v6:
time: 140 us; the launch traced here: 139 us
  starting transfers between devices  44.5 us (32%)
  blocking collectives  33.2 us (24%)
  Pallas kernels  30.3 us (22%)
  waiting for transfers between devices  28.4 us (20%)
  between operations  2.3 us (2%)
    all_to_all x2, blocking collectives, exchange(): return lax.all_to_all(pieces, axis, split_axis=0, concat_axis=0, tiled=True)  33.2 us
    all_to_all x4, starting transfers between devices, exchange(): return lax.all_to_all(pieces, axis, split_axis=0, concat_axis=0, tiled=True)  23.2 us
    all_to_all x4, waiting for transfers between devices, exchange(): return lax.all_to_all(pieces, axis, split_axis=0, concat_axis=0, tiled=True)  21.9 us
    ppermute x12, starting transfers between devices, all_around(): lax.ppermute(array, axis, [(i, (i + k) % size) for i in range(size)])  13.5 us
    pallas_call x1, Pallas kernels, apply_tile(): pl.pallas_call(apply_kernel, in_specs=[hbm(), hbm(), vmem(), vmem()], out...  10.3 us
    pallas_call x1, Pallas kernels, make_tile(): pl.pallas_call(tile_kernel, in_specs=[vmem(), vmem(), vmem()], out_specs=...  9.54 us
    ppermute x2, starting transfers between devices, other_core(): return lax.ppermute(array, CORE, [(0, 1), (1, 0)])  7.77 us
    pallas_call x1, Pallas kernels, solve(): pl.pallas_call(solve_kernel, in_specs=[vmem()] * 6 + [smem()], out_shape=...  4.85 us
  transfers between devices with their start and end apart: 18, of which 7 were waited for; matrix products, arithmetic and copies ran while one was open for 0% of the time, Pallas kernels for 7%

profile of v6, /device:TPU:1, one launch (start us, length us, event | category | flops | bytes accessed | tf_op | source)
XLA Modules:
  0.0 139.1 jit_solution(3754781845820246898)
XLA Ops:
  0.6 1.8 %spread.1 = (f32[8,88,128]{2,1,0:T(8,128)}, f32[16,128]{1,0:T(8,128)S(1)}, f32[64,128]{1,0:T(8,128)S(1)}, f32[80,128]{1,0:T(8,128)S(1)}) custom-call(f32[16,128]{1,0:T(8,128)} %points_hbm.1, f32[1,16]{1,0:T(1,128)} %bitcast.47, f32[8,128]{1,0:T(8,128)} %initial_hbm.1, f32[64,128]{1,0:T(8,128)} %ritz_hbm.1, f32[8,128]{1,0:T(8,128)} %targets_hbm.1), custom_call_target="tpu_custom_call" | custom-call | tf_op jit(solution)/shard_map/spread/pallas_call | solution.py:125
  2.4 3.4 %collective-permute-start.3 = (f32[16,128]{1,0:T(8,128)S(1)}, f32[16,128]{1,0:T(8,128)S(1)}, u32[]{:S(2)}, u32[]{:S(2)}) collective-permute-start(f32[16,128]{1,0:T(8,128)S(1)} %get-tuple-element.25), channel_id=1, source_target_pairs={{0,6},{2,0},{4,2},{6,4},{1,7},{3,1},{5,3},{7,5},{8,14},{10,8},{12,... | collective-permute-start | bytes 24584 | tf_op jit(solution)/shard_map/ppermute | solution.py:454
  5.8 0.5 collective-permute-start.2
  6.3 0.6 collective-permute-start.1
  6.9 8.2 %all-to-all-start = ((f32[8,88,128]{2,1,0:T(8,128)}), f32[8,88,128]{2,1,0:T(8,128)S(1)}, u32[]{:S(2)}, u32[]{:S(2)}) async-start(f32[8,88,128]{2,1,0:T(8,128)} %get-tuple-element.24), calls=%async_computation | async-start | bytes 720896 | tf_op jit(solution)/shard_map/all_to_all | solution.py:447
  16.5 0.0 collective-permute-done.1
  16.5 0.0 collective-permute-done.2
  16.5 0.0 collective-permute-done.3
  16.6 2.8 %collective-permute-start.6 = (f32[4,16,128]{2,1,0:T(8,128)S(1)}, f32[4,16,128]{2,1,0:T(8,128)S(1)}, u32[]{:S(2)}, u32[]{:S(2)}) collective-permute-start(f32[4,16,128]{2,1,0:T(8,128)S(1)} %bitcast_dynamic-update-slice_fusion.12), channel_id=1, source_target_pairs={{0,192},{64,0},{128,64},{192,128},{1,193},{65,1},{129,65},{193,129... | collective-permute-start | bytes 98312 | tf_op jit(solution)/shard_map/ppermute | solution.py:454
  19.4 0.3 collective-permute-start.5
  19.7 0.7 collective-permute-start.4
  20.5 3.8 %collective-permute-done.4 = f32[4,16,128]{2,1,0:T(8,128)S(1)} collective-permute-done((f32[4,16,128]{2,1,0:T(8,128)S(1)}, f32[4,16,128]{2,1,0:T(8,128)S(1)}, u32[]{:S(2)}, u32[]{:S(2)}) %collective-permute-start.4) | collective-permute-done | bytes 32800 | tf_op jit(solution)/shard_map/ppermute | solution.py:454
  24.3 2.5 %all-to-all-done.near_ref = f32[8,88,128]{2,1,0:T(8,128)S(1)} async-done(((f32[8,88,128]{2,1,0:T(8,128)}), f32[8,88,128]{2,1,0:T(8,128)S(1)}, u32[]{:S(2)}, u32[]{:S(2)}) %all-to-all-start) | async-done | bytes 360480 | tf_op jit(solution)/shard_map/all_to_all | solution.py:447
  26.8 3.2 %collective-permute-start = (f32[8,88,128]{2,1,0:T(8,128)S(1)}, f32[8,88,128]{2,1,0:T(8,128)S(1)}, u32[]{:S(2)}, u32[]{:S(2)}) collective-permute-start(f32[8,88,128]{2,1,0:T(8,128)S(1)} %all-to-all-done.near_ref), channel_id=1, source_target_pairs={{0,1},{1,0},{2,3},{3,2},{4,5},{5,4},{6,7},{7,6},{8,9},{9,8},{10,11... | collective-permute-start | bytes 1081352 | tf_op jit(solution)/shard_map/ppermute | solution.py:460
  30.0 0.0 collective-permute-done.5
  30.0 0.0 collective-permute-done.6
  30.1 1.3 collective-permute-done.far_ref
  31.3 9.5 %kernel_tile.1 = (bf16[2048,2048]{1,0:T(8,128)(2,1)}, bf16[2048,2048]{1,0:T(8,128)(2,1)}, f32[16,72,128]{2,1,0:T(8,128)}) custom-call(f32[8,88,128]{2,1,0:T(8,128)S(1)} %all-to-all-done.near_ref, f32[8,88,128]{2,1,0:T(8,128)S(1)} %collective-permute-done.far_ref, f32[16,16,128]{2,1,0:T(8,128)S(1)} %bitcast.45), custom_call_target="tpu_custom_call" | custom-call | tf_op jit(solution)/shard_map/kernel_tile/pallas_call | solution.py:194
  40.9 2.2 %collective-permute-start.9 = (f32[64,128]{1,0:T(8,128)S(1)}, f32[64,128]{1,0:T(8,128)S(1)}, u32[]{:S(2)}, u32[]{:S(2)}) collective-permute-start(f32[64,128]{1,0:T(8,128)S(1)} %get-tuple-element.32), channel_id=1, source_target_pairs={{0,6},{2,0},{4,2},{6,4},{1,7},{3,1},{5,3},{7,5},{8,14},{10,8},{12,... | collective-permute-start | bytes 98312 | tf_op jit(solution)/shard_map/ppermute | solution.py:454
  43.0 1.3 collective-permute-start.8
  44.3 0.0 collective-permute-start.7
  44.3 6.7 %all-to-all-start.1 = ((f32[16,72,128]{2,1,0:T(8,128)}), f32[16,72,128]{2,1,0:T(8,128)S(1)}, u32[]{:S(2)}, u32[]{:S(2)}) async-start(f32[16,72,128]{2,1,0:T(8,128)} %get-tuple-element.30), calls=%async_computation.1 | async-start | bytes 1179648 | tf_op jit(solution)/shard_map/all_to_all | solution.py:447
  51.0 0.0 collective-permute-done.7
  51.1 0.0 collective-permute-done.8
  51.1 0.0 collective-permute-done.9
  51.1 10.8 %all-to-all-done.1.got_ref = f32[16,72,128]{2,1,0:T(8,128)S(1)} async-done(((f32[16,72,128]{2,1,0:T(8,128)}), f32[16,72,128]{2,1,0:T(8,128)S(1)}, u32[]{:S(2)}, u32[]{:S(2)}) %all-to-all-start.1) | async-done | bytes 589856 | tf_op jit(solution)/shard_map/all_to_all | solution.py:447
  61.9 0.9 at_owner.1
  62.8 0.7 collective-permute-start.12
  63.5 0.6 collective-permute-start.11
  64.1 0.5 collective-permute-start.10
  64.6 5.0 %all-to-all-start.2 = ((f32[16,72,128]{2,1,0:T(8,128)}), f32[16,72,128]{2,1,0:T(8,128)S(1)}, u32[]{:S(2)}, u32[]{:S(2)}) async-start(f32[16,72,128]{2,1,0:T(8,128)} %at_owner.1), calls=%async_computation.2 | async-start | bytes 1179648 | tf_op jit(solution)/shard_map/all_to_all | solution.py:447
  69.6 0.6 collective-permute-done.10
  70.3 0.0 collective-permute-done.11
  70.3 0.0 collective-permute-done.12
  70.3 8.6 %all-to-all-done.2.vec_ref = f32[16,72,128]{2,1,0:T(8,128)S(1)} async-done(((f32[16,72,128]{2,1,0:T(8,128)}), f32[16,72,128]{2,1,0:T(8,128)S(1)}, u32[]{:S(2)}, u32[]{:S(2)}) %all-to-all-start.2) | async-done | bytes 589856 | tf_op jit(solution)/shard_map/all_to_all | solution.py:447
  78.9 2.1 %gram.1 = f32[8,41,128]{2,1,0:T(8,128)} custom-call(f32[16,72,128]{2,1,0:T(8,128)S(1)} %all-to-all-done.2.vec_ref, f32[16,64,128]{2,1,0:T(8,128)S(1)} %bitcast.42), custom_call_target="tpu_custom_call" | custom-call | tf_op jit(solution)/shard_map/gram/pallas_call | solution.py:262
  81.0 3.4 %all-to-all-start.3 = ((f32[8,41,128]{2,1,0:T(8,128)}), f32[8,41,128]{2,1,0:T(8,128)S(1)}, u32[]{:S(2)}, u32[]{:S(2)}) async-start(f32[8,41,128]{2,1,0:T(8,128)} %gram.1), calls=%async_computation.3 | async-start | bytes 393216 | tf_op jit(solution)/shard_map/all_to_all | solution.py:447
  84.4 10.3 %apply_tile.1 = (f32[8,2048]{1,0:T(8,128)S(1)}, bf16[384,2048]{1,0:T(8,128)(2,1)S(1)}) custom-call(bf16[2048,2048]{1,0:T(8,128)(2,1)} %get-tuple-element.26.hi_hbm, bf16[2048,2048]{1,0:T(8,128)(2,1)} %get-tuple-element.27.lo_hbm, f32[16,72,128]{2,1,0:T(8,128)S(1)} %all-to-all-done.2.vec_ref, f32[16,64,128]{2,1,0:T(8,128)S(1)} %bitcast.43), custom_call_target="tpu_custom_call" | custom-call | flops 4831838208 | bytes 16777216 | tf_op jit(solution)/shard_map/apply_tile/pallas_call | solution.py:336
  94.6 0.0 all-to-all-done.3
  94.7 4.6 %collective-permute-start.13 = (f32[41,128]{1,0:T(8,128)S(1)}, f32[41,128]{1,0:T(8,128)S(1)}, u32[]{:S(2)}, u32[]{:S(2)}) collective-permute-start(f32[41,128]{1,0:T(8,128)S(1)} %reduce_sum.9.gram_ref), channel_id=1, source_target_pairs={{0,1},{1,0},{2,3},{3,2},{4,5},{5,4},{6,7},{7,6},{8,9},{9,8},{10,11... | collective-permute-start | bytes 62984 | tf_op jit(solution)/shard_map/ppermute | solution.py:460
  99.3 0.1 pad_add_fusion.place_ref
  99.3 0.8 collective-permute-done.13.more_ref
  100.1 4.8 %solve.1 = (f32[16,8,128]{2,1,0:T(8,128)S(1)}, f32[24,128]{1,0:T(8,128)S(1)}) custom-call(f32[41,128]{1,0:T(8,128)S(1)} %reduce_sum.9.gram_ref, f32[41,128]{1,0:T(8,128)S(1)} %collective-permute-done.13.more_ref, f32[8,2048]{1,0:T(8,128)S(1)} %get-tuple-element.40.image_ref, bf16[384,2048]{1,0:T(8,128)(2,1)S(1)} %get-tuple-element.41.split_ref, ...), custom_call_target="tpu_custom_call" | custom-call | tf_op jit(solution)/shard_map/solve/pallas_call | solution.py:388
  105.0 14.4 %all_to_all.36.got_ref = f32[16,8,128]{2,1,0:T(8,128)S(1)} all-to-all(f32[16,8,128]{2,1,0:T(8,128)S(1)} %get-tuple-element.42), channel_id=1, replica_groups=mesh['row_0'=4,'row_1'=8,'col_0'=4,'col_1'=2] {'col_1','row_1'}, dimensions={0} | all-to-all | bytes 131072 | tf_op jit(solution)/shard_map/all_to_all | solution.py:447
  119.4 0.2 stats.1
  119.6 18.8 %all_to_all.37 = f32[256,1,16]{2,1,0:T(1,128)S(1)} all-to-all(f32[256,1,16]{2,1,0:T(1,128)S(1)} %bitcast.46), channel_id=1, replica_groups=mesh['row_0'=4,'row_1'=8,'col_0'=4,'col_1'=2] {'col_0','col_1','row_0','..., dimensions={0} | all-to-all | bytes 32768 | tf_op jit(solution)/shard_map/all_to_all | solution.py:447
  138.4 0.7 finish.1
  (21 shorter events, 0.2 us)
Async XLA Ops:
  2.4 14.2 %collective-permute-start.3 = (f32[16,128]{1,0:T(8,128)S(1)}, f32[16,128]{1,0:T(8,128)S(1)}, u32[]{:S(2)}, u32[]{:S(2)}) collective-permute-start(f32[16,128]{1,0:T(8,128)S(1)} %get-tuple-element.25), channel_id=1, source_target_pairs={{0,6},{2,0},{4,2},{6,4},{1,7},{3,1},{5,3},{7,5},{8,14},{10,8},{12,... | collective-permute-start | bytes 24584 | tf_op jit(solution)/shard_map/ppermute | solution.py:454
  5.8 10.8 %collective-permute-start.2 = (f32[16,128]{1,0:T(8,128)S(1)}, f32[16,128]{1,0:T(8,128)S(1)}, u32[]{:S(2)}, u32[]{:S(2)}) collective-permute-start(f32[16,128]{1,0:T(8,128)S(1)} %get-tuple-element.25), channel_id=1, source_target_pairs={{0,4},{2,6},{4,0},{6,2},{1,5},{3,7},{5,1},{7,3},{8,12},{10,14},{12... | collective-permute-start | bytes 24584 | tf_op jit(solution)/shard_map/ppermute | solution.py:454
  6.3 10.2 %collective-permute-start.1 = (f32[16,128]{1,0:T(8,128)S(1)}, f32[16,128]{1,0:T(8,128)S(1)}, u32[]{:S(2)}, u32[]{:S(2)}) collective-permute-start(f32[16,128]{1,0:T(8,128)S(1)} %get-tuple-element.25), channel_id=1, source_target_pairs={{0,2},{2,4},{4,6},{6,0},{1,3},{3,5},{5,7},{7,1},{8,10},{10,12},{12... | collective-permute-start | bytes 24584 | tf_op jit(solution)/shard_map/ppermute | solution.py:454
  6.9 20.0 %all-to-all-start = ((f32[8,88,128]{2,1,0:T(8,128)}), f32[8,88,128]{2,1,0:T(8,128)S(1)}, u32[]{:S(2)}, u32[]{:S(2)}) async-start(f32[8,88,128]{2,1,0:T(8,128)} %get-tuple-element.24), calls=%async_computation | async-start | bytes 720896 | tf_op jit(solution)/shard_map/all_to_all | solution.py:447
  16.6 13.5 %collective-permute-start.6 = (f32[4,16,128]{2,1,0:T(8,128)S(1)}, f32[4,16,128]{2,1,0:T(8,128)S(1)}, u32[]{:S(2)}, u32[]{:S(2)}) collective-permute-start(f32[4,16,128]{2,1,0:T(8,128)S(1)} %bitcast_dynamic-update-slice_fusion.12), channel_id=1, source_target_pairs={{0,192},{64,0},{128,64},{192,128},{1,193},{65,1},{129,65},{193,129... | collective-permute-start | bytes 98312 | tf_op jit(solution)/shard_map/ppermute | solution.py:454
  19.4 10.6 %collective-permute-start.5 = (f32[4,16,128]{2,1,0:T(8,128)S(1)}, f32[4,16,128]{2,1,0:T(8,128)S(1)}, u32[]{:S(2)}, u32[]{:S(2)}) collective-permute-start(f32[4,16,128]{2,1,0:T(8,128)S(1)} %bitcast_dynamic-update-slice_fusion.12), channel_id=1, source_target_pairs={{0,128},{64,192},{128,0},{192,64},{1,129},{65,193},{129,1},{193,65... | collective-permute-start | bytes 98312 | tf_op jit(solution)/shard_map/ppermute | solution.py:454
  19.7 4.6 %collective-permute-start.4 = (f32[4,16,128]{2,1,0:T(8,128)S(1)}, f32[4,16,128]{2,1,0:T(8,128)S(1)}, u32[]{:S(2)}, u32[]{:S(2)}) collective-permute-start(f32[4,16,128]{2,1,0:T(8,128)S(1)} %bitcast_dynamic-update-slice_fusion.12), channel_id=1, source_target_pairs={{0,64},{64,128},{128,192},{192,0},{1,65},{65,129},{129,193},{193,1... | collective-permute-start | bytes 98312 | tf_op jit(solution)/shard_map/ppermute | solution.py:454
  26.8 4.5 %collective-permute-start = (f32[8,88,128]{2,1,0:T(8,128)S(1)}, f32[8,88,128]{2,1,0:T(8,128)S(1)}, u32[]{:S(2)}, u32[]{:S(2)}) collective-permute-start(f32[8,88,128]{2,1,0:T(8,128)S(1)} %all-to-all-done.near_ref), channel_id=1, source_target_pairs={{0,1},{1,0},{2,3},{3,2},{4,5},{5,4},{6,7},{7,6},{8,9},{9,8},{10,11... | collective-permute-start | bytes 1081352 | tf_op jit(solution)/shard_map/ppermute | solution.py:460
  40.9 10.2 %collective-permute-start.9 = (f32[64,128]{1,0:T(8,128)S(1)}, f32[64,128]{1,0:T(8,128)S(1)}, u32[]{:S(2)}, u32[]{:S(2)}) collective-permute-start(f32[64,128]{1,0:T(8,128)S(1)} %get-tuple-element.32), channel_id=1, source_target_pairs={{0,6},{2,0},{4,2},{6,4},{1,7},{3,1},{5,3},{7,5},{8,14},{10,8},{12,... | collective-permute-start | bytes 98312 | tf_op jit(solution)/shard_map/ppermute | solution.py:454
  43.0 8.0 %collective-permute-start.8 = (f32[64,128]{1,0:T(8,128)S(1)}, f32[64,128]{1,0:T(8,128)S(1)}, u32[]{:S(2)}, u32[]{:S(2)}) collective-permute-start(f32[64,128]{1,0:T(8,128)S(1)} %get-tuple-element.32), channel_id=1, source_target_pairs={{0,4},{2,6},{4,0},{6,2},{1,5},{3,7},{5,1},{7,3},{8,12},{10,14},{12... | collective-permute-start | bytes 98312 | tf_op jit(solution)/shard_map/ppermute | solution.py:454
  44.3 6.7 %collective-permute-start.7 = (f32[64,128]{1,0:T(8,128)S(1)}, f32[64,128]{1,0:T(8,128)S(1)}, u32[]{:S(2)}, u32[]{:S(2)}) collective-permute-start(f32[64,128]{1,0:T(8,128)S(1)} %get-tuple-element.32), channel_id=1, source_target_pairs={{0,2},{2,4},{4,6},{6,0},{1,3},{3,5},{5,7},{7,1},{8,10},{10,12},{12... | collective-permute-start | bytes 98312 | tf_op jit(solution)/shard_map/ppermute | solution.py:454
  44.3 17.6 %all-to-all-start.1 = ((f32[16,72,128]{2,1,0:T(8,128)}), f32[16,72,128]{2,1,0:T(8,128)S(1)}, u32[]{:S(2)}, u32[]{:S(2)}) async-start(f32[16,72,128]{2,1,0:T(8,128)} %get-tuple-element.30), calls=%async_computation.1 | async-start | bytes 1179648 | tf_op jit(solution)/shard_map/all_to_all | solution.py:447
  62.8 7.5 %collective-permute-start.12 = (f32[4,64,128]{2,1,0:T(8,128)S(1)}, f32[4,64,128]{2,1,0:T(8,128)S(1)}, u32[]{:S(2)}, u32[]{:S(2)}) collective-permute-start(f32[4,64,128]{2,1,0:T(8,128)S(1)} %bitcast_dynamic-update-slice_fusion.4), channel_id=1, source_target_pairs={{0,192},{64,0},{128,64},{192,128},{1,193},{65,1},{129,65},{193,129... | collective-permute-start | bytes 393224 | tf_op jit(solution)/shard_map/ppermute | solution.py:454
  63.5 6.7 %collective-permute-start.11 = (f32[4,64,128]{2,1,0:T(8,128)S(1)}, f32[4,64,128]{2,1,0:T(8,128)S(1)}, u32[]{:S(2)}, u32[]{:S(2)}) collective-permute-start(f32[4,64,128]{2,1,0:T(8,128)S(1)} %bitcast_dynamic-update-slice_fusion.4), channel_id=1, source_target_pairs={{0,128},{64,192},{128,0},{192,64},{1,129},{65,193},{129,1},{193,65... | collective-permute-start | bytes 393224 | tf_op jit(solution)/shard_map/ppermute | solution.py:454
  64.1 6.2 %collective-permute-start.10 = (f32[4,64,128]{2,1,0:T(8,128)S(1)}, f32[4,64,128]{2,1,0:T(8,128)S(1)}, u32[]{:S(2)}, u32[]{:S(2)}) collective-permute-start(f32[4,64,128]{2,1,0:T(8,128)S(1)} %bitcast_dynamic-update-slice_fusion.4), channel_id=1, source_target_pairs={{0,64},{64,128},{128,192},{192,0},{1,65},{65,129},{129,193},{193,1... | collective-permute-start | bytes 393224 | tf_op jit(solution)/shard_map/ppermute | solution.py:454
  64.6 14.3 %all-to-all-start.2 = ((f32[16,72,128]{2,1,0:T(8,128)}), f32[16,72,128]{2,1,0:T(8,128)S(1)}, u32[]{:S(2)}, u32[]{:S(2)}) async-start(f32[16,72,128]{2,1,0:T(8,128)} %at_owner.1), calls=%async_computation.2 | async-start | bytes 1179648 | tf_op jit(solution)/shard_map/all_to_all | solution.py:447
  81.0 13.7 %all-to-all-start.3 = ((f32[8,41,128]{2,1,0:T(8,128)}), f32[8,41,128]{2,1,0:T(8,128)S(1)}, u32[]{:S(2)}, u32[]{:S(2)}) async-start(f32[8,41,128]{2,1,0:T(8,128)} %gram.1), calls=%async_computation.3 | async-start | bytes 393216 | tf_op jit(solution)/shard_map/all_to_all | solution.py:447
  94.7 5.5 %collective-permute-start.13 = (f32[41,128]{1,0:T(8,128)S(1)}, f32[41,128]{1,0:T(8,128)S(1)}, u32[]{:S(2)}, u32[]{:S(2)}) collective-permute-start(f32[41,128]{1,0:T(8,128)S(1)} %reduce_sum.9.gram_ref), channel_id=1, source_target_pairs={{0,1},{1,0},{2,3},{3,2},{4,5},{5,4},{6,7},{7,6},{8,9},{9,8},{10,11... | collective-permute-start | bytes 62984 | tf_op jit(solution)/shard_map/ppermute | solution.py:460

commit v7 on v6

--- a/solution.py
+++ b/solution.py
@@ -25,7 +25,7 @@
 PTS = NB * BLK
 STEP = 256
 CHUNK = 256
-READ = 256
+READ = 512
 HALF = 2 * RHS + 2 * RITZ
 PACKED = RHS + RITZ // 2 + 1
 WORLD = 256
@@ -72,10 +72,6 @@
     return pltpu.with_memory_space_constraint(array, pltpu.HBM)
 
 
-def smem():
-    return pl.BlockSpec(memory_space=pltpu.SMEM)
-
-
 def shape(*dims):
     return jax.ShapeDtypeStruct(dims, F32)
 
@@ -96,7 +92,6 @@
     targets_hbm,
     near_ref,
     pts_ref,
-    ritz_ref,
     held_ref,
     points_ref,
     scale_ref,
@@ -117,19 +112,18 @@
     for b in range(NB // 2):
         near_ref[b, pl.ds(0, FEAT), :] = scaled
         near_ref[b, pl.ds(FEAT, VEC), :] = held_ref[pl.ds(RHS, VEC), :]
-    pts_ref[...] = scaled
-    ritz_ref[...] = held_ref[pl.ds(2 * RHS, RITZ), :]
+    pts_ref[pl.ds(0, FEAT), :] = scaled
+    pts_ref[pl.ds(FEAT, RITZ), :] = held_ref[pl.ds(2 * RHS, RITZ), :]
 
 
 def spread(points, scales, initial, ritz, targets):
     return pl.pallas_call(
         spread_kernel,
         in_specs=[hbm()] * 5,
-        out_specs=[vmem()] * 4,
+        out_specs=[vmem()] * 3,
         out_shape=[
             shape(NB // 2, FEAT + VEC, BLK),
-            shape(FEAT, BLK),
-            shape(RITZ, BLK),
+            shape(FEAT + RITZ, BLK),
             shape(RHS + VEC, BLK),
         ],
         scratch_shapes=[
@@ -154,7 +148,7 @@
         hi, lo = split2(tall)
         vec_ref[lanes, pl.ds(0, BLK)] = hi
         vec_ref[lanes, pl.ds(BLK, BLK)] = lo
-        rows_ref[lanes, :] = features(out_ref[b], True).T.astype(BF16)
+        rows_ref[lanes, :] = features(out_ref[b, :FEAT, :], True).T.astype(BF16)
 
     def copies(step):
         rows = pl.ds(step * STEP, STEP)
@@ -213,11 +207,12 @@
     )(near, far, out)
 
 
-def owner_kernel(got_ref, held_ref, gain_ref, nugget_ref, out_ref):
+def owner_kernel(got_ref, held_ref, scalars_ref, out_ref):
     total = got_ref[0]
     for b in range(1, NB):
         total += got_ref[b]
-    applied = gain_ref[0] * total + nugget_ref[0] * held_ref[pl.ds(RHS, VEC), :]
+    gain, nugget = scalars_ref[pl.ds(0, 1), :], scalars_ref[pl.ds(1, 1), :]
+    applied = gain * total + nugget * held_ref[pl.ds(RHS, VEC), :]
     first = held_ref[pl.ds(0, RHS), :] - applied[:RHS]
     image = applied[RHS:]
     for b in range(NB):
@@ -225,25 +220,24 @@
         out_ref[b, pl.ds(RHS, RITZ), :] = image
 
 
-def at_owner(got, held, gain, nugget):
+def at_owner(got, held, scalars):
     return pl.pallas_call(
         owner_kernel,
-        in_specs=[vmem(), vmem(), smem(), smem()],
         out_shape=shape(NB, VEC, BLK),
         compiler_params=limit(8),
         name="at_owner",
-    )(got, held, gain, nugget)
+    )(got, held, scalars)
 
 
 def square_iota():
     return lax.broadcasted_iota(jnp.int32, (RITZ, RITZ), 0), lax.broadcasted_iota(jnp.int32, (RITZ, RITZ), 1)
 
 
-def gram_kernel(vec_ref, ritz_ref, out_ref, left_ref, right_ref):
+def gram_kernel(vec_ref, pts_ref, out_ref, left_ref, right_ref):
     for b in range(NB):
         lanes = pl.ds(b * BLK, BLK)
         left_ref[:, lanes] = vec_ref[b]
-        right_ref[pl.ds(0, RITZ), lanes] = ritz_ref[b]
+        right_ref[pl.ds(0, RITZ), lanes] = pts_ref[b, FEAT:, :]
         right_ref[pl.ds(RITZ, RITZ), lanes] = vec_ref[b, RHS:, :]
     gram = lax.dot_general(left_ref[...], right_ref[...], NT, precision=HIGH, preferred_element_type=F32)
     coarse = gram[RHS:, :RITZ]
@@ -258,14 +252,14 @@
         out_ref[b, pl.ds(RHS + RITZ // 2, 1), :] = jnp.concatenate([diagonal, diagonal], axis=1)
 
 
-def make_gram(vec, ritz):
+def make_gram(vec, pts):
     return pl.pallas_call(
         gram_kernel,
         out_shape=shape(NB // 2, PACKED, BLK),
         scratch_shapes=[pltpu.VMEM((VEC, PTS), F32), pltpu.VMEM((2 * RITZ, PTS), F32)],
         compiler_params=limit(12),
         name="gram",
-    )(vec, ritz)
+    )(vec, pts)
 
 
 def inverse(matrix):
@@ -302,7 +296,7 @@
     return jnp.concatenate(work, axis=0)[:, RITZ:]
 
 
-def apply_kernel(hi_hbm, lo_hbm, vec_ref, ritz_ref, out_ref, split_ref, rows_ref, hi_ref, lo_ref, sem):
+def apply_kernel(hi_hbm, lo_hbm, vec_ref, pts_ref, out_ref, rows_ref, hi_ref, lo_ref, sem):
     copies = []
     for step in range(PTS // READ):
         lanes = pl.ds(step * READ, READ)
@@ -317,7 +311,9 @@
     for b in range(NB):
         lanes = pl.ds(b * BLK, BLK)
         first = vec_ref[b, :RHS, :]
-        hi, lo = split2(jnp.concatenate([first, jnp.zeros_like(first), ritz_ref[b], vec_ref[b, RHS:, :]], axis=0))
+        hi, lo = split2(
+            jnp.concatenate([first, jnp.zeros_like(first), pts_ref[b, FEAT:, :], vec_ref[b, RHS:, :]], axis=0)
+        )
         rows_ref[pl.ds(0, HALF), lanes] = hi
         rows_ref[pl.ds(HALF, HALF), lanes] = lo
     for step in range(PTS // READ):
@@ -326,17 +322,14 @@
             copy.wait()
         both = jnp.dot(rows_ref[...], hi_ref[:, lanes], preferred_element_type=F32)
         more = jnp.dot(rows_ref[pl.ds(0, HALF), :], lo_ref[:, lanes], preferred_element_type=F32)
-        value = both[:HALF] + both[HALF:] + more
-        out_ref[:, lanes] = value[:RHS]
-        for part, piece in enumerate(split3(value[2 * RHS :])):
-            split_ref[pl.ds(part * 2 * RITZ, 2 * RITZ), lanes] = piece.astype(BF16)
-
-
-def apply_tile(hi, lo, vec, ritz):
+        out_ref[:, lanes] = both[:HALF] + both[HALF:] + more
+
+
+def apply_tile(hi, lo, vec, pts):
     return pl.pallas_call(
         apply_kernel,
         in_specs=[hbm(), hbm(), vmem(), vmem()],
-        out_shape=[shape(RHS, PTS), jax.ShapeDtypeStruct((6 * RITZ, PTS), BF16)],
+        out_shape=shape(HALF, PTS),
         scratch_shapes=[
             pltpu.VMEM((2 * HALF, PTS), BF16),
             pltpu.VMEM((PTS, PTS), BF16),
@@ -346,10 +339,10 @@
         compiler_params=limit(32),
         cost_estimate=pl.CostEstimate(flops=8 * HALF * PTS * PTS, bytes_accessed=4 * PTS * PTS, transcendentals=0),
         name="apply_tile",
-    )(in_hbm(hi), in_hbm(lo), vec, ritz)
-
-
-def solve_kernel(gram_ref, more_ref, image_ref, split_ref, vec_ref, held_ref, place_ref, part_ref, own_ref):
+    )(in_hbm(hi), in_hbm(lo), vec, pts)
+
+
+def solve_kernel(gram_ref, more_ref, image_ref, vec_ref, held_ref, part_ref, own_ref):
     gram = gram_ref[...] + more_ref[...]
     projected = gram[:RHS, :RITZ]
     first = gram[:RHS, RITZ:]
@@ -364,17 +357,14 @@
     turns = lax.dot_general(against, solve, NT, precision=HIGH, preferred_element_type=F32)
     zero = jnp.zeros_like(turns)
     coef = jnp.concatenate([turns, amounts], axis=1)
-    pieces = split3(coef)
-    value = image_ref[...]
-    for part, rows in ((2, 1), (1, 2), (0, 3)):
-        left = jnp.concatenate(pieces[:rows], axis=0).astype(BF16)
-        more = jnp.dot(left, split_ref[pl.ds(part * 2 * RITZ, 2 * RITZ), :], preferred_element_type=F32)
-        for q in range(rows):
-            value -= more[q * RHS : (q + 1) * RHS]
+    value = image_ref[pl.ds(0, RHS), :] - jnp.dot(
+        coef, image_ref[pl.ds(2 * RHS, 2 * RITZ), :], precision=HIGH, preferred_element_type=F32
+    )
+    core = lax.axis_index(CORE)
     for at in range(NB):
-        half = (at // (NB // 2) + place_ref[2]) % 2
+        half = (at // (NB // 2) + core) % 2
         part_ref[half * (NB // 2) + at % (NB // 2)] = value[:, at * BLK : (at + 1) * BLK]
-    mine = place_ref[1] * 4 + place_ref[0]
+    mine = lax.axis_index("row_0") * 4 + lax.axis_index("col_0")
     basis = jnp.concatenate([held_ref[pl.ds(2 * RHS, RITZ), :], vec_ref[mine, RHS:, :]], axis=0)
     wanted = jnp.concatenate(
         [coef, jnp.concatenate([zero, amounts], axis=1), jnp.concatenate([-amounts, zero], axis=1)], axis=0
@@ -384,23 +374,22 @@
     own_ref[...] = base - jnp.dot(wanted, basis, precision=HIGH, preferred_element_type=F32)
 
 
-def solve(gram, more, image, split, vec, held, place):
+def solve(gram, more, image, vec, held):
     return pl.pallas_call(
         solve_kernel,
-        in_specs=[vmem()] * 6 + [smem()],
         out_shape=[shape(NB, RHS, BLK), shape(3 * RHS, BLK)],
         compiler_params=limit(12),
         name="solve",
-    )(gram, more, image, split, vec, held, place)
-
-
-def stats_kernel(got_ref, own_ref, gain_ref, nugget_ref, applied_ref, out_ref):
+    )(gram, more, image, vec, held)
+
+
+def stats_kernel(got_ref, own_ref, scalars_ref, applied_ref, out_ref):
     total = got_ref[0]
     for b in range(1, NB):
         total += got_ref[b]
     direction = own_ref[pl.ds(0, RHS), :]
     residual = own_ref[pl.ds(RHS, RHS), :]
-    applied = gain_ref[0] * total + nugget_ref[0] * direction
+    applied = scalars_ref[pl.ds(0, 1), :] * total + scalars_ref[pl.ds(1, 1), :] * direction
     applied_ref[...] = applied
     sums = jnp.concatenate(
         [
@@ -414,14 +403,13 @@
         out_ref[pl.ds(b * RHS, RHS), :] = sums
 
 
-def make_stats(got, own, gain, nugget):
+def make_stats(got, own, scalars):
     return pl.pallas_call(
         stats_kernel,
-        in_specs=[vmem(), vmem(), smem(), smem()],
         out_shape=[shape(RHS, BLK), shape(WORLD, 2 * RHS)],
         compiler_params=limit(8),
         name="stats",
-    )(got, own, gain, nugget)
+    )(got, own, scalars)
 
 
 def finish_kernel(got_ref, own_ref, applied_ref, solution_ref, residual_ref):
@@ -461,28 +449,24 @@
 
 
 def local(points, inv_scales, amplitude, noise_var, targets, initial, ritz_basis):
-    near, pts, ritz, held = spread(points, inv_scales[None, :], initial, ritz_basis, targets)
-    place = jnp.stack([lax.axis_index("col_0"), lax.axis_index("row_0"), lax.axis_index(CORE)]).astype(jnp.int32)
+    near, pts, held = spread(points, inv_scales[None, :], initial, ritz_basis, targets)
+    scalars = jnp.concatenate([amplitude, noise_var])
+    scalars = jnp.broadcast_to(scalars[:, None], (2, BLK))
     near = exchange(near, Z)
     pts = all_around(pts, "col_0")
-    pts = all_around(pts, "row_0").reshape(NB, FEAT, BLK)
+    pts = all_around(pts, "row_0").reshape(NB, FEAT + RITZ, BLK)
+    near, scalars = lax.optimization_barrier((near, scalars))
     far = other_core(near)
     hi, lo, part = make_tile(near, far, pts)
 
-    part, ritz = lax.optimization_barrier((part, ritz))
-    part = exchange(part, XY)
-    ritz = all_around(ritz, "col_0")
-    own = at_owner(part, held, amplitude, noise_var)
-    own, ritz = lax.optimization_barrier((own, ritz))
-    vec = exchange(own, XY)
-    ritz = all_around(ritz, "row_0").reshape(NB, RITZ, BLK)
-    gram = make_gram(vec, ritz)
+    vec = exchange(at_owner(exchange(part, XY), held, scalars), XY)
+    gram = make_gram(vec, pts)
     vec, gram = lax.optimization_barrier((vec, gram))
-    image, split = apply_tile(hi, lo, vec, ritz)
-    image, split, gram = lax.optimization_barrier((image, split, exchange(gram, Z)))
+    image = apply_tile(hi, lo, vec, pts)
+    image, gram = lax.optimization_barrier((image, exchange(gram, Z)))
     gram = jnp.sum(gram, axis=0)
-    part, own = solve(gram, other_core(gram), image, split, vec, held, place)
-    applied, stats = make_stats(exchange(part, CZ), own, amplitude, noise_var)
+    part, own = solve(gram, other_core(gram), image, vec, held)
+    applied, stats = make_stats(exchange(part, CZ), own, scalars)
     return tuple(finish(exchange(stats, EVERY), own, applied))
 
 

time: 140 us -> 129 us (0.921)
  blocking collectives: 33.2 us -> 60.7 us
  starting transfers between devices: 44.5 us -> 27.3 us
  waiting for transfers between devices: 28.4 us -> 12.9 us
  Pallas kernels: 30.3 us -> 25.2 us
    all_to_all x2 -> x4, blocking collectives: 33.2 us -> 60.7 us  [exchange(): return lax.all_to_all(pieces, axis, split_axis=0, concat_axis=0, tiled=True)]
    all_to_all x4 -> x2, waiting for transfers between devices: 21.9 us -> 1.61 us  [exchange(): return lax.all_to_all(pieces, axis, split_axis=0, concat_axis=0, tiled=True)]
    all_to_all x4 -> x2, starting transfers between devices: 23.2 us -> 13.5 us  [exchange(): return lax.all_to_all(pieces, axis, split_axis=0, concat_axis=0, tiled=True)]
    ppermute x12 -> x6, starting transfers between devices: 13.5 us -> 8.35 us  [all_around(): lax.ppermute(array, axis, [(i, (i + k) % size) for i in range(size)])]
    ppermute x12 -> x6, waiting for transfers between devices: 4.49 us -> 9.18 us  [all_around(): lax.ppermute(array, axis, [(i, (i + k) % size) for i in range(size)])]
    pallas_call x1, Pallas kernels: 10.3 us -> 7.12 us  [apply_tile(): pl.pallas_call(apply_kernel, in_specs=[hbm(), hbm(), vmem(), vmem()], out...]
    ppermute x2, starting transfers between devices: 7.77 us -> 5.43 us  [other_core(): return lax.ppermute(array, CORE, [(0, 1), (1, 0)])]
  transfers between devices with their start and end apart: 18 -> 10, of which waited for: 7 -> 4; matrix products, arithmetic and copies ran while one was open for 0% -> 0% of each run, Pallas kernels for 7% -> 6%
where the time goes in v7:
time: 129 us; the launch traced here: 128 us
  blocking collectives  60.7 us (47%)
  starting transfers between devices  27.3 us (21%)
  Pallas kernels  25.2 us (20%)
  waiting for transfers between devices  12.9 us (10%)
  between operations  2.12 us (2%)
    all_to_all x4, blocking collectives, exchange(): return lax.all_to_all(pieces, axis, split_axis=0, concat_axis=0, tiled=True)  60.7 us
    all_to_all x2, starting transfers between devices, exchange(): return lax.all_to_all(pieces, axis, split_axis=0, concat_axis=0, tiled=True)  13.5 us
    ppermute x6, waiting for transfers between devices, all_around(): lax.ppermute(array, axis, [(i, (i + k) % size) for i in range(size)])  9.18 us
    pallas_call x1, Pallas kernels, make_tile(): pl.pallas_call(tile_kernel, in_specs=[vmem(), vmem(), vmem()], out_specs=...  8.69 us
    ppermute x6, starting transfers between devices, all_around(): lax.ppermute(array, axis, [(i, (i + k) % size) for i in range(size)])  8.35 us
    pallas_call x1, Pallas kernels, apply_tile(): pl.pallas_call(apply_kernel, in_specs=[hbm(), hbm(), vmem(), vmem()], out...  7.12 us
    ppermute x2, starting transfers between devices, other_core(): return lax.ppermute(array, CORE, [(0, 1), (1, 0)])  5.43 us
    pallas_call x1, Pallas kernels, solve(): pl.pallas_call(solve_kernel, out_shape=[shape(NB, RHS, BLK), shape(3 * RH...  4.55 us
  transfers between devices with their start and end apart: 10, of which 4 were waited for; matrix products, arithmetic and copies ran while one was open for 0% of the time, Pallas kernels for 6%

profile of v7, /device:TPU:1, one launch (start us, length us, event | category | flops | bytes accessed | tf_op | source)
XLA Modules:
  0.0 128.5 jit_solution(689769204533405816)
XLA Ops:
  0.6 1.7 %spread.1 = (f32[8,88,128]{2,1,0:T(8,128)}, f32[80,128]{1,0:T(8,128)S(1)}, f32[80,128]{1,0:T(8,128)S(1)}) custom-call(f32[16,128]{1,0:T(8,128)} %points_hbm.1, f32[1,16]{1,0:T(1,128)} %bitcast.27, f32[8,128]{1,0:T(8,128)} %initial_hbm.1, f32[64,128]{1,0:T(8,128)} %ritz_hbm.1, f32[8,128]{1,0:T(8,128)} %targets_hbm.1), custom_call_target="tpu_custom_call" | custom-call | tf_op jit(solution)/shard_map/spread/pallas_call | solution.py:120
  2.4 3.4 %collective-permute-start.3 = (f32[80,128]{1,0:T(8,128)S(1)}, f32[80,128]{1,0:T(8,128)S(1)}, u32[]{:S(2)}, u32[]{:S(2)}) collective-permute-start(f32[80,128]{1,0:T(8,128)S(1)} %get-tuple-element.20), channel_id=1, source_target_pairs={{0,6},{2,0},{4,2},{6,4},{1,7},{3,1},{5,3},{7,5},{8,14},{10,8},{12,... | collective-permute-start | bytes 122888 | tf_op jit(solution)/shard_map/ppermute | solution.py:442
  5.8 0.5 collective-permute-start.2
  6.3 0.6 collective-permute-start.1
  6.9 8.2 %all-to-all-start = ((f32[8,88,128]{2,1,0:T(8,128)}), f32[8,88,128]{2,1,0:T(8,128)S(1)}, u32[]{:S(2)}, u32[]{:S(2)}) async-start(f32[8,88,128]{2,1,0:T(8,128)} %get-tuple-element.18), calls=%async_computation | async-start | bytes 720896 | tf_op jit(solution)/shard_map/all_to_all | solution.py:435
  16.4 0.1 pad_maximum_fusion
  16.5 0.0 collective-permute-done.1
  16.6 0.0 collective-permute-done.2
  16.6 0.0 collective-permute-done.3
  16.6 2.8 %collective-permute-start.6 = (f32[4,80,128]{2,1,0:T(8,128)S(1)}, f32[4,80,128]{2,1,0:T(8,128)S(1)}, u32[]{:S(2)}, u32[]{:S(2)}) collective-permute-start(f32[4,80,128]{2,1,0:T(8,128)S(1)} %bitcast_dynamic-update-slice_fusion.4), channel_id=1, source_target_pairs={{0,192},{64,0},{128,64},{192,128},{1,193},{65,1},{129,65},{193,129... | collective-permute-start | bytes 491528 | tf_op jit(solution)/shard_map/ppermute | solution.py:442
  19.4 0.3 collective-permute-start.5
  19.8 0.7 collective-permute-start.4
  20.5 9.2 %collective-permute-done.4 = f32[4,80,128]{2,1,0:T(8,128)S(1)} collective-permute-done((f32[4,80,128]{2,1,0:T(8,128)S(1)}, f32[4,80,128]{2,1,0:T(8,128)S(1)}, u32[]{:S(2)}, u32[]{:S(2)}) %collective-permute-start.4) | collective-permute-done | bytes 163872 | tf_op jit(solution)/shard_map/ppermute | solution.py:442
  29.7 0.0 all-to-all-done.near_ref
  29.7 0.1 broadcast_in_dim.42.scalars_ref
  29.8 1.6 %collective-permute-start = (f32[8,88,128]{2,1,0:T(8,128)S(1)}, f32[8,88,128]{2,1,0:T(8,128)S(1)}, u32[]{:S(2)}, u32[]{:S(2)}) collective-permute-start(f32[8,88,128]{2,1,0:T(8,128)S(1)} %all-to-all-done.near_ref), channel_id=1, source_target_pairs={{0,1},{1,0},{2,3},{3,2},{4,5},{5,4},{6,7},{7,6},{8,9},{9,8},{10,11... | collective-permute-start | bytes 1081352 | tf_op jit(solution)/shard_map/ppermute | solution.py:448
  31.4 0.0 collective-permute-done.5
  31.4 0.0 collective-permute-done.6
  31.4 1.2 collective-permute-done.far_ref
  32.7 8.7 %kernel_tile.1 = (bf16[2048,2048]{1,0:T(8,128)(2,1)}, bf16[2048,2048]{1,0:T(8,128)(2,1)}, f32[16,72,128]{2,1,0:T(8,128)S(1)}) custom-call(f32[8,88,128]{2,1,0:T(8,128)S(1)} %all-to-all-done.near_ref, f32[8,88,128]{2,1,0:T(8,128)S(1)} %collective-permute-done.far_ref, f32[16,80,128]{2,1,0:T(8,128)S(1)} %bitcast.22), custom_call_target="tpu_custom_call" | custom-call | tf_op jit(solution)/shard_map/kernel_tile/pallas_call | solution.py:188
  41.4 16.0 %all_to_all.36.got_ref = f32[16,72,128]{2,1,0:T(8,128)S(1)} all-to-all(f32[16,72,128]{2,1,0:T(8,128)S(1)} %get-tuple-element.23), channel_id=1, replica_groups=mesh['row_0'=4,'row_1'=8,'col_0'=4,'col_1'=2] {'row_0','col_0'}, dimensions={0} | all-to-all | bytes 1179648 | tf_op jit(solution)/shard_map/all_to_all | solution.py:435
  57.4 0.1 at_owner.1
  57.5 14.0 %all_to_all.37.vec_ref = f32[16,72,128]{2,1,0:T(8,128)S(1)} all-to-all(f32[16,72,128]{2,1,0:T(8,128)S(1)} %at_owner.1), channel_id=1, replica_groups=mesh['row_0'=4,'row_1'=8,'col_0'=4,'col_1'=2] {'row_0','col_0'}, dimensions={0} | all-to-all | bytes 1179648 | tf_op jit(solution)/shard_map/all_to_all | solution.py:435
  71.5 2.1 %gram.1 = f32[8,41,128]{2,1,0:T(8,128)} custom-call(f32[16,72,128]{2,1,0:T(8,128)S(1)} %all_to_all.37.vec_ref, f32[16,80,128]{2,1,0:T(8,128)S(1)} %bitcast.23), custom_call_target="tpu_custom_call" | custom-call | tf_op jit(solution)/shard_map/gram/pallas_call | solution.py:256
  73.5 5.3 %all-to-all-start.3 = ((f32[8,41,128]{2,1,0:T(8,128)}), f32[8,41,128]{2,1,0:T(8,128)S(1)}, u32[]{:S(2)}, u32[]{:S(2)}) async-start(f32[8,41,128]{2,1,0:T(8,128)} %gram.1), calls=%async_computation.3 | async-start | bytes 393216 | tf_op jit(solution)/shard_map/all_to_all | solution.py:435
  78.9 7.1 %apply_tile.1.image_ref = f32[144,2048]{1,0:T(8,128)S(1)} custom-call(bf16[2048,2048]{1,0:T(8,128)(2,1)} %get-tuple-element.21.hi_hbm, bf16[2048,2048]{1,0:T(8,128)(2,1)} %get-tuple-element.22.lo_hbm, f32[16,72,128]{2,1,0:T(8,128)S(1)} %all_to_all.37.vec_ref, f32[16,80,128]{2,1,0:T(8,128)S(1)} %bitcast.24), custom_call_target="tpu_custom_call" | custom-call | flops 4831838208 | bytes 16777216 | tf_op jit(solution)/shard_map/apply_tile/pallas_call | solution.py:329
  86.0 1.6 %all-to-all-done.3 = f32[8,41,128]{2,1,0:T(8,128)S(1)} async-done(((f32[8,41,128]{2,1,0:T(8,128)}), f32[8,41,128]{2,1,0:T(8,128)S(1)}, u32[]{:S(2)}, u32[]{:S(2)}) %all-to-all-start.3) | async-done | bytes 167968 | tf_op jit(solution)/shard_map/all_to_all | solution.py:435
  87.6 3.9 %collective-permute-start.7 = (f32[41,128]{1,0:T(8,128)S(1)}, f32[41,128]{1,0:T(8,128)S(1)}, u32[]{:S(2)}, u32[]{:S(2)}) collective-permute-start(f32[41,128]{1,0:T(8,128)S(1)} %reduce_sum.9.gram_ref), channel_id=1, source_target_pairs={{0,1},{1,0},{2,3},{3,2},{4,5},{5,4},{6,7},{7,6},{8,9},{9,8},{10,11... | collective-permute-start | bytes 62984 | tf_op jit(solution)/shard_map/ppermute | solution.py:448
  91.5 0.8 collective-permute-done.7.more_ref
  92.3 4.5 %solve.1 = (f32[16,8,128]{2,1,0:T(8,128)S(1)}, f32[24,128]{1,0:T(8,128)S(1)}) custom-call(f32[41,128]{1,0:T(8,128)S(1)} %reduce_sum.9.gram_ref, f32[41,128]{1,0:T(8,128)S(1)} %collective-permute-done.7.more_ref, f32[144,2048]{1,0:T(8,128)S(1)} %apply_tile.1.image_ref, f32[16,72,128]{2,1,0:T(8,128)S(1)} %all_to_all.37.vec_ref, ...), custom_call_target="tpu_custom_call" | custom-call | tf_op jit(solution)/shard_map/solve/pallas_call | solution.py:378
  96.9 11.8 %all_to_all.38.got_ref = f32[16,8,128]{2,1,0:T(8,128)S(1)} all-to-all(f32[16,8,128]{2,1,0:T(8,128)S(1)} %get-tuple-element.30), channel_id=1, replica_groups=mesh['row_0'=4,'row_1'=8,'col_0'=4,'col_1'=2] {'col_1','row_1'}, dimensions={0} | all-to-all | bytes 131072 | tf_op jit(solution)/shard_map/all_to_all | solution.py:435
  108.7 0.2 stats.1
  108.9 18.8 %all_to_all.39 = f32[256,1,16]{2,1,0:T(1,128)S(1)} all-to-all(f32[256,1,16]{2,1,0:T(1,128)S(1)} %bitcast.26), channel_id=1, replica_groups=mesh['row_0'=4,'row_1'=8,'col_0'=4,'col_1'=2] {'col_0','col_1','row_0','..., dimensions={0} | all-to-all | bytes 32768 | tf_op jit(solution)/shard_map/all_to_all | solution.py:435
  127.8 0.7 finish.1
  (11 shorter events, 0.2 us)
Async XLA Ops:
  2.4 14.2 %collective-permute-start.3 = (f32[80,128]{1,0:T(8,128)S(1)}, f32[80,128]{1,0:T(8,128)S(1)}, u32[]{:S(2)}, u32[]{:S(2)}) collective-permute-start(f32[80,128]{1,0:T(8,128)S(1)} %get-tuple-element.20), channel_id=1, source_target_pairs={{0,6},{2,0},{4,2},{6,4},{1,7},{3,1},{5,3},{7,5},{8,14},{10,8},{12,... | collective-permute-start | bytes 122888 | tf_op jit(solution)/shard_map/ppermute | solution.py:442
  5.8 10.8 %collective-permute-start.2 = (f32[80,128]{1,0:T(8,128)S(1)}, f32[80,128]{1,0:T(8,128)S(1)}, u32[]{:S(2)}, u32[]{:S(2)}) collective-permute-start(f32[80,128]{1,0:T(8,128)S(1)} %get-tuple-element.20), channel_id=1, source_target_pairs={{0,4},{2,6},{4,0},{6,2},{1,5},{3,7},{5,1},{7,3},{8,12},{10,14},{12... | collective-permute-start | bytes 122888 | tf_op jit(solution)/shard_map/ppermute | solution.py:442
  6.3 10.3 %collective-permute-start.1 = (f32[80,128]{1,0:T(8,128)S(1)}, f32[80,128]{1,0:T(8,128)S(1)}, u32[]{:S(2)}, u32[]{:S(2)}) collective-permute-start(f32[80,128]{1,0:T(8,128)S(1)} %get-tuple-element.20), channel_id=1, source_target_pairs={{0,2},{2,4},{4,6},{6,0},{1,3},{3,5},{5,7},{7,1},{8,10},{10,12},{12... | collective-permute-start | bytes 122888 | tf_op jit(solution)/shard_map/ppermute | solution.py:442
  6.9 22.9 %all-to-all-start = ((f32[8,88,128]{2,1,0:T(8,128)}), f32[8,88,128]{2,1,0:T(8,128)S(1)}, u32[]{:S(2)}, u32[]{:S(2)}) async-start(f32[8,88,128]{2,1,0:T(8,128)} %get-tuple-element.18), calls=%async_computation | async-start | bytes 720896 | tf_op jit(solution)/shard_map/all_to_all | solution.py:435
  16.6 14.8 %collective-permute-start.6 = (f32[4,80,128]{2,1,0:T(8,128)S(1)}, f32[4,80,128]{2,1,0:T(8,128)S(1)}, u32[]{:S(2)}, u32[]{:S(2)}) collective-permute-start(f32[4,80,128]{2,1,0:T(8,128)S(1)} %bitcast_dynamic-update-slice_fusion.4), channel_id=1, source_target_pairs={{0,192},{64,0},{128,64},{192,128},{1,193},{65,1},{129,65},{193,129... | collective-permute-start | bytes 491528 | tf_op jit(solution)/shard_map/ppermute | solution.py:442
  19.4 11.9 %collective-permute-start.5 = (f32[4,80,128]{2,1,0:T(8,128)S(1)}, f32[4,80,128]{2,1,0:T(8,128)S(1)}, u32[]{:S(2)}, u32[]{:S(2)}) collective-permute-start(f32[4,80,128]{2,1,0:T(8,128)S(1)} %bitcast_dynamic-update-slice_fusion.4), channel_id=1, source_target_pairs={{0,128},{64,192},{128,0},{192,64},{1,129},{65,193},{129,1},{193,65... | collective-permute-start | bytes 491528 | tf_op jit(solution)/shard_map/ppermute | solution.py:442
  19.8 9.9 %collective-permute-start.4 = (f32[4,80,128]{2,1,0:T(8,128)S(1)}, f32[4,80,128]{2,1,0:T(8,128)S(1)}, u32[]{:S(2)}, u32[]{:S(2)}) collective-permute-start(f32[4,80,128]{2,1,0:T(8,128)S(1)} %bitcast_dynamic-update-slice_fusion.4), channel_id=1, source_target_pairs={{0,64},{64,128},{128,192},{192,0},{1,65},{65,129},{129,193},{193,1... | collective-permute-start | bytes 491528 | tf_op jit(solution)/shard_map/ppermute | solution.py:442
  29.8 2.9 %collective-permute-start = (f32[8,88,128]{2,1,0:T(8,128)S(1)}, f32[8,88,128]{2,1,0:T(8,128)S(1)}, u32[]{:S(2)}, u32[]{:S(2)}) collective-permute-start(f32[8,88,128]{2,1,0:T(8,128)S(1)} %all-to-all-done.near_ref), channel_id=1, source_target_pairs={{0,1},{1,0},{2,3},{3,2},{4,5},{5,4},{6,7},{7,6},{8,9},{9,8},{10,11... | collective-permute-start | bytes 1081352 | tf_op jit(solution)/shard_map/ppermute | solution.py:448
  73.5 14.1 %all-to-all-start.3 = ((f32[8,41,128]{2,1,0:T(8,128)}), f32[8,41,128]{2,1,0:T(8,128)S(1)}, u32[]{:S(2)}, u32[]{:S(2)}) async-start(f32[8,41,128]{2,1,0:T(8,128)} %gram.1), calls=%async_computation.3 | async-start | bytes 393216 | tf_op jit(solution)/shard_map/all_to_all | solution.py:435
  87.6 4.7 %collective-permute-start.7 = (f32[41,128]{1,0:T(8,128)S(1)}, f32[41,128]{1,0:T(8,128)S(1)}, u32[]{:S(2)}, u32[]{:S(2)}) collective-permute-start(f32[41,128]{1,0:T(8,128)S(1)} %reduce_sum.9.gram_ref), channel_id=1, source_target_pairs={{0,1},{1,0},{2,3},{3,2},{4,5},{5,4},{6,7},{7,6},{8,9},{9,8},{10,11... | collective-permute-start | bytes 62984 | tf_op jit(solution)/shard_map/ppermute | solution.py:448

commit v8 on v7

--- a/solution.py
+++ b/solution.py
@@ -137,7 +137,7 @@
 
 
 def tile_kernel(
-    near_ref, far_ref, out_ref, hi_hbm, lo_hbm, part_ref, hi_ref, lo_ref, cols_ref, rows_ref, vec_ref, sem
+    near_ref, far_ref, out_ref, mark_ref, hi_hbm, lo_hbm, part_ref, hi_ref, lo_ref, cols_ref, rows_ref, vec_ref, sem
 ):
     for b in range(NB):
         src = near_ref if b < NB // 2 else far_ref
@@ -184,10 +184,10 @@
             copy.wait()
 
 
-def make_tile(near, far, out):
+def make_tile(near, far, out, mark):
     return pl.pallas_call(
         tile_kernel,
-        in_specs=[vmem(), vmem(), vmem()],
+        in_specs=[vmem(), vmem(), vmem(), vmem()],
         out_specs=[hbm(), hbm(), vmem()],
         out_shape=[
             pltpu.HBM((PTS, PTS), BF16),
@@ -204,7 +204,7 @@
         ],
         compiler_params=limit(40),
         name="kernel_tile",
-    )(near, far, out)
+    )(near, far, out, mark)
 
 
 def owner_kernel(got_ref, held_ref, scalars_ref, out_ref):
@@ -452,12 +452,13 @@
     near, pts, held = spread(points, inv_scales[None, :], initial, ritz_basis, targets)
     scalars = jnp.concatenate([amplitude, noise_var])
     scalars = jnp.broadcast_to(scalars[:, None], (2, BLK))
+    pts = all_around(pts, "col_0")
     near = exchange(near, Z)
-    pts = all_around(pts, "col_0")
     pts = all_around(pts, "row_0").reshape(NB, FEAT + RITZ, BLK)
     near, scalars = lax.optimization_barrier((near, scalars))
     far = other_core(near)
-    hi, lo, part = make_tile(near, far, pts)
+    mark = near[0, :8] * 0.5
+    hi, lo, part = make_tile(near, far, pts, mark)
 
     vec = exchange(at_owner(exchange(part, XY), held, scalars), XY)
     gram = make_gram(vec, pts)

time: 129 us -> 129 us (level)
  no operation moved by 1% of the time
where the time goes in v8:
time: 129 us
  blocking collectives  60.7 us (47%)
  starting transfers between devices  27.3 us (21%)
  Pallas kernels  25.2 us (20%)
  waiting for transfers between devices  12.9 us (10%)
  between operations  2.13 us (2%)
    all_to_all x4, blocking collectives, exchange(): return lax.all_to_all(pieces, axis, split_axis=0, concat_axis=0, tiled=True)  60.7 us
    all_to_all x2, starting transfers between devices, exchange(): return lax.all_to_all(pieces, axis, split_axis=0, concat_axis=0, tiled=True)  13.6 us
    ppermute x6, waiting for transfers between devices, all_around(): lax.ppermute(array, axis, [(i, (i + k) % size) for i in range(size)])  9.18 us
    pallas_call x1, Pallas kernels, make_tile(): pl.pallas_call(tile_kernel, in_specs=[vmem(), vmem(), vmem(), vmem()], ou...  8.69 us
    ppermute x6, starting transfers between devices, all_around(): lax.ppermute(array, axis, [(i, (i + k) % size) for i in range(size)])  8.35 us
    pallas_call x1, Pallas kernels, apply_tile(): pl.pallas_call(apply_kernel, in_specs=[hbm(), hbm(), vmem(), vmem()], out...  7.12 us
    ppermute x2, starting transfers between devices, other_core(): return lax.ppermute(array, CORE, [(0, 1), (1, 0)])  5.41 us
    pallas_call x1, Pallas kernels, solve(): pl.pallas_call(solve_kernel, out_shape=[shape(NB, RHS, BLK), shape(3 * RH...  4.55 us
  transfers between devices with their start and end apart: 10, of which 4 were waited for; matrix products, arithmetic and copies ran while one was open for 0% of the time, Pallas kernels for 6%

profile of v8, /device:TPU:1, one launch (start us, length us, event | category | flops | bytes accessed | tf_op | source)
XLA Modules:
  0.0 128.5 jit_solution(1575768831875091123)
XLA Ops:
  0.6 1.7 %spread.1 = (f32[8,88,128]{2,1,0:T(8,128)}, f32[80,128]{1,0:T(8,128)S(1)}, f32[80,128]{1,0:T(8,128)S(1)}) custom-call(f32[16,128]{1,0:T(8,128)} %points_hbm.1, f32[1,16]{1,0:T(1,128)} %bitcast.29, f32[8,128]{1,0:T(8,128)} %initial_hbm.1, f32[64,128]{1,0:T(8,128)} %ritz_hbm.1, f32[8,128]{1,0:T(8,128)} %targets_hbm.1), custom_call_target="tpu_custom_call" | custom-call | tf_op jit(solution)/shard_map/spread/pallas_call | solution.py:120
  2.4 3.4 %collective-permute-start.3 = (f32[80,128]{1,0:T(8,128)S(1)}, f32[80,128]{1,0:T(8,128)S(1)}, u32[]{:S(2)}, u32[]{:S(2)}) collective-permute-start(f32[80,128]{1,0:T(8,128)S(1)} %get-tuple-element.20), channel_id=1, source_target_pairs={{0,6},{2,0},{4,2},{6,4},{1,7},{3,1},{5,3},{7,5},{8,14},{10,8},{12,... | collective-permute-start | bytes 122888 | tf_op jit(solution)/shard_map/ppermute | solution.py:442
  5.8 0.5 collective-permute-start.2
  6.3 0.6 collective-permute-start.1
  6.9 8.2 %all-to-all-start = ((f32[8,88,128]{2,1,0:T(8,128)}), f32[8,88,128]{2,1,0:T(8,128)S(1)}, u32[]{:S(2)}, u32[]{:S(2)}) async-start(f32[8,88,128]{2,1,0:T(8,128)} %get-tuple-element.18), calls=%async_computation | async-start | bytes 720896 | tf_op jit(solution)/shard_map/all_to_all | solution.py:435
  16.4 0.1 pad_maximum_fusion
  16.5 0.0 collective-permute-done.1
  16.6 0.0 collective-permute-done.2
  16.6 0.0 collective-permute-done.3
  16.6 2.8 %collective-permute-start.6 = (f32[4,80,128]{2,1,0:T(8,128)S(1)}, f32[4,80,128]{2,1,0:T(8,128)S(1)}, u32[]{:S(2)}, u32[]{:S(2)}) collective-permute-start(f32[4,80,128]{2,1,0:T(8,128)S(1)} %bitcast_dynamic-update-slice_fusion.4), channel_id=1, source_target_pairs={{0,192},{64,0},{128,64},{192,128},{1,193},{65,1},{129,65},{193,129... | collective-permute-start | bytes 491528 | tf_op jit(solution)/shard_map/ppermute | solution.py:442
  19.4 0.3 collective-permute-start.5
  19.8 0.7 collective-permute-start.4
  20.5 9.2 %collective-permute-done.4 = f32[4,80,128]{2,1,0:T(8,128)S(1)} collective-permute-done((f32[4,80,128]{2,1,0:T(8,128)S(1)}, f32[4,80,128]{2,1,0:T(8,128)S(1)}, u32[]{:S(2)}, u32[]{:S(2)}) %collective-permute-start.4) | collective-permute-done | bytes 163872 | tf_op jit(solution)/shard_map/ppermute | solution.py:442
  29.7 0.0 collective-permute-done.5
  29.8 0.0 all-to-all-done.near_ref
  29.8 0.1 broadcast_in_dim.42.scalars_ref
  29.8 1.6 %collective-permute-start = (f32[8,88,128]{2,1,0:T(8,128)S(1)}, f32[8,88,128]{2,1,0:T(8,128)S(1)}, u32[]{:S(2)}, u32[]{:S(2)}) collective-permute-start(f32[8,88,128]{2,1,0:T(8,128)S(1)} %all-to-all-done.near_ref), channel_id=1, source_target_pairs={{0,1},{1,0},{2,3},{3,2},{4,5},{5,4},{6,7},{7,6},{8,9},{9,8},{10,11... | collective-permute-start | bytes 1081352 | tf_op jit(solution)/shard_map/ppermute | solution.py:448
  31.4 0.0 collective-permute-done.6
  31.4 1.3 collective-permute-done.far_ref
  32.7 8.7 %kernel_tile.1 = (bf16[2048,2048]{1,0:T(8,128)(2,1)}, bf16[2048,2048]{1,0:T(8,128)(2,1)}, f32[16,72,128]{2,1,0:T(8,128)S(1)}) custom-call(f32[8,88,128]{2,1,0:T(8,128)S(1)} %all-to-all-done.near_ref, f32[8,88,128]{2,1,0:T(8,128)S(1)} %collective-permute-done.far_ref, f32[16,80,128]{2,1,0:T(8,128)S(1)} %bitcast.24, f32[8,128]{1,0:T(8,128)S(1)} %multiply_bitcast_fusion.mark_ref), custom_call_target="tpu_custom_call" | custom-call | tf_op jit(solution)/shard_map/kernel_tile/pallas_call | solution.py:188
  41.4 16.0 %all_to_all.36.got_ref = f32[16,72,128]{2,1,0:T(8,128)S(1)} all-to-all(f32[16,72,128]{2,1,0:T(8,128)S(1)} %get-tuple-element.23), channel_id=1, replica_groups=mesh['row_0'=4,'row_1'=8,'col_0'=4,'col_1'=2] {'row_0','col_0'}, dimensions={0} | all-to-all | bytes 1179648 | tf_op jit(solution)/shard_map/all_to_all | solution.py:435
  57.4 0.1 at_owner.1
  57.5 14.0 %all_to_all.37.vec_ref = f32[16,72,128]{2,1,0:T(8,128)S(1)} all-to-all(f32[16,72,128]{2,1,0:T(8,128)S(1)} %at_owner.1), channel_id=1, replica_groups=mesh['row_0'=4,'row_1'=8,'col_0'=4,'col_1'=2] {'row_0','col_0'}, dimensions={0} | all-to-all | bytes 1179648 | tf_op jit(solution)/shard_map/all_to_all | solution.py:435
  71.5 2.1 %gram.1 = f32[8,41,128]{2,1,0:T(8,128)} custom-call(f32[16,72,128]{2,1,0:T(8,128)S(1)} %all_to_all.37.vec_ref, f32[16,80,128]{2,1,0:T(8,128)S(1)} %bitcast.25), custom_call_target="tpu_custom_call" | custom-call | tf_op jit(solution)/shard_map/gram/pallas_call | solution.py:256
  73.5 5.4 %all-to-all-start.3 = ((f32[8,41,128]{2,1,0:T(8,128)}), f32[8,41,128]{2,1,0:T(8,128)S(1)}, u32[]{:S(2)}, u32[]{:S(2)}) async-start(f32[8,41,128]{2,1,0:T(8,128)} %gram.1), calls=%async_computation.3 | async-start | bytes 393216 | tf_op jit(solution)/shard_map/all_to_all | solution.py:435
  78.9 7.1 %apply_tile.1.image_ref = f32[144,2048]{1,0:T(8,128)S(1)} custom-call(bf16[2048,2048]{1,0:T(8,128)(2,1)} %get-tuple-element.21.hi_hbm, bf16[2048,2048]{1,0:T(8,128)(2,1)} %get-tuple-element.22.lo_hbm, f32[16,72,128]{2,1,0:T(8,128)S(1)} %all_to_all.37.vec_ref, f32[16,80,128]{2,1,0:T(8,128)S(1)} %bitcast.26), custom_call_target="tpu_custom_call" | custom-call | flops 4831838208 | bytes 16777216 | tf_op jit(solution)/shard_map/apply_tile/pallas_call | solution.py:329
  86.0 1.6 %all-to-all-done.3 = f32[8,41,128]{2,1,0:T(8,128)S(1)} async-done(((f32[8,41,128]{2,1,0:T(8,128)}), f32[8,41,128]{2,1,0:T(8,128)S(1)}, u32[]{:S(2)}, u32[]{:S(2)}) %all-to-all-start.3) | async-done | bytes 167968 | tf_op jit(solution)/shard_map/all_to_all | solution.py:435
  87.7 3.9 %collective-permute-start.7 = (f32[41,128]{1,0:T(8,128)S(1)}, f32[41,128]{1,0:T(8,128)S(1)}, u32[]{:S(2)}, u32[]{:S(2)}) collective-permute-start(f32[41,128]{1,0:T(8,128)S(1)} %reduce_sum.9.gram_ref), channel_id=1, source_target_pairs={{0,1},{1,0},{2,3},{3,2},{4,5},{5,4},{6,7},{7,6},{8,9},{9,8},{10,11... | collective-permute-start | bytes 62984 | tf_op jit(solution)/shard_map/ppermute | solution.py:448
  91.5 0.8 collective-permute-done.7.more_ref
  92.4 4.5 %solve.1 = (f32[16,8,128]{2,1,0:T(8,128)S(1)}, f32[24,128]{1,0:T(8,128)S(1)}) custom-call(f32[41,128]{1,0:T(8,128)S(1)} %reduce_sum.9.gram_ref, f32[41,128]{1,0:T(8,128)S(1)} %collective-permute-done.7.more_ref, f32[144,2048]{1,0:T(8,128)S(1)} %apply_tile.1.image_ref, f32[16,72,128]{2,1,0:T(8,128)S(1)} %all_to_all.37.vec_ref, ...), custom_call_target="tpu_custom_call" | custom-call | tf_op jit(solution)/shard_map/solve/pallas_call | solution.py:378
  96.9 11.8 %all_to_all.38.got_ref = f32[16,8,128]{2,1,0:T(8,128)S(1)} all-to-all(f32[16,8,128]{2,1,0:T(8,128)S(1)} %get-tuple-element.30), channel_id=1, replica_groups=mesh['row_0'=4,'row_1'=8,'col_0'=4,'col_1'=2] {'col_1','row_1'}, dimensions={0} | all-to-all | bytes 131072 | tf_op jit(solution)/shard_map/all_to_all | solution.py:435
  108.8 0.2 stats.1
  109.0 18.8 %all_to_all.39 = f32[256,1,16]{2,1,0:T(1,128)S(1)} all-to-all(f32[256,1,16]{2,1,0:T(1,128)S(1)} %bitcast.28), channel_id=1, replica_groups=mesh['row_0'=4,'row_1'=8,'col_0'=4,'col_1'=2] {'col_0','col_1','row_0','..., dimensions={0} | all-to-all | bytes 32768 | tf_op jit(solution)/shard_map/all_to_all | solution.py:435
  127.8 0.7 finish.1
  (12 shorter events, 0.2 us)
Async XLA Ops:
  2.4 14.2 %collective-permute-start.3 = (f32[80,128]{1,0:T(8,128)S(1)}, f32[80,128]{1,0:T(8,128)S(1)}, u32[]{:S(2)}, u32[]{:S(2)}) collective-permute-start(f32[80,128]{1,0:T(8,128)S(1)} %get-tuple-element.20), channel_id=1, source_target_pairs={{0,6},{2,0},{4,2},{6,4},{1,7},{3,1},{5,3},{7,5},{8,14},{10,8},{12,... | collective-permute-start | bytes 122888 | tf_op jit(solution)/shard_map/ppermute | solution.py:442
  5.8 10.8 %collective-permute-start.2 = (f32[80,128]{1,0:T(8,128)S(1)}, f32[80,128]{1,0:T(8,128)S(1)}, u32[]{:S(2)}, u32[]{:S(2)}) collective-permute-start(f32[80,128]{1,0:T(8,128)S(1)} %get-tuple-element.20), channel_id=1, source_target_pairs={{0,4},{2,6},{4,0},{6,2},{1,5},{3,7},{5,1},{7,3},{8,12},{10,14},{12... | collective-permute-start | bytes 122888 | tf_op jit(solution)/shard_map/ppermute | solution.py:442
  6.3 10.3 %collective-permute-start.1 = (f32[80,128]{1,0:T(8,128)S(1)}, f32[80,128]{1,0:T(8,128)S(1)}, u32[]{:S(2)}, u32[]{:S(2)}) collective-permute-start(f32[80,128]{1,0:T(8,128)S(1)} %get-tuple-element.20), channel_id=1, source_target_pairs={{0,2},{2,4},{4,6},{6,0},{1,3},{3,5},{5,7},{7,1},{8,10},{10,12},{12... | collective-permute-start | bytes 122888 | tf_op jit(solution)/shard_map/ppermute | solution.py:442
  6.9 22.9 %all-to-all-start = ((f32[8,88,128]{2,1,0:T(8,128)}), f32[8,88,128]{2,1,0:T(8,128)S(1)}, u32[]{:S(2)}, u32[]{:S(2)}) async-start(f32[8,88,128]{2,1,0:T(8,128)} %get-tuple-element.18), calls=%async_computation | async-start | bytes 720896 | tf_op jit(solution)/shard_map/all_to_all | solution.py:435
  16.6 14.8 %collective-permute-start.6 = (f32[4,80,128]{2,1,0:T(8,128)S(1)}, f32[4,80,128]{2,1,0:T(8,128)S(1)}, u32[]{:S(2)}, u32[]{:S(2)}) collective-permute-start(f32[4,80,128]{2,1,0:T(8,128)S(1)} %bitcast_dynamic-update-slice_fusion.4), channel_id=1, source_target_pairs={{0,192},{64,0},{128,64},{192,128},{1,193},{65,1},{129,65},{193,129... | collective-permute-start | bytes 491528 | tf_op jit(solution)/shard_map/ppermute | solution.py:442
  19.4 10.3 %collective-permute-start.5 = (f32[4,80,128]{2,1,0:T(8,128)S(1)}, f32[4,80,128]{2,1,0:T(8,128)S(1)}, u32[]{:S(2)}, u32[]{:S(2)}) collective-permute-start(f32[4,80,128]{2,1,0:T(8,128)S(1)} %bitcast_dynamic-update-slice_fusion.4), channel_id=1, source_target_pairs={{0,128},{64,192},{128,0},{192,64},{1,129},{65,193},{129,1},{193,65... | collective-permute-start | bytes 491528 | tf_op jit(solution)/shard_map/ppermute | solution.py:442
  19.8 9.9 %collective-permute-start.4 = (f32[4,80,128]{2,1,0:T(8,128)S(1)}, f32[4,80,128]{2,1,0:T(8,128)S(1)}, u32[]{:S(2)}, u32[]{:S(2)}) collective-permute-start(f32[4,80,128]{2,1,0:T(8,128)S(1)} %bitcast_dynamic-update-slice_fusion.4), channel_id=1, source_target_pairs={{0,64},{64,128},{128,192},{192,0},{1,65},{65,129},{129,193},{193,1... | collective-permute-start | bytes 491528 | tf_op jit(solution)/shard_map/ppermute | solution.py:442
  29.8 2.9 %collective-permute-start = (f32[8,88,128]{2,1,0:T(8,128)S(1)}, f32[8,88,128]{2,1,0:T(8,128)S(1)}, u32[]{:S(2)}, u32[]{:S(2)}) collective-permute-start(f32[8,88,128]{2,1,0:T(8,128)S(1)} %all-to-all-done.near_ref), channel_id=1, source_target_pairs={{0,1},{1,0},{2,3},{3,2},{4,5},{5,4},{6,7},{7,6},{8,9},{9,8},{10,11... | collective-permute-start | bytes 1081352 | tf_op jit(solution)/shard_map/ppermute | solution.py:448
  73.5 14.1 %all-to-all-start.3 = ((f32[8,41,128]{2,1,0:T(8,128)}), f32[8,41,128]{2,1,0:T(8,128)S(1)}, u32[]{:S(2)}, u32[]{:S(2)}) async-start(f32[8,41,128]{2,1,0:T(8,128)} %gram.1), calls=%async_computation.3 | async-start | bytes 393216 | tf_op jit(solution)/shard_map/all_to_all | solution.py:435
  87.7 4.7 %collective-permute-start.7 = (f32[41,128]{1,0:T(8,128)S(1)}, f32[41,128]{1,0:T(8,128)S(1)}, u32[]{:S(2)}, u32[]{:S(2)}) collective-permute-start(f32[41,128]{1,0:T(8,128)S(1)} %reduce_sum.9.gram_ref), channel_id=1, source_target_pairs={{0,1},{1,0},{2,3},{3,2},{4,5},{5,4},{6,7},{7,6},{8,9},{9,8},{10,11... | collective-permute-start | bytes 62984 | tf_op jit(solution)/shard_map/ppermute | solution.py:448

commit v9 on v8

--- a/solution.py
+++ b/solution.py
@@ -20,6 +20,7 @@
 RITZ = 64
 RHS = 8
 VEC = RHS + RITZ
+LEFT = VEC + 8
 BLK = 128
 NB = 16
 PTS = NB * BLK
@@ -236,10 +237,21 @@
 def gram_kernel(vec_ref, pts_ref, out_ref, left_ref, right_ref):
     for b in range(NB):
         lanes = pl.ds(b * BLK, BLK)
-        left_ref[:, lanes] = vec_ref[b]
-        right_ref[pl.ds(0, RITZ), lanes] = pts_ref[b, FEAT:, :]
-        right_ref[pl.ds(RITZ, RITZ), lanes] = vec_ref[b, RHS:, :]
-    gram = lax.dot_general(left_ref[...], right_ref[...], NT, precision=HIGH, preferred_element_type=F32)
+        pad = jnp.zeros((LEFT - VEC, BLK), F32)
+        image = split3(vec_ref[b])
+        basis = split3(pts_ref[b, FEAT:, :])
+        for q in range(3):
+            left_ref[pl.ds(q * LEFT, LEFT), lanes] = jnp.concatenate([image[q], pad], axis=0).astype(BF16)
+            right_ref[pl.ds(q * 2 * RITZ, RITZ), lanes] = basis[q].astype(BF16)
+            right_ref[pl.ds(q * 2 * RITZ + RITZ, RITZ), lanes] = image[q][RHS:].astype(BF16)
+    gram = jnp.zeros((VEC, 2 * RITZ), F32)
+    for q in (2, 1, 0):
+        rows = 3 - q
+        left = left_ref[pl.ds(0, rows * LEFT), :]
+        right = right_ref[pl.ds(q * 2 * RITZ, 2 * RITZ), :]
+        total = lax.dot_general(left, right, NT, preferred_element_type=F32)
+        for r in range(rows - 1, -1, -1):
+            gram += total[r * LEFT : r * LEFT + VEC]
     coarse = gram[RHS:, :RITZ]
     coarse = 0.5 * (coarse + coarse.T)
     image = gram[RHS:, RITZ:]
@@ -256,7 +268,7 @@
     return pl.pallas_call(
         gram_kernel,
         out_shape=shape(NB // 2, PACKED, BLK),
-        scratch_shapes=[pltpu.VMEM((VEC, PTS), F32), pltpu.VMEM((2 * RITZ, PTS), F32)],
+        scratch_shapes=[pltpu.VMEM((3 * LEFT, PTS), BF16), pltpu.VMEM((6 * RITZ, PTS), BF16)],
         compiler_params=limit(12),
         name="gram",
     )(vec, pts)
@@ -342,6 +354,10 @@
     )(in_hbm(hi), in_hbm(lo), vec, pts)
 
 
+def exact(left, right):
+    return jnp.dot(left, right, precision=HIGH, preferred_element_type=F32)
+
+
 def solve_kernel(gram_ref, more_ref, image_ref, vec_ref, held_ref, part_ref, own_ref):
     gram = gram_ref[...] + more_ref[...]
     projected = gram[:RHS, :RITZ]
@@ -353,25 +369,20 @@
     image = jnp.where(j < i, square, jnp.where(j > i, turned, gram[RHS + RITZ // 2 :, :RITZ]))
     solve = inverse(coarse)
     amounts = lax.dot_general(projected, solve, NT, precision=HIGH, preferred_element_type=F32)
-    against = first - jnp.dot(amounts, image, precision=HIGH, preferred_element_type=F32)
+    against = first - exact(amounts, image)
     turns = lax.dot_general(against, solve, NT, precision=HIGH, preferred_element_type=F32)
-    zero = jnp.zeros_like(turns)
-    coef = jnp.concatenate([turns, amounts], axis=1)
-    value = image_ref[pl.ds(0, RHS), :] - jnp.dot(
-        coef, image_ref[pl.ds(2 * RHS, 2 * RITZ), :], precision=HIGH, preferred_element_type=F32
-    )
+    value = image_ref[pl.ds(0, RHS), :] - exact(amounts, image_ref[pl.ds(2 * RHS + RITZ, RITZ), :])
+    value = value - exact(turns, image_ref[pl.ds(2 * RHS, RITZ), :])
     core = lax.axis_index(CORE)
     for at in range(NB):
         half = (at // (NB // 2) + core) % 2
         part_ref[half * (NB // 2) + at % (NB // 2)] = value[:, at * BLK : (at + 1) * BLK]
     mine = lax.axis_index("row_0") * 4 + lax.axis_index("col_0")
-    basis = jnp.concatenate([held_ref[pl.ds(2 * RHS, RITZ), :], vec_ref[mine, RHS:, :]], axis=0)
-    wanted = jnp.concatenate(
-        [coef, jnp.concatenate([zero, amounts], axis=1), jnp.concatenate([-amounts, zero], axis=1)], axis=0
-    )
-    base = vec_ref[mine, :RHS, :]
-    base = jnp.concatenate([base, base, held_ref[pl.ds(RHS, RHS), :]], axis=0)
-    own_ref[...] = base - jnp.dot(wanted, basis, precision=HIGH, preferred_element_type=F32)
+    ritz = held_ref[pl.ds(2 * RHS, RITZ), :]
+    residual = vec_ref[mine, :RHS, :] - exact(amounts, vec_ref[mine, RHS:, :])
+    own_ref[pl.ds(0, RHS), :] = residual - exact(turns, ritz)
+    own_ref[pl.ds(RHS, RHS), :] = residual
+    own_ref[pl.ds(2 * RHS, RHS), :] = held_ref[pl.ds(RHS, RHS), :] + exact(amounts, ritz)
 
 
 def solve(gram, more, image, vec, held):

time: 129 us -> 129 us (level)
  no operation moved by 1% of the time
where the time goes in v9:
time: 129 us; the launch traced here: 128 us
  blocking collectives  60.7 us (47%)
  starting transfers between devices  27.6 us (21%)
  Pallas kernels  24.8 us (19%)
  waiting for transfers between devices  12.9 us (10%)
  between operations  2.13 us (2%)
    all_to_all x4, blocking collectives, exchange(): return lax.all_to_all(pieces, axis, split_axis=0, concat_axis=0, tiled=True)  60.7 us
    all_to_all x2, starting transfers between devices, exchange(): return lax.all_to_all(pieces, axis, split_axis=0, concat_axis=0, tiled=True)  13.6 us
    ppermute x6, waiting for transfers between devices, all_around(): lax.ppermute(array, axis, [(i, (i + k) % size) for i in range(size)])  9.18 us
    pallas_call x1, Pallas kernels, make_tile(): pl.pallas_call(tile_kernel, in_specs=[vmem(), vmem(), vmem(), vmem()], ou...  8.69 us
    ppermute x6, starting transfers between devices, all_around(): lax.ppermute(array, axis, [(i, (i + k) % size) for i in range(size)])  8.35 us
    pallas_call x1, Pallas kernels, apply_tile(): pl.pallas_call(apply_kernel, in_specs=[hbm(), hbm(), vmem(), vmem()], out...  7.12 us
    ppermute x2, starting transfers between devices, other_core(): return lax.ppermute(array, CORE, [(0, 1), (1, 0)])  5.64 us
    pallas_call x1, Pallas kernels, solve(): pl.pallas_call(solve_kernel, out_shape=[shape(NB, RHS, BLK), shape(3 * RH...  4.42 us
  transfers between devices with their start and end apart: 10, of which 4 were waited for; matrix products, arithmetic and copies ran while one was open for 0% of the time, Pallas kernels for 6%

profile of v9, /device:TPU:1, one launch (start us, length us, event | category | flops | bytes accessed | tf_op | source)
XLA Modules:
  0.0 128.4 jit_solution(8157745267231275967)
XLA Ops:
  0.6 1.7 %spread.1 = (f32[8,88,128]{2,1,0:T(8,128)}, f32[80,128]{1,0:T(8,128)S(1)}, f32[80,128]{1,0:T(8,128)S(1)}) custom-call(f32[16,128]{1,0:T(8,128)} %points_hbm.1, f32[1,16]{1,0:T(1,128)} %bitcast.29, f32[8,128]{1,0:T(8,128)} %initial_hbm.1, f32[64,128]{1,0:T(8,128)} %ritz_hbm.1, f32[8,128]{1,0:T(8,128)} %targets_hbm.1), custom_call_target="tpu_custom_call" | custom-call | tf_op jit(solution)/shard_map/spread/pallas_call | solution.py:121
  2.4 3.4 %collective-permute-start.3 = (f32[80,128]{1,0:T(8,128)S(1)}, f32[80,128]{1,0:T(8,128)S(1)}, u32[]{:S(2)}, u32[]{:S(2)}) collective-permute-start(f32[80,128]{1,0:T(8,128)S(1)} %get-tuple-element.20), channel_id=1, source_target_pairs={{0,6},{2,0},{4,2},{6,4},{1,7},{3,1},{5,3},{7,5},{8,14},{10,8},{12,... | collective-permute-start | bytes 122888 | tf_op jit(solution)/shard_map/ppermute | solution.py:453
  5.8 0.5 collective-permute-start.2
  6.3 0.6 collective-permute-start.1
  6.9 8.2 %all-to-all-start = ((f32[8,88,128]{2,1,0:T(8,128)}), f32[8,88,128]{2,1,0:T(8,128)S(1)}, u32[]{:S(2)}, u32[]{:S(2)}) async-start(f32[8,88,128]{2,1,0:T(8,128)} %get-tuple-element.18), calls=%async_computation | async-start | bytes 720896 | tf_op jit(solution)/shard_map/all_to_all | solution.py:446
  16.4 0.1 pad_maximum_fusion
  16.5 0.0 collective-permute-done.1
  16.6 0.0 collective-permute-done.2
  16.6 0.0 collective-permute-done.3
  16.6 2.8 %collective-permute-start.6 = (f32[4,80,128]{2,1,0:T(8,128)S(1)}, f32[4,80,128]{2,1,0:T(8,128)S(1)}, u32[]{:S(2)}, u32[]{:S(2)}) collective-permute-start(f32[4,80,128]{2,1,0:T(8,128)S(1)} %bitcast_dynamic-update-slice_fusion.4), channel_id=1, source_target_pairs={{0,192},{64,0},{128,64},{192,128},{1,193},{65,1},{129,65},{193,129... | collective-permute-start | bytes 491528 | tf_op jit(solution)/shard_map/ppermute | solution.py:453
  19.4 0.3 collective-permute-start.5
  19.8 0.7 collective-permute-start.4
  20.5 9.2 %collective-permute-done.4 = f32[4,80,128]{2,1,0:T(8,128)S(1)} collective-permute-done((f32[4,80,128]{2,1,0:T(8,128)S(1)}, f32[4,80,128]{2,1,0:T(8,128)S(1)}, u32[]{:S(2)}, u32[]{:S(2)}) %collective-permute-start.4) | collective-permute-done | bytes 163872 | tf_op jit(solution)/shard_map/ppermute | solution.py:453
  29.7 0.0 collective-permute-done.5
  29.8 0.0 all-to-all-done.near_ref
  29.8 0.1 broadcast_in_dim.42.scalars_ref
  29.8 1.6 %collective-permute-start = (f32[8,88,128]{2,1,0:T(8,128)S(1)}, f32[8,88,128]{2,1,0:T(8,128)S(1)}, u32[]{:S(2)}, u32[]{:S(2)}) collective-permute-start(f32[8,88,128]{2,1,0:T(8,128)S(1)} %all-to-all-done.near_ref), channel_id=1, source_target_pairs={{0,1},{1,0},{2,3},{3,2},{4,5},{5,4},{6,7},{7,6},{8,9},{9,8},{10,11... | collective-permute-start | bytes 1081352 | tf_op jit(solution)/shard_map/ppermute | solution.py:459
  31.4 0.0 collective-permute-done.6
  31.4 1.3 collective-permute-done.far_ref
  32.7 8.7 %kernel_tile.1 = (bf16[2048,2048]{1,0:T(8,128)(2,1)}, bf16[2048,2048]{1,0:T(8,128)(2,1)}, f32[16,72,128]{2,1,0:T(8,128)S(1)}) custom-call(f32[8,88,128]{2,1,0:T(8,128)S(1)} %all-to-all-done.near_ref, f32[8,88,128]{2,1,0:T(8,128)S(1)} %collective-permute-done.far_ref, f32[16,80,128]{2,1,0:T(8,128)S(1)} %bitcast.24, f32[8,128]{1,0:T(8,128)S(1)} %multiply_bitcast_fusion.mark_ref), custom_call_target="tpu_custom_call" | custom-call | tf_op jit(solution)/shard_map/kernel_tile/pallas_call | solution.py:189
  41.4 16.0 %all_to_all.36.got_ref = f32[16,72,128]{2,1,0:T(8,128)S(1)} all-to-all(f32[16,72,128]{2,1,0:T(8,128)S(1)} %get-tuple-element.23), channel_id=1, replica_groups=mesh['row_0'=4,'row_1'=8,'col_0'=4,'col_1'=2] {'row_0','col_0'}, dimensions={0} | all-to-all | bytes 1179648 | tf_op jit(solution)/shard_map/all_to_all | solution.py:446
  57.4 0.1 at_owner.1
  57.5 14.0 %all_to_all.37.vec_ref = f32[16,72,128]{2,1,0:T(8,128)S(1)} all-to-all(f32[16,72,128]{2,1,0:T(8,128)S(1)} %at_owner.1), channel_id=1, replica_groups=mesh['row_0'=4,'row_1'=8,'col_0'=4,'col_1'=2] {'row_0','col_0'}, dimensions={0} | all-to-all | bytes 1179648 | tf_op jit(solution)/shard_map/all_to_all | solution.py:446
  71.5 1.8 %gram.1 = f32[8,41,128]{2,1,0:T(8,128)} custom-call(f32[16,72,128]{2,1,0:T(8,128)S(1)} %all_to_all.37.vec_ref, f32[16,80,128]{2,1,0:T(8,128)S(1)} %bitcast.25), custom_call_target="tpu_custom_call" | custom-call | tf_op jit(solution)/shard_map/gram/pallas_call | solution.py:268
  73.3 5.4 %all-to-all-start.3 = ((f32[8,41,128]{2,1,0:T(8,128)}), f32[8,41,128]{2,1,0:T(8,128)S(1)}, u32[]{:S(2)}, u32[]{:S(2)}) async-start(f32[8,41,128]{2,1,0:T(8,128)} %gram.1), calls=%async_computation.3 | async-start | bytes 393216 | tf_op jit(solution)/shard_map/all_to_all | solution.py:446
  78.7 7.1 %apply_tile.1.image_ref = f32[144,2048]{1,0:T(8,128)S(1)} custom-call(bf16[2048,2048]{1,0:T(8,128)(2,1)} %get-tuple-element.21.hi_hbm, bf16[2048,2048]{1,0:T(8,128)(2,1)} %get-tuple-element.22.lo_hbm, f32[16,72,128]{2,1,0:T(8,128)S(1)} %all_to_all.37.vec_ref, f32[16,80,128]{2,1,0:T(8,128)S(1)} %bitcast.26), custom_call_target="tpu_custom_call" | custom-call | flops 4831838208 | bytes 16777216 | tf_op jit(solution)/shard_map/apply_tile/pallas_call | solution.py:341
  85.8 1.6 %all-to-all-done.3 = f32[8,41,128]{2,1,0:T(8,128)S(1)} async-done(((f32[8,41,128]{2,1,0:T(8,128)}), f32[8,41,128]{2,1,0:T(8,128)S(1)}, u32[]{:S(2)}, u32[]{:S(2)}) %all-to-all-start.3) | async-done | bytes 167968 | tf_op jit(solution)/shard_map/all_to_all | solution.py:446
  87.4 4.1 %collective-permute-start.7 = (f32[41,128]{1,0:T(8,128)S(1)}, f32[41,128]{1,0:T(8,128)S(1)}, u32[]{:S(2)}, u32[]{:S(2)}) collective-permute-start(f32[41,128]{1,0:T(8,128)S(1)} %reduce_sum.9.gram_ref), channel_id=1, source_target_pairs={{0,1},{1,0},{2,3},{3,2},{4,5},{5,4},{6,7},{7,6},{8,9},{9,8},{10,11... | collective-permute-start | bytes 62984 | tf_op jit(solution)/shard_map/ppermute | solution.py:459
  91.5 0.8 collective-permute-done.7.more_ref
  92.4 4.4 %solve.1 = (f32[16,8,128]{2,1,0:T(8,128)S(1)}, f32[24,128]{1,0:T(8,128)S(1)}) custom-call(f32[41,128]{1,0:T(8,128)S(1)} %reduce_sum.9.gram_ref, f32[41,128]{1,0:T(8,128)S(1)} %collective-permute-done.7.more_ref, f32[144,2048]{1,0:T(8,128)S(1)} %apply_tile.1.image_ref, f32[16,72,128]{2,1,0:T(8,128)S(1)} %all_to_all.37.vec_ref, ...), custom_call_target="tpu_custom_call" | custom-call | tf_op jit(solution)/shard_map/solve/pallas_call | solution.py:389
  96.8 11.9 %all_to_all.38.got_ref = f32[16,8,128]{2,1,0:T(8,128)S(1)} all-to-all(f32[16,8,128]{2,1,0:T(8,128)S(1)} %get-tuple-element.30), channel_id=1, replica_groups=mesh['row_0'=4,'row_1'=8,'col_0'=4,'col_1'=2] {'col_1','row_1'}, dimensions={0} | all-to-all | bytes 131072 | tf_op jit(solution)/shard_map/all_to_all | solution.py:446
  108.6 0.2 stats.1
  108.9 18.8 %all_to_all.39 = f32[256,1,16]{2,1,0:T(1,128)S(1)} all-to-all(f32[256,1,16]{2,1,0:T(1,128)S(1)} %bitcast.28), channel_id=1, replica_groups=mesh['row_0'=4,'row_1'=8,'col_0'=4,'col_1'=2] {'col_0','col_1','row_0','..., dimensions={0} | all-to-all | bytes 32768 | tf_op jit(solution)/shard_map/all_to_all | solution.py:446
  127.7 0.7 finish.1
  (12 shorter events, 0.2 us)
Async XLA Ops:
  2.4 14.2 %collective-permute-start.3 = (f32[80,128]{1,0:T(8,128)S(1)}, f32[80,128]{1,0:T(8,128)S(1)}, u32[]{:S(2)}, u32[]{:S(2)}) collective-permute-start(f32[80,128]{1,0:T(8,128)S(1)} %get-tuple-element.20), channel_id=1, source_target_pairs={{0,6},{2,0},{4,2},{6,4},{1,7},{3,1},{5,3},{7,5},{8,14},{10,8},{12,... | collective-permute-start | bytes 122888 | tf_op jit(solution)/shard_map/ppermute | solution.py:453
  5.8 10.8 %collective-permute-start.2 = (f32[80,128]{1,0:T(8,128)S(1)}, f32[80,128]{1,0:T(8,128)S(1)}, u32[]{:S(2)}, u32[]{:S(2)}) collective-permute-start(f32[80,128]{1,0:T(8,128)S(1)} %get-tuple-element.20), channel_id=1, source_target_pairs={{0,4},{2,6},{4,0},{6,2},{1,5},{3,7},{5,1},{7,3},{8,12},{10,14},{12... | collective-permute-start | bytes 122888 | tf_op jit(solution)/shard_map/ppermute | solution.py:453
  6.3 10.3 %collective-permute-start.1 = (f32[80,128]{1,0:T(8,128)S(1)}, f32[80,128]{1,0:T(8,128)S(1)}, u32[]{:S(2)}, u32[]{:S(2)}) collective-permute-start(f32[80,128]{1,0:T(8,128)S(1)} %get-tuple-element.20), channel_id=1, source_target_pairs={{0,2},{2,4},{4,6},{6,0},{1,3},{3,5},{5,7},{7,1},{8,10},{10,12},{12... | collective-permute-start | bytes 122888 | tf_op jit(solution)/shard_map/ppermute | solution.py:453
  6.9 22.9 %all-to-all-start = ((f32[8,88,128]{2,1,0:T(8,128)}), f32[8,88,128]{2,1,0:T(8,128)S(1)}, u32[]{:S(2)}, u32[]{:S(2)}) async-start(f32[8,88,128]{2,1,0:T(8,128)} %get-tuple-element.18), calls=%async_computation | async-start | bytes 720896 | tf_op jit(solution)/shard_map/all_to_all | solution.py:446
  16.6 14.8 %collective-permute-start.6 = (f32[4,80,128]{2,1,0:T(8,128)S(1)}, f32[4,80,128]{2,1,0:T(8,128)S(1)}, u32[]{:S(2)}, u32[]{:S(2)}) collective-permute-start(f32[4,80,128]{2,1,0:T(8,128)S(1)} %bitcast_dynamic-update-slice_fusion.4), channel_id=1, source_target_pairs={{0,192},{64,0},{128,64},{192,128},{1,193},{65,1},{129,65},{193,129... | collective-permute-start | bytes 491528 | tf_op jit(solution)/shard_map/ppermute | solution.py:453
  19.4 10.3 %collective-permute-start.5 = (f32[4,80,128]{2,1,0:T(8,128)S(1)}, f32[4,80,128]{2,1,0:T(8,128)S(1)}, u32[]{:S(2)}, u32[]{:S(2)}) collective-permute-start(f32[4,80,128]{2,1,0:T(8,128)S(1)} %bitcast_dynamic-update-slice_fusion.4), channel_id=1, source_target_pairs={{0,128},{64,192},{128,0},{192,64},{1,129},{65,193},{129,1},{193,65... | collective-permute-start | bytes 491528 | tf_op jit(solution)/shard_map/ppermute | solution.py:453
  19.8 9.9 %collective-permute-start.4 = (f32[4,80,128]{2,1,0:T(8,128)S(1)}, f32[4,80,128]{2,1,0:T(8,128)S(1)}, u32[]{:S(2)}, u32[]{:S(2)}) collective-permute-start(f32[4,80,128]{2,1,0:T(8,128)S(1)} %bitcast_dynamic-update-slice_fusion.4), channel_id=1, source_target_pairs={{0,64},{64,128},{128,192},{192,0},{1,65},{65,129},{129,193},{193,1... | collective-permute-start | bytes 491528 | tf_op jit(solution)/shard_map/ppermute | solution.py:453
  29.8 2.9 %collective-permute-start = (f32[8,88,128]{2,1,0:T(8,128)S(1)}, f32[8,88,128]{2,1,0:T(8,128)S(1)}, u32[]{:S(2)}, u32[]{:S(2)}) collective-permute-start(f32[8,88,128]{2,1,0:T(8,128)S(1)} %all-to-all-done.near_ref), channel_id=1, source_target_pairs={{0,1},{1,0},{2,3},{3,2},{4,5},{5,4},{6,7},{7,6},{8,9},{9,8},{10,11... | collective-permute-start | bytes 1081352 | tf_op jit(solution)/shard_map/ppermute | solution.py:459
  73.3 14.1 %all-to-all-start.3 = ((f32[8,41,128]{2,1,0:T(8,128)}), f32[8,41,128]{2,1,0:T(8,128)S(1)}, u32[]{:S(2)}, u32[]{:S(2)}) async-start(f32[8,41,128]{2,1,0:T(8,128)} %gram.1), calls=%async_computation.3 | async-start | bytes 393216 | tf_op jit(solution)/shard_map/all_to_all | solution.py:446
  87.4 4.9 %collective-permute-start.7 = (f32[41,128]{1,0:T(8,128)S(1)}, f32[41,128]{1,0:T(8,128)S(1)}, u32[]{:S(2)}, u32[]{:S(2)}) collective-permute-start(f32[41,128]{1,0:T(8,128)S(1)} %reduce_sum.9.gram_ref), channel_id=1, source_target_pairs={{0,1},{1,0},{2,3},{3,2},{4,5},{5,4},{6,7},{7,6},{8,9},{9,8},{10,11... | collective-permute-start | bytes 62984 | tf_op jit(solution)/shard_map/ppermute | solution.py:459

commit v10 on v9

--- a/solution.py
+++ b/solution.py
@@ -145,10 +145,8 @@
         at = b % (NB // 2)
         lanes = pl.ds(b * BLK, BLK)
         cols_ref[:, lanes] = features(src[at, :FEAT, :], False).astype(BF16)
-        tall = jnp.concatenate([src[at, FEAT:, :], jnp.zeros((BLK - VEC, BLK), F32)], axis=0).T
-        hi, lo = split2(tall)
-        vec_ref[lanes, pl.ds(0, BLK)] = hi
-        vec_ref[lanes, pl.ds(BLK, BLK)] = lo
+        pieces = [*split3(src[at, FEAT:, :]), jnp.zeros((2 * BLK - 3 * VEC, BLK), F32)]
+        vec_ref[lanes, :] = jnp.concatenate(pieces, axis=0).T.astype(BF16)
         rows_ref[lanes, :] = features(out_ref[b, :FEAT, :], True).T.astype(BF16)
 
     def copies(step):
@@ -177,9 +175,11 @@
                 hi_ref[rows, lanes] = hi
                 lo_ref[rows, lanes] = lo
         if step > 0:
-            both = total[:, :BLK] + total[:, BLK:]
             for h in range(STEP // BLK):
-                part_ref[(step - 1) * (STEP // BLK) + h] = both[h * BLK : (h + 1) * BLK].T[:VEC]
+                tall = total[h * BLK : (h + 1) * BLK].T
+                part_ref[(step - 1) * (STEP // BLK) + h] = (
+                    tall[:VEC] + tall[VEC : 2 * VEC] + tall[2 * VEC : 3 * VEC]
+                )
     for step in range(steps):
         for copy in copies(step):
             copy.wait()
@@ -323,18 +323,17 @@
     for b in range(NB):
         lanes = pl.ds(b * BLK, BLK)
         first = vec_ref[b, :RHS, :]
-        hi, lo = split2(
-            jnp.concatenate([first, jnp.zeros_like(first), pts_ref[b, FEAT:, :], vec_ref[b, RHS:, :]], axis=0)
-        )
-        rows_ref[pl.ds(0, HALF), lanes] = hi
-        rows_ref[pl.ds(HALF, HALF), lanes] = lo
+        rows = jnp.concatenate([first, jnp.zeros_like(first), pts_ref[b, FEAT:, :], vec_ref[b, RHS:, :]], axis=0)
+        for q, piece in enumerate(split3(rows)):
+            rows_ref[pl.ds(q * HALF, HALF), lanes] = piece.astype(BF16)
     for step in range(PTS // READ):
         lanes = pl.ds(step * READ, READ)
         for copy in copies[step]:
             copy.wait()
         both = jnp.dot(rows_ref[...], hi_ref[:, lanes], preferred_element_type=F32)
-        more = jnp.dot(rows_ref[pl.ds(0, HALF), :], lo_ref[:, lanes], preferred_element_type=F32)
-        out_ref[:, lanes] = both[:HALF] + both[HALF:] + more
+        more = jnp.dot(rows_ref[pl.ds(0, 2 * HALF), :], lo_ref[:, lanes], preferred_element_type=F32)
+        both = both[: 2 * HALF] + more + jnp.concatenate([jnp.zeros_like(both[:HALF]), both[2 * HALF :]], axis=0)
+        out_ref[:, lanes] = both[:HALF] + both[HALF:]
 
 
 def apply_tile(hi, lo, vec, pts):
@@ -343,7 +342,7 @@
         in_specs=[hbm(), hbm(), vmem(), vmem()],
         out_shape=shape(HALF, PTS),
         scratch_shapes=[
-            pltpu.VMEM((2 * HALF, PTS), BF16),
+            pltpu.VMEM((3 * HALF, PTS), BF16),
             pltpu.VMEM((PTS, PTS), BF16),
             pltpu.VMEM((PTS, PTS), BF16),
             pltpu.SemaphoreType.DMA((2, PTS // READ)),

time: 129 us -> 131 us (1.016)
  Pallas kernels: 24.8 us -> 26.8 us
  blocking collectives: 60.7 us -> 62.6 us
  waiting for transfers between devices: 12.9 us -> 11.3 us
    pallas_call x1, Pallas kernels: 7.12 us -> 9.06 us  [apply_tile(): pl.pallas_call(apply_kernel, in_specs=[hbm(), hbm(), vmem(), vmem()], out...]
    all_to_all x4, blocking collectives: 60.7 us -> 62.6 us  [exchange(): return lax.all_to_all(pieces, axis, split_axis=0, concat_axis=0, tiled=True)]
    all_to_all x2, waiting for transfers between devices: 1.61 us -> 0.01 us  [exchange(): return lax.all_to_all(pieces, axis, split_axis=0, concat_axis=0, tiled=True)]
  transfers between devices with their start and end apart: 10 -> 10, of which waited for: 4 -> 3; matrix products, arithmetic and copies ran while one was open for 0% -> 0% of each run, Pallas kernels for 6% -> 7%
where the time goes in v10:
time: 131 us; the launch traced here: 130 us
  blocking collectives  62.6 us (48%)
  starting transfers between devices  27 us (21%)
  Pallas kernels  26.8 us (20%)
  waiting for transfers between devices  11.3 us (9%)
  between operations  2.14 us (2%)
    all_to_all x4, blocking collectives, exchange(): return lax.all_to_all(pieces, axis, split_axis=0, concat_axis=0, tiled=True)  62.6 us
    all_to_all x2, starting transfers between devices, exchange(): return lax.all_to_all(pieces, axis, split_axis=0, concat_axis=0, tiled=True)  13.6 us
    ppermute x6, waiting for transfers between devices, all_around(): lax.ppermute(array, axis, [(i, (i + k) % size) for i in range(size)])  9.18 us
    pallas_call x1, Pallas kernels, apply_tile(): pl.pallas_call(apply_kernel, in_specs=[hbm(), hbm(), vmem(), vmem()], out...  9.06 us
    pallas_call x1, Pallas kernels, make_tile(): pl.pallas_call(tile_kernel, in_specs=[vmem(), vmem(), vmem(), vmem()], ou...  8.74 us
    ppermute x6, starting transfers between devices, all_around(): lax.ppermute(array, axis, [(i, (i + k) % size) for i in range(size)])  8.35 us
    ppermute x2, starting transfers between devices, other_core(): return lax.ppermute(array, CORE, [(0, 1), (1, 0)])  5.08 us
    pallas_call x1, Pallas kernels, solve(): pl.pallas_call(solve_kernel, out_shape=[shape(NB, RHS, BLK), shape(3 * RH...  4.42 us
  transfers between devices with their start and end apart: 10, of which 3 were waited for; matrix products, arithmetic and copies ran while one was open for 0% of the time, Pallas kernels for 7%

profile of v10, /device:TPU:1, one launch (start us, length us, event | category | flops | bytes accessed | tf_op | source)
XLA Modules:
  0.0 130.2 jit_solution(589504523716732023)
XLA Ops:
  0.6 1.7 %spread.1 = (f32[8,88,128]{2,1,0:T(8,128)}, f32[80,128]{1,0:T(8,128)S(1)}, f32[80,128]{1,0:T(8,128)S(1)}) custom-call(f32[16,128]{1,0:T(8,128)} %points_hbm.1, f32[1,16]{1,0:T(1,128)} %bitcast.29, f32[8,128]{1,0:T(8,128)} %initial_hbm.1, f32[64,128]{1,0:T(8,128)} %ritz_hbm.1, f32[8,128]{1,0:T(8,128)} %targets_hbm.1), custom_call_target="tpu_custom_call" | custom-call | tf_op jit(solution)/shard_map/spread/pallas_call | solution.py:121
  2.4 3.4 %collective-permute-start.3 = (f32[80,128]{1,0:T(8,128)S(1)}, f32[80,128]{1,0:T(8,128)S(1)}, u32[]{:S(2)}, u32[]{:S(2)}) collective-permute-start(f32[80,128]{1,0:T(8,128)S(1)} %get-tuple-element.20), channel_id=1, source_target_pairs={{0,6},{2,0},{4,2},{6,4},{1,7},{3,1},{5,3},{7,5},{8,14},{10,8},{12,... | collective-permute-start | bytes 122888 | tf_op jit(solution)/shard_map/ppermute | solution.py:452
  5.8 0.5 collective-permute-start.2
  6.3 0.6 collective-permute-start.1
  6.9 8.2 %all-to-all-start = ((f32[8,88,128]{2,1,0:T(8,128)}), f32[8,88,128]{2,1,0:T(8,128)S(1)}, u32[]{:S(2)}, u32[]{:S(2)}) async-start(f32[8,88,128]{2,1,0:T(8,128)} %get-tuple-element.18), calls=%async_computation | async-start | bytes 720896 | tf_op jit(solution)/shard_map/all_to_all | solution.py:445
  16.4 0.1 pad_maximum_fusion
  16.5 0.0 collective-permute-done.1
  16.6 0.0 collective-permute-done.2
  16.6 0.0 collective-permute-done.3
  16.6 2.8 %collective-permute-start.6 = (f32[4,80,128]{2,1,0:T(8,128)S(1)}, f32[4,80,128]{2,1,0:T(8,128)S(1)}, u32[]{:S(2)}, u32[]{:S(2)}) collective-permute-start(f32[4,80,128]{2,1,0:T(8,128)S(1)} %bitcast_dynamic-update-slice_fusion.4), channel_id=1, source_target_pairs={{0,192},{64,0},{128,64},{192,128},{1,193},{65,1},{129,65},{193,129... | collective-permute-start | bytes 491528 | tf_op jit(solution)/shard_map/ppermute | solution.py:452
  19.4 0.3 collective-permute-start.5
  19.8 0.7 collective-permute-start.4
  20.5 9.2 %collective-permute-done.4 = f32[4,80,128]{2,1,0:T(8,128)S(1)} collective-permute-done((f32[4,80,128]{2,1,0:T(8,128)S(1)}, f32[4,80,128]{2,1,0:T(8,128)S(1)}, u32[]{:S(2)}, u32[]{:S(2)}) %collective-permute-start.4) | collective-permute-done | bytes 163872 | tf_op jit(solution)/shard_map/ppermute | solution.py:452
  29.7 0.0 collective-permute-done.5
  29.8 0.0 all-to-all-done.near_ref
  29.8 0.1 broadcast_in_dim.42.scalars_ref
  29.8 1.6 %collective-permute-start = (f32[8,88,128]{2,1,0:T(8,128)S(1)}, f32[8,88,128]{2,1,0:T(8,128)S(1)}, u32[]{:S(2)}, u32[]{:S(2)}) collective-permute-start(f32[8,88,128]{2,1,0:T(8,128)S(1)} %all-to-all-done.near_ref), channel_id=1, source_target_pairs={{0,1},{1,0},{2,3},{3,2},{4,5},{5,4},{6,7},{7,6},{8,9},{9,8},{10,11... | collective-permute-start | bytes 1081352 | tf_op jit(solution)/shard_map/ppermute | solution.py:458
  31.4 0.0 collective-permute-done.6
  31.4 1.3 collective-permute-done.far_ref
  32.7 8.7 %kernel_tile.1 = (bf16[2048,2048]{1,0:T(8,128)(2,1)}, bf16[2048,2048]{1,0:T(8,128)(2,1)}, f32[16,72,128]{2,1,0:T(8,128)S(1)}) custom-call(f32[8,88,128]{2,1,0:T(8,128)S(1)} %all-to-all-done.near_ref, f32[8,88,128]{2,1,0:T(8,128)S(1)} %collective-permute-done.far_ref, f32[16,80,128]{2,1,0:T(8,128)S(1)} %bitcast.24, f32[8,128]{1,0:T(8,128)S(1)} %multiply_bitcast_fusion.mark_ref), custom_call_target="tpu_custom_call" | custom-call | tf_op jit(solution)/shard_map/kernel_tile/pallas_call | solution.py:189
  41.5 16.0 %all_to_all.36.got_ref = f32[16,72,128]{2,1,0:T(8,128)S(1)} all-to-all(f32[16,72,128]{2,1,0:T(8,128)S(1)} %get-tuple-element.23), channel_id=1, replica_groups=mesh['row_0'=4,'row_1'=8,'col_0'=4,'col_1'=2] {'row_0','col_0'}, dimensions={0} | all-to-all | bytes 1179648 | tf_op jit(solution)/shard_map/all_to_all | solution.py:445
  57.4 0.1 at_owner.1
  57.5 14.0 %all_to_all.37.vec_ref = f32[16,72,128]{2,1,0:T(8,128)S(1)} all-to-all(f32[16,72,128]{2,1,0:T(8,128)S(1)} %at_owner.1), channel_id=1, replica_groups=mesh['row_0'=4,'row_1'=8,'col_0'=4,'col_1'=2] {'row_0','col_0'}, dimensions={0} | all-to-all | bytes 1179648 | tf_op jit(solution)/shard_map/all_to_all | solution.py:445
  71.5 1.8 %gram.1 = f32[8,41,128]{2,1,0:T(8,128)} custom-call(f32[16,72,128]{2,1,0:T(8,128)S(1)} %all_to_all.37.vec_ref, f32[16,80,128]{2,1,0:T(8,128)S(1)} %bitcast.25), custom_call_target="tpu_custom_call" | custom-call | tf_op jit(solution)/shard_map/gram/pallas_call | solution.py:268
  73.3 5.4 %all-to-all-start.3 = ((f32[8,41,128]{2,1,0:T(8,128)}), f32[8,41,128]{2,1,0:T(8,128)S(1)}, u32[]{:S(2)}, u32[]{:S(2)}) async-start(f32[8,41,128]{2,1,0:T(8,128)} %gram.1), calls=%async_computation.3 | async-start | bytes 393216 | tf_op jit(solution)/shard_map/all_to_all | solution.py:445
  78.7 9.1 %apply_tile.1.image_ref = f32[144,2048]{1,0:T(8,128)S(1)} custom-call(bf16[2048,2048]{1,0:T(8,128)(2,1)} %get-tuple-element.21.hi_hbm, bf16[2048,2048]{1,0:T(8,128)(2,1)} %get-tuple-element.22.lo_hbm, f32[16,72,128]{2,1,0:T(8,128)S(1)} %all_to_all.37.vec_ref, f32[16,80,128]{2,1,0:T(8,128)S(1)} %bitcast.26), custom_call_target="tpu_custom_call" | custom-call | flops 4831838208 | bytes 16777216 | tf_op jit(solution)/shard_map/apply_tile/pallas_call | solution.py:340
  87.8 0.0 all-to-all-done.3
  87.8 3.5 %collective-permute-start.7 = (f32[41,128]{1,0:T(8,128)S(1)}, f32[41,128]{1,0:T(8,128)S(1)}, u32[]{:S(2)}, u32[]{:S(2)}) collective-permute-start(f32[41,128]{1,0:T(8,128)S(1)} %reduce_sum.9.gram_ref), channel_id=1, source_target_pairs={{0,1},{1,0},{2,3},{3,2},{4,5},{5,4},{6,7},{7,6},{8,9},{9,8},{10,11... | collective-permute-start | bytes 62984 | tf_op jit(solution)/shard_map/ppermute | solution.py:458
  91.3 0.8 collective-permute-done.7.more_ref
  92.2 4.4 %solve.1 = (f32[16,8,128]{2,1,0:T(8,128)S(1)}, f32[24,128]{1,0:T(8,128)S(1)}) custom-call(f32[41,128]{1,0:T(8,128)S(1)} %reduce_sum.9.gram_ref, f32[41,128]{1,0:T(8,128)S(1)} %collective-permute-done.7.more_ref, f32[144,2048]{1,0:T(8,128)S(1)} %apply_tile.1.image_ref, f32[16,72,128]{2,1,0:T(8,128)S(1)} %all_to_all.37.vec_ref, ...), custom_call_target="tpu_custom_call" | custom-call | tf_op jit(solution)/shard_map/solve/pallas_call | solution.py:388
  96.6 13.8 %all_to_all.38.got_ref = f32[16,8,128]{2,1,0:T(8,128)S(1)} all-to-all(f32[16,8,128]{2,1,0:T(8,128)S(1)} %get-tuple-element.30), channel_id=1, replica_groups=mesh['row_0'=4,'row_1'=8,'col_0'=4,'col_1'=2] {'col_1','row_1'}, dimensions={0} | all-to-all | bytes 131072 | tf_op jit(solution)/shard_map/all_to_all | solution.py:445
  110.4 0.2 stats.1
  110.6 18.8 %all_to_all.39 = f32[256,1,16]{2,1,0:T(1,128)S(1)} all-to-all(f32[256,1,16]{2,1,0:T(1,128)S(1)} %bitcast.28), channel_id=1, replica_groups=mesh['row_0'=4,'row_1'=8,'col_0'=4,'col_1'=2] {'col_0','col_1','row_0','..., dimensions={0} | all-to-all | bytes 32768 | tf_op jit(solution)/shard_map/all_to_all | solution.py:445
  129.4 0.7 finish.1
  (12 shorter events, 0.2 us)
Async XLA Ops:
  2.4 14.2 %collective-permute-start.3 = (f32[80,128]{1,0:T(8,128)S(1)}, f32[80,128]{1,0:T(8,128)S(1)}, u32[]{:S(2)}, u32[]{:S(2)}) collective-permute-start(f32[80,128]{1,0:T(8,128)S(1)} %get-tuple-element.20), channel_id=1, source_target_pairs={{0,6},{2,0},{4,2},{6,4},{1,7},{3,1},{5,3},{7,5},{8,14},{10,8},{12,... | collective-permute-start | bytes 122888 | tf_op jit(solution)/shard_map/ppermute | solution.py:452
  5.8 10.8 %collective-permute-start.2 = (f32[80,128]{1,0:T(8,128)S(1)}, f32[80,128]{1,0:T(8,128)S(1)}, u32[]{:S(2)}, u32[]{:S(2)}) collective-permute-start(f32[80,128]{1,0:T(8,128)S(1)} %get-tuple-element.20), channel_id=1, source_target_pairs={{0,4},{2,6},{4,0},{6,2},{1,5},{3,7},{5,1},{7,3},{8,12},{10,14},{12... | collective-permute-start | bytes 122888 | tf_op jit(solution)/shard_map/ppermute | solution.py:452
  6.3 10.3 %collective-permute-start.1 = (f32[80,128]{1,0:T(8,128)S(1)}, f32[80,128]{1,0:T(8,128)S(1)}, u32[]{:S(2)}, u32[]{:S(2)}) collective-permute-start(f32[80,128]{1,0:T(8,128)S(1)} %get-tuple-element.20), channel_id=1, source_target_pairs={{0,2},{2,4},{4,6},{6,0},{1,3},{3,5},{5,7},{7,1},{8,10},{10,12},{12... | collective-permute-start | bytes 122888 | tf_op jit(solution)/shard_map/ppermute | solution.py:452
  6.9 22.9 %all-to-all-start = ((f32[8,88,128]{2,1,0:T(8,128)}), f32[8,88,128]{2,1,0:T(8,128)S(1)}, u32[]{:S(2)}, u32[]{:S(2)}) async-start(f32[8,88,128]{2,1,0:T(8,128)} %get-tuple-element.18), calls=%async_computation | async-start | bytes 720896 | tf_op jit(solution)/shard_map/all_to_all | solution.py:445
  16.6 14.8 %collective-permute-start.6 = (f32[4,80,128]{2,1,0:T(8,128)S(1)}, f32[4,80,128]{2,1,0:T(8,128)S(1)}, u32[]{:S(2)}, u32[]{:S(2)}) collective-permute-start(f32[4,80,128]{2,1,0:T(8,128)S(1)} %bitcast_dynamic-update-slice_fusion.4), channel_id=1, source_target_pairs={{0,192},{64,0},{128,64},{192,128},{1,193},{65,1},{129,65},{193,129... | collective-permute-start | bytes 491528 | tf_op jit(solution)/shard_map/ppermute | solution.py:452
  19.4 10.3 %collective-permute-start.5 = (f32[4,80,128]{2,1,0:T(8,128)S(1)}, f32[4,80,128]{2,1,0:T(8,128)S(1)}, u32[]{:S(2)}, u32[]{:S(2)}) collective-permute-start(f32[4,80,128]{2,1,0:T(8,128)S(1)} %bitcast_dynamic-update-slice_fusion.4), channel_id=1, source_target_pairs={{0,128},{64,192},{128,0},{192,64},{1,129},{65,193},{129,1},{193,65... | collective-permute-start | bytes 491528 | tf_op jit(solution)/shard_map/ppermute | solution.py:452
  19.8 9.9 %collective-permute-start.4 = (f32[4,80,128]{2,1,0:T(8,128)S(1)}, f32[4,80,128]{2,1,0:T(8,128)S(1)}, u32[]{:S(2)}, u32[]{:S(2)}) collective-permute-start(f32[4,80,128]{2,1,0:T(8,128)S(1)} %bitcast_dynamic-update-slice_fusion.4), channel_id=1, source_target_pairs={{0,64},{64,128},{128,192},{192,0},{1,65},{65,129},{129,193},{193,1... | collective-permute-start | bytes 491528 | tf_op jit(solution)/shard_map/ppermute | solution.py:452
  29.8 2.9 %collective-permute-start = (f32[8,88,128]{2,1,0:T(8,128)S(1)}, f32[8,88,128]{2,1,0:T(8,128)S(1)}, u32[]{:S(2)}, u32[]{:S(2)}) collective-permute-start(f32[8,88,128]{2,1,0:T(8,128)S(1)} %all-to-all-done.near_ref), channel_id=1, source_target_pairs={{0,1},{1,0},{2,3},{3,2},{4,5},{5,4},{6,7},{7,6},{8,9},{9,8},{10,11... | collective-permute-start | bytes 1081352 | tf_op jit(solution)/shard_map/ppermute | solution.py:458
  73.3 14.5 %all-to-all-start.3 = ((f32[8,41,128]{2,1,0:T(8,128)}), f32[8,41,128]{2,1,0:T(8,128)S(1)}, u32[]{:S(2)}, u32[]{:S(2)}) async-start(f32[8,41,128]{2,1,0:T(8,128)} %gram.1), calls=%async_computation.3 | async-start | bytes 393216 | tf_op jit(solution)/shard_map/all_to_all | solution.py:445
  87.8 4.4 %collective-permute-start.7 = (f32[41,128]{1,0:T(8,128)S(1)}, f32[41,128]{1,0:T(8,128)S(1)}, u32[]{:S(2)}, u32[]{:S(2)}) collective-permute-start(f32[41,128]{1,0:T(8,128)S(1)} %reduce_sum.9.gram_ref), channel_id=1, source_target_pairs={{0,1},{1,0},{2,3},{3,2},{4,5},{5,4},{6,7},{7,6},{8,9},{9,8},{10,11... | collective-permute-start | bytes 62984 | tf_op jit(solution)/shard_map/ppermute | solution.py:458
